TPU v7x, 32 devices: a whole 2x2x4 slice. The times are simulated.
32 devices in a mesh: grp: 4 (over y, x), dev: 8 (over z, core).
Axes of the slice: x: 2, y: 2, z: 4, core: 2. Of those that a mesh axis runs over, the one named last changes fastest.
Arguments:
- points: bfloat16 [65536, 256], P(('grp', 'dev')), may hold values from -6 to 6
- ridge: float32 [1024], replicated, may hold values from 0.25 to 2
- landmark_ids: int32 [1024], replicated, may hold values from 0 to 65535, as said below
Outputs:
- features: bfloat16 [65536, 1024], P(('grp', 'dev'))
Inputs may be any that keep to these rules, and one draw needn't show every extreme that they name: `landmark_ids`: sorted ascending, all distinct.
All inputs are finite; a program needn't handle non-finite values.
Results may differ from a plain program's by a relative error of at most 0.0015.
Values may be sent and summed in bfloat16 or wider, within the bound.
No kernel may reach another device: no remote copies, remote signals or barrier semaphores. Data moves between devices by JAX's collectives and lax.ppermute only.
A program may use at most 128 MiB of HBM per device.

v0:
```python
import jax
import jax.numpy as jnp
from jax import lax
from jax.sharding import PartitionSpec as P


def kernel_block(left, right):
    left_sq = jnp.sum(jnp.square(left.astype(jnp.float32)), axis=1)
    right_sq = jnp.sum(jnp.square(right.astype(jnp.float32)), axis=1)
    inner = jnp.dot(left, right.T, preferred_element_type=jnp.float32)
    width = left.shape[1]
    return jnp.exp(-(left_sq[:, None] + right_sq[None, :] - 2.0 * inner) / (2.0 * width))


def shards(points, ridge, landmark_ids):
    count = points.shape[0]
    start = lax.axis_index(("grp", "dev")) * count
    offset = landmark_ids - start
    inside = (offset >= 0) & (offset < count)
    picked = points[jnp.clip(offset, 0, count - 1)]
    filled = jnp.where(inside[:, None], picked.astype(jnp.float32), 0.0)
    marks = lax.psum(filled, ("grp", "dev")).astype(jnp.bfloat16)
    core = kernel_block(marks, marks) + jnp.diag(ridge)
    lower = jnp.linalg.cholesky(core)
    cross = kernel_block(points, marks)
    raw = lax.linalg.triangular_solve(lower, cross, left_side=False, lower=True, transpose_a=True)
    total_rows = count * lax.axis_size(("grp", "dev"))
    totals, squares = lax.psum(
        (jnp.sum(raw, axis=0), jnp.sum(jnp.square(raw), axis=0)), ("grp", "dev")
    )
    mean = totals / total_rows
    var = jnp.maximum(squares / total_rows - jnp.square(mean), 0.0)
    centered = raw - mean[None, :]
    return (centered / jnp.sqrt(var + 1e-05)[None, :]).astype(jnp.bfloat16)


def solution(mesh):
    placed = (P(("grp", "dev"), None), P(), P())
    return jax.shard_map(
        shards, mesh=mesh, in_specs=placed, out_specs=P(("grp", "dev"), None), check_vma=False
    )
```

profile of v0, /device:TPU:0, one launch (start us, length us, event | category | flops | bytes accessed | tf_op | source)
XLA Modules:
  0.0 495.3 jit_solution(2860757767389505931)
XLA Ops:
  1.4 1.6 multiply_reduce_fusion.1
  3.0 4.9 gather_fusion
  8.1 53.3 %all-reduce.3 = bf16[1024,256]{1,0:T(8,128)(2,1)S(1)} all-reduce(f32[1024,256]{1,0:T(8,128)S(1)} %convert_select_fusion), channel_id=1, replica_groups=mesh['grp'=4,'dev'=8] {'grp','dev'}, use_global_device_ids=true, to_apply=%region_1.2 | all-reduce | flops 262144 | bytes 1572864 | tf_op jit(solution)/shard_map/psum | solution.py:22
  61.6 4.3 fusion.2
  66.0 5.6 %subtract_negate_fusion = (f32[1024,1024]{0,1:T(8,128)}, f32[1024,1024]{0,1:T(8,128)}, f32[1024,1024]{0,1:T(8,128)}) fusion(f32[1024]{0:T(1024)S(1)} %multiply_reduce_fusion.2, bf16[1024,256]{1,0:T(8,128)(2,1)S(1)} %all-reduce.3), kind=kOutput, calls=%fused_computation.27 | convolution fusion | flops 541065216 | bytes 13111296 | tf_op jit(solution)/shard_map/dot_general | solution.py:10
  71.6 5.4 %copy.5 = f32[1024,1024]{1,0:T(8,128)} copy(f32[1024,1024]{0,1:T(8,128)} %get-tuple-element.76) | data formatting | bytes 8388608 | tf_op jit(solution)/shard_map/neg | solution.py:12
  76.9 5.3 %copy.6 = f32[1024,1024]{1,0:T(8,128)} copy(f32[1024,1024]{0,1:T(8,128)} %get-tuple-element.77) | data formatting | bytes 8388608 | tf_op jit(solution)/shard_map/add | solution.py:12
  82.3 6.3 %fusion.16 = f32[1024,1024]{1,0:T(8,128)S(1)} fusion(f32[1024,1024]{1,0:T(8,128)} %copy.6, f32[1024,1024]{1,0:T(8,128)} %copy.5, f32[1024,1024]{0,1:T(8,128)} %get-tuple-element.78, f32[1024]{0:T(1024)S(1)} %copy-done.5), kind=kLoop, calls=%fused_computation.24 | loop fusion | flops 13631488 | bytes 16781312 | tf_op jit(solution)/shard_map/jit(cholesky)/div | solution.py:24
  88.6 2.0 copy-done.2
  90.6 11.7 %cholesky.222 = f32[128,128]{1,0:T(8,128)S(1)} custom-call(f32[128,128]{1,0:T(8,128)S(1)} %cholesky.577), custom_call_target="Cholesky" | custom-call | tf_op jit(solution)/shard_map/jit(cholesky)/cholesky | solution.py:24
  102.4 9.8 %custom-call.62 = f32[1,128,128]{1,2,0:T(8,128)S(1)} custom-call(f32[1,128,128]{2,1,0:T(8,128)S(1)} %get-tuple-element.73), custom_call_target="InvertDiagBlocksLowerTriangular" | custom-call | tf_op jit(solution)/shard_map/jit(cholesky)/cholesky | solution.py:24
  112.2 2.5 cholesky.254
  114.7 2.3 constant_dynamic-update-slice_fusion.32
  117.0 1.5 convolution_subtract_fusion.5
  118.6 11.7 %cholesky.243 = f32[128,128]{1,0:T(8,128)S(1)} custom-call(f32[128,128]{1,0:T(8,128)S(1)} %cholesky.581), custom_call_target="Cholesky" | custom-call | tf_op jit(solution)/shard_map/jit(cholesky)/cholesky | solution.py:24
  132.9 10.2 %custom-call.63 = f32[1,128,128]{1,2,0:T(8,128)S(1)} custom-call(f32[1,128,128]{2,1,0:T(8,128)S(1)} %get-tuple-element.70), custom_call_target="InvertDiagBlocksLowerTriangular" | custom-call | tf_op jit(solution)/shard_map/jit(cholesky)/cholesky | solution.py:24
  143.1 1.2 convolution_dynamic-update-slice_fusion.1
  144.3 2.1 convolution_subtract_fusion.6
  146.4 11.7 %cholesky.466 = f32[128,128]{1,0:T(8,128)S(1)} custom-call(f32[128,128]{1,0:T(8,128)S(1)} %cholesky.586), custom_call_target="Cholesky" | custom-call | tf_op jit(solution)/shard_map/jit(cholesky)/cholesky | solution.py:24
  160.1 9.8 %custom-call.64 = f32[1,128,128]{1,2,0:T(8,128)S(1)} custom-call(f32[1,128,128]{2,1,0:T(8,128)S(1)} %get-tuple-element.67), custom_call_target="InvertDiagBlocksLowerTriangular" | custom-call | tf_op jit(solution)/shard_map/jit(cholesky)/cholesky | solution.py:24
  169.9 1.1 convolution_dynamic-update-slice_fusion.2
  171.0 2.3 convolution_subtract_fusion.7
  173.4 11.9 %cholesky.485 = f32[128,128]{1,0:T(8,128)S(1)} custom-call(f32[128,128]{1,0:T(8,128)S(1)} %cholesky.591), custom_call_target="Cholesky" | custom-call | tf_op jit(solution)/shard_map/jit(cholesky)/cholesky | solution.py:24
  187.2 9.8 %custom-call.65 = f32[1,128,128]{1,2,0:T(8,128)S(1)} custom-call(f32[1,128,128]{2,1,0:T(8,128)S(1)} %get-tuple-element.64), custom_call_target="InvertDiagBlocksLowerTriangular" | custom-call | tf_op jit(solution)/shard_map/jit(cholesky)/cholesky | solution.py:24
  198.1 2.3 convolution_subtract_fusion.8
  200.4 11.7 %cholesky.504 = f32[128,128]{1,0:T(8,128)S(1)} custom-call(f32[128,128]{1,0:T(8,128)S(1)} %cholesky.596), custom_call_target="Cholesky" | custom-call | tf_op jit(solution)/shard_map/jit(cholesky)/cholesky | solution.py:24
  214.0 9.8 %custom-call.66 = f32[1,128,128]{1,2,0:T(8,128)S(1)} custom-call(f32[1,128,128]{2,1,0:T(8,128)S(1)} %get-tuple-element.61), custom_call_target="InvertDiagBlocksLowerTriangular" | custom-call | tf_op jit(solution)/shard_map/jit(cholesky)/cholesky | solution.py:24
  224.8 2.5 convolution_subtract_fusion.9
  227.4 11.7 %cholesky.524 = f32[128,128]{1,0:T(8,128)S(1)} custom-call(f32[128,128]{1,0:T(8,128)S(1)} %cholesky.601), custom_call_target="Cholesky" | custom-call | tf_op jit(solution)/shard_map/jit(cholesky)/cholesky | solution.py:24
  241.0 9.8 %custom-call.67 = f32[1,128,128]{1,2,0:T(8,128)S(1)} custom-call(f32[1,128,128]{2,1,0:T(8,128)S(1)} %get-tuple-element.58), custom_call_target="InvertDiagBlocksLowerTriangular" | custom-call | tf_op jit(solution)/shard_map/jit(cholesky)/cholesky | solution.py:24
  251.8 2.1 convolution_subtract_fusion.10
  253.9 11.7 %cholesky.544 = f32[128,128]{1,0:T(8,128)S(1)} custom-call(f32[128,128]{1,0:T(8,128)S(1)} %cholesky.606), custom_call_target="Cholesky" | custom-call | tf_op jit(solution)/shard_map/jit(cholesky)/cholesky | solution.py:24
  267.5 10.2 %custom-call.68 = f32[1,128,128]{1,2,0:T(8,128)S(1)} custom-call(f32[1,128,128]{2,1,0:T(8,128)S(1)} %get-tuple-element.55), custom_call_target="InvertDiagBlocksLowerTriangular" | custom-call | tf_op jit(solution)/shard_map/jit(cholesky)/cholesky | solution.py:24
  278.6 1.8 convolution_subtract_fusion.11
  280.4 11.7 %cholesky.562 = f32[128,128]{1,0:T(8,128)S(1)} custom-call(f32[128,128]{1,0:T(8,128)S(1)} %convolution_subtract_fusion.11), custom_call_target="Cholesky" | custom-call | tf_op jit(solution)/shard_map/jit(cholesky)/cholesky | solution.py:24
  293.9 4.9 select_select_fusion
  298.8 22.5 %while.1 = (s32[]{:T(128)}, f32[1024,1024]{1,0:T(8,128)}, s32[8,2]{0,1:T(2,128)S(1)}, f32[8,128,128]{2,1,0:T(8,128)S(1)}, s32[]{:T(128)}) while((s32[]{:T(128)}, f32[1024,1024]{1,0:T(8,128)}, s32[8,2]{0,1:T(2,128)S(1)}, f32[8,128,128]{2,1,0:T(8,128)S(1)}, s32[]{:T(128)}) %tuple.61), condition=%wide.while_cond, body=%wide.while_body.sunk | while | flops 2 | bytes 131189 | solution.py:26
  299.4 2.2 bitcast_dynamic-update-slice_fusion.2
  302.2 2.2 bitcast_dynamic-update-slice_fusion.2
  305.0 2.2 bitcast_dynamic-update-slice_fusion.2
  307.8 2.2 bitcast_dynamic-update-slice_fusion.2
  310.6 2.2 bitcast_dynamic-update-slice_fusion.2
  313.5 2.2 bitcast_dynamic-update-slice_fusion.2
  316.3 2.2 bitcast_dynamic-update-slice_fusion.2
  319.1 2.1 bitcast_dynamic-update-slice_fusion.2
  321.2 78.8 %custom-call.69 = f32[8,128,128]{1,2,0:T(8,128)S(1)} custom-call(f32[8,128,128]{2,1,0:T(8,128)S(1)} %get-tuple-element.12), custom_call_target="InvertDiagBlocksLowerTriangular" | custom-call | tf_op jit(solution)/shard_map/triangular_solve | solution.py:26
  400.0 2.7 constant_dynamic-update-slice_fusion.17
  402.8 2.5 convolution_subtract_fusion.4
  405.3 1.3 constant_dynamic-update-slice_fusion.16
  406.6 2.3 convolution_subtract_fusion.3
  408.9 1.3 constant_dynamic-update-slice_fusion.15
  410.2 3.1 fusion.23
  413.3 2.3 constant_dynamic-update-slice_fusion.14
  415.6 5.0 %fusion.26 = f32[2048,128]{0,1:T(8,128)} fusion(f32[2048,128]{0,1:T(8,128)} %get-tuple-element.84, f32[2048,128]{0,1:T(8,128)S(1)} %get-tuple-element.83, f32[2048,128]{0,1:T(8,128)S(1)} %get-tuple-element.82, f32[2048,128]{0,1:T(8,128)S(1)} %get-tuple-element.81, f32[2048,1024]{0,1:T(8,128)S(1)} %bitcast.124, f32[1024,1024]{1,0:T(8,128)} %get-tuple-element.131), kind=kOutput, calls=%fused_computation.42 | convolution fusion | flops 1614020608 | bytes 6553600 | tf_op jit(solution)/shard_map/triangular_solve | solution.py:26
  420.6 2.4 constant_dynamic-update-slice_fusion.13
  423.0 4.3 convolution_subtract_fusion.2
  427.3 1.1 constant_dynamic-update-slice_fusion.12
  428.5 4.6 convolution_subtract_fusion
  434.2 5.8 %convolution_subtract_fusion.1 = f32[2048,128]{0,1:T(8,128)S(1)} fusion(f32[2048,896]{0,1:T(8,128)S(1)} %get-tuple-element.27, f32[2048,1024]{0,1:T(8,128)S(1)} %bitcast.124, f32[1024,1024]{1,0:T(8,128)} %get-tuple-element.131), kind=kOutput, calls=%fused_computation.38 | convolution fusion | flops 2818834432 | bytes 9895936 | tf_op jit(solution)/shard_map/triangular_solve | solution.py:26
  439.9 1.1 convolution_dynamic-update-slice_fusion
  442.1 2.1 copy-done
  444.3 38.9 %all-reduce.1 = (f32[1024]{0:T(1024)S(1)}, f32[1024]{0:T(1024)S(1)}) all-reduce(f32[1024]{0:T(1024)S(1)} %get-tuple-element.14, f32[1024]{0:T(1024)S(1)} %get-tuple-element.13), channel_id=1, replica_groups=mesh['grp'=4,'dev'=8] {'grp','dev'}, use_global_device_ids=true, to_apply=%region_22.23 | all-reduce | flops 2048 | bytes 16384 | tf_op jit(solution)/shard_map/psum | solution.py:28
  483.1 5.3 %divide_convert_fusion = bf16[2048,1024]{0,1:T(8,128)(2,1)} fusion(f32[2048,1024]{0,1:T(8,128)} %copy-done, f32[1024]{0:T(1024)S(1)} %get-tuple-element.75, f32[1024]{0:T(1024)S(1)} %get-tuple-element.74), kind=kLoop, calls=%fused_computation.7 | loop fusion | flops 6291456 | bytes 12591104 | tf_op jit(solution)/shard_map/convert_element_type | solution.py:34
  488.5 6.4 %copy.7 = bf16[2048,1024]{1,0:T(8,128)(2,1)} copy(bf16[2048,1024]{0,1:T(8,128)(2,1)} %divide_convert_fusion) | data formatting | bytes 8388608 | tf_op jit(solution)/shard_map/convert_element_type | solution.py:34
  (67 shorter events, 21.9 us)
Async XLA Ops:
  3.0 58.6 %copy-start.1 = (bf16[2048,256]{1,0:T(8,128)(2,1)S(1)}, bf16[2048,256]{1,0:T(8,128)(2,1)}, u32[]{:S(2)}) copy-start(bf16[2048,256]{1,0:T(8,128)(2,1)} %param.3) | copy-start | bytes 3145732
  76.9 5.4 %copy-start.5 = (f32[1024]{0:T(1024)S(1)}, f32[1024]{0:T(1024)}, u32[]{:S(2)}) copy-start(f32[1024]{0:T(1024)} %param.4) | copy-start | bytes 12292
  88.6 2.0 copy-start.2
  400.0 5.3 %copy-start.3 = (f32[8,128,128]{1,2,0:T(8,128)}, f32[8,128,128]{1,2,0:T(8,128)S(1)}, u32[]{:S(2)}) copy-start(f32[8,128,128]{1,2,0:T(8,128)S(1)} %custom-call.69) | copy-start | bytes 1572868
  400.0 6.6 %slice-start = ((s8[8388608]{0:T(1024)(128)(4,1)}), s8[4194304]{0:T(1024)(128)(4,1)S(1)}, s32[]{:S(2)}) async-start(s8[8388608]{0:T(1024)(128)(4,1)} %bitcast.123), calls=%async_computation | async-start | bytes 8388608
  402.8 3.8 slice-start.1
  406.6 2.3 copy-start.4
  441.0 3.2 copy-start
where the time goes:
time: 502 us; the launch traced here: 495 us
  other arithmetic  272 us (54%)
  blocking collectives  92.1 us (18%)
  matrix products  74 us (15%)
  local copies, waits for them, and re-layouts  51 us (10%)
  between operations  5.8 us (1%)
    another operation x30, other arithmetic, shards(): lower = jnp.linalg.cholesky(core)  172 us
    another operation x3, other arithmetic, shards(): lax.linalg.triangular_solve(lower, cross, left_side=False, lower=True, tr...  83.7 us
    psum x1, blocking collectives, shards(): marks = lax.psum(filled, ('grp', 'dev')).astype(jnp.bfloat16)  53.3 us
    another operation x15, matrix products, shards(): lax.linalg.triangular_solve(lower, cross, left_side=False, lower=True, tr...  40.8 us
    psum x1, blocking collectives, shards(): lax.psum((jnp.sum(raw, axis=0), jnp.sum(jnp.square(raw), axis=0)), ('grp'...  38.9 us
    another operation x14, matrix products, shards(): lower = jnp.linalg.cholesky(core)  23.2 us
    another operation x24, local copies, waits for them, and re-layouts  22.3 us

commit v1 on v0

v1 whole, which is shorter than its diff:
```python
import functools
import math

import jax
import jax.numpy as jnp
from jax import lax
from jax.experimental import pallas as pl
from jax.experimental.pallas import tpu as pltpu
from jax.sharding import PartitionSpec as P

AXES = ("grp", "dev")
B = 128
S = 256
TILE = 512


def split(x):
    hi = x.astype(jnp.bfloat16)
    return hi, (x - hi.astype(jnp.float32)).astype(jnp.bfloat16)


def dot_nt(left, right):
    return lax.dot_general(left, right, (((1,), (1,)), ((), ())), preferred_element_type=jnp.float32)


def left3(x):
    hi, lo = split(x)
    return jnp.concatenate([hi, lo, hi], axis=1)


def right3(x):
    hi, lo = split(x)
    return jnp.concatenate([hi, hi, lo], axis=1)


def factor_block(a_ref, sub, lane):
    n = B // 8
    rows = [a_ref[8 * t:8 * t + 8, :] for t in range(n)]
    out = []
    for k in range(n):
        first = 8 * k
        group = rows[k]
        cols = [jnp.broadcast_to(group[:, first + b:first + b + 1], (8, B)) for b in range(8)]
        below = {
            t: [jnp.broadcast_to(rows[t][:, first + j:first + j + 1], (8, B)) for j in range(8)]
            for t in range(k + 1, n)
        }
        pivot = (lane >= first) & (lane < first + 8)
        start = jnp.where(pivot, (lane - first == sub).astype(jnp.float32), group)
        s = {(a, b): jnp.broadcast_to(cols[b][a:a + 1, :], (8, B)) for b in range(8) for a in range(b + 1)}
        y = [jnp.broadcast_to(start[i:i + 1, :], (8, B)) for i in range(8)]
        follow = k + 1 < n
        if follow:
            z = list(below[k + 1])
            acc = jnp.where(pivot, 0.0, rows[k + 1])
        inv = []
        for j in range(8):
            r = lax.rsqrt(s[(j, j)])
            inv.append(r)
            for b in range(j + 1, 8):
                s[(j, b)] = s[(j, b)] * r
            y[j] = y[j] * r
            if follow:
                z[j] = z[j] * r
                acc = acc - z[j] * y[j]
            for b in range(j + 1, 8):
                for a in range(j + 1, b + 1):
                    s[(a, b)] = s[(a, b)] - s[(j, a)] * s[(j, b)]
            for b in range(j + 1, 8):
                y[b] = y[b] - s[(j, b)] * y[j]
                if follow:
                    z[b] = z[b] - s[(j, b)] * z[j]
        w = y[7]
        for i in range(7):
            w = jnp.where(sub == i, y[i], w)
        out.append(jnp.where(lane < first + 8, w, 0.0))
        if follow:
            rows[k + 1] = acc
        if k + 2 < n:
            q = [None] * 8
            for j in range(7, -1, -1):
                v = y[j]
                for i in range(j + 1, 8):
                    v = v - s[(j, i)] * q[i]
                q[j] = v * inv[j]
            for t in range(k + 2, n):
                v = jnp.where(pivot, 0.0, rows[t])
                for j in range(8):
                    v = v - below[t][j] * q[j]
                rows[t] = v
    return out


def square_sums(x):
    hi, lo = split(jnp.square(x.astype(jnp.float32)))
    both = jnp.concatenate([hi, lo], axis=1)
    return dot_nt(jnp.ones((8, both.shape[1]), jnp.bfloat16), both), dot_nt(both, jnp.ones((B, both.shape[1]), jnp.bfloat16))


def factor(a_ref, d_ref, w3_ref, l3_ref):
    nb, m, _ = a_ref.shape
    sub = lax.broadcasted_iota(jnp.int32, (8, B), 0)
    lane = lax.broadcasted_iota(jnp.int32, (8, B), 1)

    def panel(p, carry):
        d_ref[0] = a_ref[p, pl.ds(pl.multiple_of(p * B, B), B), :]
        for k, rows in enumerate(factor_block(d_ref.at[0], sub, lane)):
            d_ref[0, 8 * k:8 * k + 8, :] = rows

        def finish(q):
            w = d_ref[0]
            top = (q + 1) * B
            step, odd = divmod(q, S // B)
            if top < m:
                block = dot_nt(left3(a_ref[q, top:, :]), right3(w))
                hi, lo = split(block)
                if (step + 1) * S < m:
                    at = step * 3 * S + odd * B
                    l3_ref[top:, at:at + B] = hi
                    l3_ref[top:, at + S:at + S + B] = hi
                    l3_ref[top:, at + 2 * S:at + 2 * S + B] = lo
                left = jnp.concatenate([hi, lo, hi], axis=1)
                right = jnp.concatenate([hi, hi, lo], axis=1)
                for j in range(q + 1, nb):
                    o = (j - q - 1) * B
                    a_ref[j, j * B:, :] -= dot_nt(left[o:], right[o:o + B])
            if odd == 0:
                d_ref[1] = w
                d_ref[2] = block[:B]
            else:
                w0 = d_ref[1]
                inner = lax.dot_general(left3(d_ref[2]), jnp.concatenate([split(w0)[0], split(w0)[0], split(w0)[1]], axis=0), (((1,), (0,)), ((), ())), preferred_element_type=jnp.float32)
                hi, lo = split(inner)
                corner = -lax.dot_general(left3(w), jnp.concatenate([hi, hi, lo], axis=0), (((1,), (0,)), ((), ())), preferred_element_type=jnp.float32)
                upper = jnp.concatenate([w0, jnp.zeros_like(w0)], axis=1)
                lower = jnp.concatenate([corner, w], axis=1)
                w3_ref[step * S:(step + 1) * S, :] = right3(jnp.concatenate([upper, lower], axis=0))

        for q in range(nb):
            pl.when(p == q)(functools.partial(finish, q))
        return carry

    lax.fori_loop(0, nb, panel, 0)


def kernel(src_ref, dst_ref, rows_ref, points_ref, ridge_ref, raw_ref, stat_ref,
           marks_ref, packed_ref, a_ref, d_ref, w3_ref, l3_ref, r3_ref):
    i = pl.program_id(0)
    m, width = marks_ref.shape
    scale = 1.0 / (2.0 * width)
    cap = packed_ref.shape[1] - m

    @pl.when(i == 0)
    def _():
        def place(d, carry):
            rows = rows_ref[pl.ds(pl.multiple_of(src_ref[d] * cap, cap), cap), :].astype(jnp.float32)
            for c in range(width // B):
                packed_ref[c, pl.ds(dst_ref[d], cap), :] = rows[:, c * B:(c + 1) * B]
            return carry
        lax.fori_loop(0, src_ref.shape[0], place, 0)
        marks_ref[...] = jnp.concatenate([packed_ref[c, :m] for c in range(width // B)], axis=1).astype(jnp.bfloat16)
        marks = marks_ref[...]
        along, down = square_sums(marks)
        stat_ref[...] = jnp.zeros_like(stat_ref)
        d_ref[3, 0:8, :] = jnp.zeros((8, B), jnp.float32)
        for j in range(m // B):
            inner = dot_nt(marks, marks[j * B:(j + 1) * B])
            block = jnp.exp(-(down + along[0:1, j * B:(j + 1) * B] - 2.0 * inner) * scale)
            a_ref[j] = block
            row = lax.broadcasted_iota(jnp.int32, (B, B), 0)
            col = lax.broadcasted_iota(jnp.int32, (B, B), 1)
            a_ref[j, j * B:(j + 1) * B, :] += jnp.where(row == col, ridge_ref[0:1, j * B:(j + 1) * B], 0.0)
        factor(a_ref, d_ref, w3_ref, l3_ref)

    points = points_ref[...]
    _, down = square_sums(points)
    down = jnp.concatenate([down] * (S // B), axis=1)
    marks = marks_ref[...]
    along, _ = square_sums(marks)
    count = points.shape[0]
    before = (i * count).astype(jnp.float32)
    share = count / (before + count)
    for p in range(m // S):
        here = slice(p * S, (p + 1) * S)
        inner = dot_nt(points, marks[here])
        cross = jnp.exp(-(down + along[0:1, here] - 2.0 * inner) * scale)
        if p:
            cross = cross - dot_nt(r3_ref[:, :p * 3 * S], l3_ref[here, :p * 3 * S])
        raw = dot_nt(left3(cross), w3_ref[here, :])
        raw_ref[:, here] = raw
        if p + 1 < m // S:
            r3_ref[:, p * 3 * S:(p + 1) * 3 * S] = left3(raw)
        mean = jnp.mean(raw, axis=0, keepdims=True)
        spread = jnp.sum(jnp.square(raw - mean), axis=0, keepdims=True)
        delta = mean - stat_ref[0:1, here]
        stat_ref[1:2, here] += spread + jnp.square(delta) * (before * share)
        stat_ref[0:1, here] += delta * share


def exchange(x, bit):
    dev = lax.axis_size("dev")
    axis, flip = ("dev", bit) if bit < dev else ("grp", bit // dev)
    size = lax.axis_size(axis)
    return lax.ppermute(x, axis, [(k, k ^ flip) for k in range(size)])


def shards(points, ridge, landmark_ids):
    count, width = points.shape
    m = landmark_ids.shape[0]
    devices = lax.axis_size(AXES)
    me = lax.axis_index(AXES)
    mean = m / devices
    cap = min(m, 16 * math.ceil((mean + 5.6 * math.sqrt(mean)) / 16))
    bits = [1 << b for b in range(devices.bit_length() - 1)]
    order = bits[1:] + bits[:1]

    bounds = jnp.sum(landmark_ids[None, :] < (jnp.arange(devices + 1) * count)[:, None], axis=1, dtype=jnp.int32)
    low = bounds[:-1]
    fits = jnp.max(bounds[1:] - low) <= cap

    def packed(points, ids):
        mine = lax.dynamic_slice(jnp.pad(ids, (0, cap)), (low[me],), (cap,))
        rows = points[jnp.clip(mine - me * count, 0, count - 1)]
        for bit in order:
            rows = jnp.concatenate([rows, exchange(rows, bit)], axis=0)
        far = jnp.arange(devices, dtype=jnp.int32) ^ me
        place = jnp.zeros_like(far)
        for k, bit in enumerate(order):
            place = place + jnp.where((far & bit) != 0, 1 << k, 0)
        return rows, place, low

    def summed(points, ids):
        offset = ids - me * count
        inside = (offset >= 0) & (offset < count)
        picked = points[jnp.clip(offset, 0, count - 1)]
        rows = lax.psum(jnp.where(inside[:, None], picked.astype(jnp.float32), 0.0), AXES).astype(points.dtype)
        rows = jnp.pad(rows, ((0, max(0, devices * cap - m)), (0, 0)))
        place = jnp.arange(devices, dtype=jnp.int32) % (m // cap)
        return rows, place, place * cap

    rows, src, dst = lax.cond(fits, packed, summed, points, landmark_ids)

    raw, stat = pl.pallas_call(
        kernel,
        grid_spec=pltpu.PrefetchScalarGridSpec(
            num_scalar_prefetch=2,
            grid=(count // TILE,),
            in_specs=[
                pl.BlockSpec(rows.shape, lambda i, *_: (0, 0), pipeline_mode=pl.Buffered(1)),
                pl.BlockSpec((TILE, width), lambda i, *_: (i, 0)),
                pl.BlockSpec((1, m), lambda i, *_: (0, 0)),
            ],
            out_specs=[
                pl.BlockSpec((TILE, m), lambda i, *_: (i, 0)),
                pl.BlockSpec((8, m), lambda i, *_: (0, 0)),
            ],
            scratch_shapes=[
                pltpu.VMEM((m, width), jnp.bfloat16),
                pltpu.VMEM((width // B, m + cap, B), jnp.float32),
                pltpu.VMEM((m // B, m, B), jnp.float32),
                pltpu.VMEM((4, B, B), jnp.float32),
                pltpu.VMEM((m, 3 * S), jnp.bfloat16),
                pltpu.VMEM((m, 3 * (m - S)), jnp.bfloat16),
                pltpu.VMEM((TILE, 3 * (m - S)), jnp.bfloat16),
            ],
        ),
        out_shape=(jax.ShapeDtypeStruct((count, m), jnp.float32), jax.ShapeDtypeStruct((8, m), jnp.float32)),
        compiler_params=pltpu.CompilerParams(vmem_limit_bytes=60 << 20, dimension_semantics=("arbitrary",)),
        name="nystrom",
    )(src, dst, rows, points, ridge[None, :])

    stat = stat[:2]
    total = count
    for bit in bits:
        other = exchange(stat, bit)
        delta = other[0] - stat[0]
        stat = jnp.stack([0.5 * (stat[0] + other[0]), stat[1] + other[1] + jnp.square(delta) * (0.5 * total)])
        total *= 2
    var = stat[1] / total
    return ((raw - stat[0][None, :]) / jnp.sqrt(var + 1e-05)[None, :]).astype(jnp.bfloat16)


def solution(mesh):
    placed = (P(AXES, None), P(), P())
    return jax.shard_map(shards, mesh=mesh, in_specs=placed, out_specs=P(AXES, None), check_vma=False)
```

time: 502 us -> 128 us (0.25); the launches traced: 495 us -> 128 us
  other arithmetic: 272 us -> 10.1 us
  blocking collectives: 92.1 us -> 0 us
  matrix products: 74 us -> 0 us
  Pallas kernels: 0 us -> 69.4 us
  local copies, waits for them, and re-layouts: 51 us -> 7.48 us
  waiting for transfers between devices: 0 us -> 19.5 us
  starting transfers between devices: 0 us -> 18.7 us
  between operations: 5.8 us -> 0.72 us
    another operation x33 -> x4, other arithmetic: 256 us -> 0.05 us  [shards(): jnp.stack([0.5 * (stat[0] + other[0]), stat[1] + other[1] + jnp.square(de...]
    psum x2 -> x0, blocking collectives: 92.1 us -> none  [the longest x1 53.3 us: shards(): marks = lax.psum(filled, ('grp', 'dev')).astype(jnp.bfloat16)]
    pallas_call x0 -> x1, Pallas kernels: none -> 69.4 us  [shards(): pl.pallas_call(kernel, grid_spec=pltpu.PrefetchScalarGridSpec(num_scalar_...]
    another operation x29 -> x0, matrix products: 64.1 us -> none  [the longest x15 40.8 us: shards(): lax.linalg.triangular_solve(lower, cross, left_side=False, lower=True, tr...]
    another operation x33 -> x0, local copies, waits for them, and re-layouts: 24.9 us -> none
    ppermute x0 -> x10, waiting for transfers between devices: none -> 19.5 us  [exchange(): return lax.ppermute(x, axis, [(k, k ^ flip) for k in range(size)])]
    ppermute x0 -> x10, starting transfers between devices: none -> 18.7 us  [exchange(): return lax.ppermute(x, axis, [(k, k ^ flip) for k in range(size)])]
    dot_general x2 -> x0, matrix products: 9.96 us -> none  [kernel_block(): inner = jnp.dot(left, right.T, preferred_element_type=jnp.float32)]
  transfers between devices with their start and end apart: 0 -> 10, of which waited for: 0 -> 10; matrix products, arithmetic and copies ran while one was open for 0% -> 2% of each run, Pallas kernels for 0% -> 0%
where the time goes in v1:
time: 128 us
  Pallas kernels  69.4 us (54%)
  waiting for transfers between devices  19.5 us (15%)
  starting transfers between devices  18.7 us (15%)
  other arithmetic  10.1 us (8%)
  local copies, waits for them, and re-layouts  7.48 us (6%)
  loops' own time  1.98 us (2%)
    pallas_call x1, Pallas kernels, shards(): pl.pallas_call(kernel, grid_spec=pltpu.PrefetchScalarGridSpec(num_scalar_...  69.4 us
    ppermute x10, waiting for transfers between devices, exchange(): return lax.ppermute(x, axis, [(k, k ^ flip) for k in range(size)])  19.5 us
    ppermute x10, starting transfers between devices, exchange(): return lax.ppermute(x, axis, [(k, k ^ flip) for k in range(size)])  18.7 us
    convert_element_type x1, other arithmetic, shards(): ((raw - stat[0][None, :]) / jnp.sqrt(var + 1e-05)[None, :]).astype(jnp.bf...  6.69 us
  transfers between devices with their start and end apart: 10, of which 10 were waited for; matrix products, arithmetic and copies ran while one was open for 2% of the time, Pallas kernels for 0%

profile of v1, /device:TPU:0, one launch (start us, length us, event | category | flops | bytes accessed | tf_op | source)
XLA Modules:
  0.0 127.8 jit_solution(4178511364125625703)
XLA Ops:
  0.0 0.9 convert_reduce_fusion
  0.9 0.7 fusion.10
  2.3 30.6 %conditional.1 = (bf16[2048,256]{1,0:T(8,128)(2,1)}, s32[32]{0:T(128)S(1)}, s32[32]{0:T(128)S(1)}) conditional(s32[]{:T(128)} %convert_element_type.18, (s32[]{:T(128)}, s32[1024]{0:T(1024)}, bf16[2048,256]{1,0:T(8,128)(2,1)}) %tuple.13, (s32[1024]{0:T(1024)}, s32[]{:T(128)}, s32[32]{0:T(128)S(1)}, bf16[2048,256]{1,0:T(8,128)(2,1)}) %tuple.14), branch_computations={%region_2.4_spmd, %region_4.5_spmd} | conditional | flops 1574855 | bytes 7677128 | solution.py:241
  2.3 0.6 dynamic_slice.4
  4.8 0.8 compare_select_fusion.1
  5.6 2.0 %gather_fusion = bf16[64,256]{1,0:T(8,128)(2,1)S(1)} fusion(bf16[2048,256]{1,0:T(8,128)(2,1)} %get-tuple-element.22, s32[1024]{0:T(1024)S(1)} %pad_clamp_fusion), kind=kCustom, calls=%fused_computation.1 | custom fusion | bytes 65792 | tf_op jit(solution)/shard_map/cond/branch_1_fun/gather | solution.py:223
  7.6 3.1 %collective-permute-start = (bf16[64,256]{1,0:T(8,128)(2,1)S(1)}, bf16[64,256]{1,0:T(8,128)(2,1)S(1)}, u32[]{:S(2)}, u32[]{:S(2)}) collective-permute-start(bf16[64,256]{1,0:T(8,128)(2,1)S(1)} %gather_fusion), channel_id=1, source_target_pairs={{0,2},{1,3},{2,0},{3,1},{4,6},{5,7},{6,4},{7,5},{8,10},{9,11},{10,... | collective-permute-start | bytes 98312 | tf_op jit(solution)/shard_map/cond/branch_1_fun/ppermute | solution.py:204
  10.7 1.9 %collective-permute-done = bf16[64,256]{1,0:T(8,128)(2,1)S(1)} collective-permute-done((bf16[64,256]{1,0:T(8,128)(2,1)S(1)}, bf16[64,256]{1,0:T(8,128)(2,1)S(1)}, u32[]{:S(2)}, u32[]{:S(2)}) %collective-permute-start) | collective-permute-done | bytes 32800 | tf_op jit(solution)/shard_map/cond/branch_1_fun/ppermute | solution.py:204
  12.6 3.0 %collective-permute-start.1 = (bf16[128,256]{1,0:T(8,128)(2,1)S(1)}, bf16[128,256]{1,0:T(8,128)(2,1)S(1)}, u32[]{:S(2)}, u32[]{:S(2)}) collective-permute-start(bf16[128,256]{1,0:T(8,128)(2,1)S(1)} %pad_maximum_fusion.2), channel_id=1, source_target_pairs={{0,4},{1,5},{2,6},{3,7},{4,0},{5,1},{6,2},{7,3},{8,12},{9,13},{10,... | collective-permute-start | bytes 196616 | tf_op jit(solution)/shard_map/cond/branch_1_fun/ppermute | solution.py:204
  15.7 2.2 %collective-permute-done.1 = bf16[128,256]{1,0:T(8,128)(2,1)S(1)} collective-permute-done((bf16[128,256]{1,0:T(8,128)(2,1)S(1)}, bf16[128,256]{1,0:T(8,128)(2,1)S(1)}, u32[]{:S(2)}, u32[]{:S(2)}) %collective-permute-start.1) | collective-permute-done | bytes 65568 | tf_op jit(solution)/shard_map/cond/branch_1_fun/ppermute | solution.py:204
  17.9 1.9 %collective-permute-start.2 = (bf16[256,256]{1,0:T(8,128)(2,1)S(1)}, bf16[256,256]{1,0:T(8,128)(2,1)S(1)}, u32[]{:S(2)}, u32[]{:S(2)}) collective-permute-start(bf16[256,256]{1,0:T(8,128)(2,1)S(1)} %pad_maximum_fusion.1), channel_id=1, source_target_pairs={{0,8},{8,0},{16,24},{24,16},{1,9},{9,1},{17,25},{25,17},{2,10},{10... | collective-permute-start | bytes 393224 | tf_op jit(solution)/shard_map/cond/branch_1_fun/ppermute | solution.py:204
  19.8 0.6 constant_dynamic-update-slice_fusion.4
  20.4 2.5 %collective-permute-done.2 = bf16[256,256]{1,0:T(8,128)(2,1)S(1)} collective-permute-done((bf16[256,256]{1,0:T(8,128)(2,1)S(1)}, bf16[256,256]{1,0:T(8,128)(2,1)S(1)}, u32[]{:S(2)}, u32[]{:S(2)}) %collective-permute-start.2) | collective-permute-done | bytes 131104 | tf_op jit(solution)/shard_map/cond/branch_1_fun/ppermute | solution.py:204
  23.0 1.9 %collective-permute-start.3 = (bf16[512,256]{1,0:T(8,128)(2,1)S(1)}, bf16[512,256]{1,0:T(8,128)(2,1)S(1)}, u32[]{:S(2)}, u32[]{:S(2)}) collective-permute-start(bf16[512,256]{1,0:T(8,128)(2,1)S(1)} %pad_maximum_fusion), channel_id=1, source_target_pairs={{0,16},{8,24},{16,0},{24,8},{1,17},{9,25},{17,1},{25,9},{2,18},{10... | collective-permute-start | bytes 786440 | tf_op jit(solution)/shard_map/cond/branch_1_fun/ppermute | solution.py:204
  24.9 0.6 constant_dynamic-update-slice_fusion.3
  25.5 0.6 constant_dynamic-update-slice_fusion.2
  26.1 0.7 constant_dynamic-update-slice_fusion.1
  26.8 2.6 %collective-permute-done.3 = bf16[512,256]{1,0:T(8,128)(2,1)S(1)} collective-permute-done((bf16[512,256]{1,0:T(8,128)(2,1)S(1)}, bf16[512,256]{1,0:T(8,128)(2,1)S(1)}, u32[]{:S(2)}, u32[]{:S(2)}) %collective-permute-start.3) | collective-permute-done | bytes 262176 | tf_op jit(solution)/shard_map/cond/branch_1_fun/ppermute | solution.py:204
  29.4 0.7 constant_dynamic-update-slice_fusion
  30.1 0.0 collective-permute-start.4
  30.2 1.9 %collective-permute-done.4 = bf16[1024,256]{1,0:T(8,128)(2,1)S(1)} collective-permute-done((bf16[1024,256]{1,0:T(8,128)(2,1)S(1)}, bf16[1024,256]{1,0:T(8,128)(2,1)S(1)}, u32[]{:S(2)}, u32[]{:S(2)}) %collective-permute-start.4) | collective-permute-done | bytes 524320 | tf_op jit(solution)/shard_map/cond/branch_1_fun/ppermute | solution.py:204
  32.1 0.8 constant_dynamic-update-slice_fusion.5
  32.9 69.4 %nystrom.1 = (f32[2048,1024]{1,0:T(8,128)}, f32[8,1024]{1,0:T(8,128)}) custom-call(s32[32]{0:T(128)S(1)} %get-tuple-element.31.src_ref, s32[32]{0:T(128)S(1)} %get-tuple-element.32.dst_ref, bf16[2048,256]{1,0:T(8,128)(2,1)} %get-tuple-element.33.rows_ref, bf16[2048,256]{1,0:T(8,128)(2,1)} %points_ref.1, f32[1,1024]{1,0:T(1,128)} %bitcast.6), custom_call_target="tpu_custom_call" | custom-call | tf_op jit(solution)/shard_map/nystrom/pallas_call | solution.py:243
  102.3 0.8 slice.56
  103.0 0.1 collective-permute-start.5
  103.1 1.0 collective-permute-done.5
  104.2 0.9 fusion.9
  105.1 2.0 %collective-permute-start.6 = (f32[2,1024]{1,0:T(2,128)S(1)}, f32[2,1024]{1,0:T(2,128)S(1)}, u32[]{:S(2)}, u32[]{:S(2)}) collective-permute-start(f32[2,1024]{1,0:T(2,128)S(1)} %pad_maximum_fusion.3), channel_id=1, source_target_pairs={{0,2},{1,3},{2,0},{3,1},{4,6},{5,7},{6,4},{7,5},{8,10},{9,11},{10,... | collective-permute-start | bytes 24584 | tf_op jit(solution)/shard_map/ppermute | solution.py:204
  107.0 1.7 %collective-permute-done.6 = f32[2,1024]{1,0:T(2,128)S(1)} collective-permute-done((f32[2,1024]{1,0:T(2,128)S(1)}, f32[2,1024]{1,0:T(2,128)S(1)}, u32[]{:S(2)}, u32[]{:S(2)}) %collective-permute-start.6) | collective-permute-done | bytes 8224 | tf_op jit(solution)/shard_map/ppermute | solution.py:204
  108.8 3.1 %collective-permute-start.7 = (f32[2,1024]{1,0:T(2,128)S(1)}, f32[2,1024]{1,0:T(2,128)S(1)}, u32[]{:S(2)}, u32[]{:S(2)}) collective-permute-start(f32[2,1024]{1,0:T(2,128)S(1)} %pad_maximum_fusion.4), channel_id=1, source_target_pairs={{0,4},{1,5},{2,6},{3,7},{4,0},{5,1},{6,2},{7,3},{8,12},{9,13},{10,... | collective-permute-start | bytes 24584 | tf_op jit(solution)/shard_map/ppermute | solution.py:204
  112.0 1.6 %collective-permute-done.7 = f32[2,1024]{1,0:T(2,128)S(1)} collective-permute-done((f32[2,1024]{1,0:T(2,128)S(1)}, f32[2,1024]{1,0:T(2,128)S(1)}, u32[]{:S(2)}, u32[]{:S(2)}) %collective-permute-start.7) | collective-permute-done | bytes 8224 | tf_op jit(solution)/shard_map/ppermute | solution.py:204
  113.6 1.7 %collective-permute-start.8 = (f32[2,1024]{1,0:T(2,128)S(1)}, f32[2,1024]{1,0:T(2,128)S(1)}, u32[]{:S(2)}, u32[]{:S(2)}) collective-permute-start(f32[2,1024]{1,0:T(2,128)S(1)} %pad_maximum_fusion.5), channel_id=1, source_target_pairs={{0,8},{8,0},{16,24},{24,16},{1,9},{9,1},{17,25},{25,17},{2,10},{10... | collective-permute-start | bytes 24584 | tf_op jit(solution)/shard_map/ppermute | solution.py:204
  115.4 2.0 %collective-permute-done.8 = f32[2,1024]{1,0:T(2,128)S(1)} collective-permute-done((f32[2,1024]{1,0:T(2,128)S(1)}, f32[2,1024]{1,0:T(2,128)S(1)}, u32[]{:S(2)}, u32[]{:S(2)}) %collective-permute-start.8) | collective-permute-done | bytes 8224 | tf_op jit(solution)/shard_map/ppermute | solution.py:204
  117.4 1.8 %collective-permute-start.9 = (f32[2,1024]{1,0:T(2,128)S(1)}, f32[2,1024]{1,0:T(2,128)S(1)}, u32[]{:S(2)}, u32[]{:S(2)}) collective-permute-start(f32[2,1024]{1,0:T(2,128)S(1)} %pad_maximum_fusion.6), channel_id=1, source_target_pairs={{0,16},{8,24},{16,0},{24,8},{1,17},{9,25},{17,1},{25,9},{2,18},{10... | collective-permute-start | bytes 24584 | tf_op jit(solution)/shard_map/ppermute | solution.py:204
  119.1 2.0 %collective-permute-done.9 = f32[2,1024]{1,0:T(2,128)S(1)} collective-permute-done((f32[2,1024]{1,0:T(2,128)S(1)}, f32[2,1024]{1,0:T(2,128)S(1)}, u32[]{:S(2)}, u32[]{:S(2)}) %collective-permute-start.9) | collective-permute-done | bytes 8224 | tf_op jit(solution)/shard_map/ppermute | solution.py:204
  121.1 6.7 %divide_convert_fusion = bf16[2048,1024]{1,0:T(8,128)(2,1)} fusion(f32[2048,1024]{1,0:T(8,128)} %get-tuple-element.34, f32[1024]{0:T(1024)S(1)} %bitcast.5, f32[1024]{0:T(1024)S(1)} %bitcast.4), kind=kLoop, calls=%fused_computation.34 | loop fusion | flops 6291456 | bytes 12591104 | tf_op jit(solution)/shard_map/convert_element_type | solution.py:280
  (14 shorter events, 0.2 us)
Async XLA Ops:
  7.6 5.0 %collective-permute-start = (bf16[64,256]{1,0:T(8,128)(2,1)S(1)}, bf16[64,256]{1,0:T(8,128)(2,1)S(1)}, u32[]{:S(2)}, u32[]{:S(2)}) collective-permute-start(bf16[64,256]{1,0:T(8,128)(2,1)S(1)} %gather_fusion), channel_id=1, source_target_pairs={{0,2},{1,3},{2,0},{3,1},{4,6},{5,7},{6,4},{7,5},{8,10},{9,11},{10,... | collective-permute-start | bytes 98312 | tf_op jit(solution)/shard_map/cond/branch_1_fun/ppermute | solution.py:204
  12.6 5.3 %collective-permute-start.1 = (bf16[128,256]{1,0:T(8,128)(2,1)S(1)}, bf16[128,256]{1,0:T(8,128)(2,1)S(1)}, u32[]{:S(2)}, u32[]{:S(2)}) collective-permute-start(bf16[128,256]{1,0:T(8,128)(2,1)S(1)} %pad_maximum_fusion.2), channel_id=1, source_target_pairs={{0,4},{1,5},{2,6},{3,7},{4,0},{5,1},{6,2},{7,3},{8,12},{9,13},{10,... | collective-permute-start | bytes 196616 | tf_op jit(solution)/shard_map/cond/branch_1_fun/ppermute | solution.py:204
  17.9 5.0 %collective-permute-start.2 = (bf16[256,256]{1,0:T(8,128)(2,1)S(1)}, bf16[256,256]{1,0:T(8,128)(2,1)S(1)}, u32[]{:S(2)}, u32[]{:S(2)}) collective-permute-start(bf16[256,256]{1,0:T(8,128)(2,1)S(1)} %pad_maximum_fusion.1), channel_id=1, source_target_pairs={{0,8},{8,0},{16,24},{24,16},{1,9},{9,1},{17,25},{25,17},{2,10},{10... | collective-permute-start | bytes 393224 | tf_op jit(solution)/shard_map/cond/branch_1_fun/ppermute | solution.py:204
  23.0 6.4 %collective-permute-start.3 = (bf16[512,256]{1,0:T(8,128)(2,1)S(1)}, bf16[512,256]{1,0:T(8,128)(2,1)S(1)}, u32[]{:S(2)}, u32[]{:S(2)}) collective-permute-start(bf16[512,256]{1,0:T(8,128)(2,1)S(1)} %pad_maximum_fusion), channel_id=1, source_target_pairs={{0,16},{8,24},{16,0},{24,8},{1,17},{9,25},{17,1},{25,9},{2,18},{10... | collective-permute-start | bytes 786440 | tf_op jit(solution)/shard_map/cond/branch_1_fun/ppermute | solution.py:204
  30.1 1.9 %collective-permute-start.4 = (bf16[1024,256]{1,0:T(8,128)(2,1)S(1)}, bf16[1024,256]{1,0:T(8,128)(2,1)S(1)}, u32[]{:S(2)}, u32[]{:S(2)}) collective-permute-start(bf16[1024,256]{1,0:T(8,128)(2,1)S(1)} %get-tuple-element.38), channel_id=1, source_target_pairs={{0,1},{1,0},{2,3},{3,2},{4,5},{5,4},{6,7},{7,6},{8,9},{9,8},{10,11... | collective-permute-start | bytes 1572872 | tf_op jit(solution)/shard_map/cond/branch_1_fun/ppermute | solution.py:204
  103.0 1.2 collective-permute-start.5
  105.1 3.7 %collective-permute-start.6 = (f32[2,1024]{1,0:T(2,128)S(1)}, f32[2,1024]{1,0:T(2,128)S(1)}, u32[]{:S(2)}, u32[]{:S(2)}) collective-permute-start(f32[2,1024]{1,0:T(2,128)S(1)} %pad_maximum_fusion.3), channel_id=1, source_target_pairs={{0,2},{1,3},{2,0},{3,1},{4,6},{5,7},{6,4},{7,5},{8,10},{9,11},{10,... | collective-permute-start | bytes 24584 | tf_op jit(solution)/shard_map/ppermute | solution.py:204
  108.8 4.8 %collective-permute-start.7 = (f32[2,1024]{1,0:T(2,128)S(1)}, f32[2,1024]{1,0:T(2,128)S(1)}, u32[]{:S(2)}, u32[]{:S(2)}) collective-permute-start(f32[2,1024]{1,0:T(2,128)S(1)} %pad_maximum_fusion.4), channel_id=1, source_target_pairs={{0,4},{1,5},{2,6},{3,7},{4,0},{5,1},{6,2},{7,3},{8,12},{9,13},{10,... | collective-permute-start | bytes 24584 | tf_op jit(solution)/shard_map/ppermute | solution.py:204
  113.6 3.7 %collective-permute-start.8 = (f32[2,1024]{1,0:T(2,128)S(1)}, f32[2,1024]{1,0:T(2,128)S(1)}, u32[]{:S(2)}, u32[]{:S(2)}) collective-permute-start(f32[2,1024]{1,0:T(2,128)S(1)} %pad_maximum_fusion.5), channel_id=1, source_target_pairs={{0,8},{8,0},{16,24},{24,16},{1,9},{9,1},{17,25},{25,17},{2,10},{10... | collective-permute-start | bytes 24584 | tf_op jit(solution)/shard_map/ppermute | solution.py:204
  117.4 3.7 %collective-permute-start.9 = (f32[2,1024]{1,0:T(2,128)S(1)}, f32[2,1024]{1,0:T(2,128)S(1)}, u32[]{:S(2)}, u32[]{:S(2)}) collective-permute-start(f32[2,1024]{1,0:T(2,128)S(1)} %pad_maximum_fusion.6), channel_id=1, source_target_pairs={{0,16},{8,24},{16,0},{24,8},{1,17},{9,25},{17,1},{25,9},{2,18},{10... | collective-permute-start | bytes 24584 | tf_op jit(solution)/shard_map/ppermute | solution.py:204

commit v2 on v1

v2 whole, which is shorter than its diff:
```python
import functools
import math

import jax
import jax.numpy as jnp
from jax import lax
from jax.experimental import pallas as pl
from jax.experimental.pallas import tpu as pltpu
from jax.sharding import PartitionSpec as P

AXES = ("grp", "dev")
B = 128
S = 256
ROWS = 512


def split(x):
    hi = x.astype(jnp.bfloat16)
    return hi, (x - hi.astype(jnp.float32)).astype(jnp.bfloat16)


def dot(left, right, dims=((1,), (0,))):
    return lax.dot_general(left, right, (dims, ((), ())), preferred_element_type=jnp.float32)


def dot_nt(left, right):
    return dot(left, right, ((1,), (1,)))


def dot3(left, right):
    return dot(left[0], right[0]) + dot(left[1], right[0]) + dot(left[0], right[1])


def dot3_narrow(left, right):
    left = jnp.concatenate([left[0], left[1], left[0]], axis=1)
    right = jnp.concatenate([right[0], right[0], right[1]], axis=0)
    return dot(left, right)


def factor_block(d_ref, c_ref, sub, lane):
    n = B // 8
    rows = [d_ref[8 * t:8 * t + 8, :] for t in range(n)]
    for k in range(n):
        first = 8 * k
        group = rows[k]
        slot = (k % 2) * 64
        for b in range(8):
            c_ref[slot + 8 * b:slot + 8 * b + 8, :] = jnp.broadcast_to(group[:, first + b:first + b + 1], (8, B))
        below = {
            t: [jnp.broadcast_to(rows[t][:, first + j:first + j + 1], (8, B)) for j in range(8)]
            for t in range(k + 1, n)
        }
        pivot = (lane >= first) & (lane < first + 8)
        start = jnp.where(pivot, (lane - first == sub).astype(jnp.float32), group)
        s = {}
        for b in range(8):
            for a in range(b + 1):
                at = slot + 8 * b + a
                s[(a, b)] = jnp.broadcast_to(c_ref[at:at + 1, :], (8, B))
        y = [jnp.broadcast_to(start[i:i + 1, :], (8, B)) for i in range(8)]
        follow = k + 1 < n
        if follow:
            z = list(below[k + 1])
            acc = jnp.where(pivot, 0.0, rows[k + 1])
        inv = []
        for j in range(8):
            r = lax.rsqrt(s[(j, j)])
            inv.append(r)
            for b in range(j + 1, 8):
                s[(j, b)] = s[(j, b)] * r
            y[j] = y[j] * r
            if follow:
                z[j] = z[j] * r
                acc = acc - z[j] * y[j]
            for b in range(j + 1, 8):
                for a in range(j + 1, b + 1):
                    s[(a, b)] = s[(a, b)] - s[(j, a)] * s[(j, b)]
            for b in range(j + 1, 8):
                y[b] = y[b] - s[(j, b)] * y[j]
                if follow:
                    z[b] = z[b] - s[(j, b)] * z[j]
        w = y[7]
        for i in range(7):
            w = jnp.where(sub == i, y[i], w)
        d_ref[first:first + 8, :] = jnp.where(lane < first + 8, w, 0.0)
        if follow:
            rows[k + 1] = acc
        if k + 2 < n:
            q = [None] * 8
            for j in range(7, -1, -1):
                v = y[j]
                for i in range(j + 1, 8):
                    v = v - s[(j, i)] * q[i]
                q[j] = v * inv[j]
            for t in range(k + 2, n):
                v = jnp.where(pivot, 0.0, rows[t])
                for j in range(8):
                    v = v - below[t][j] * q[j]
                rows[t] = v
        yield k


def square_sums(x):
    hi, lo = split(jnp.square(x.astype(jnp.float32)))
    both = jnp.concatenate([hi, lo], axis=1)
    return dot_nt(jnp.ones((8, both.shape[1]), jnp.bfloat16), both), dot_nt(both, jnp.ones((B, both.shape[1]), jnp.bfloat16))


def wide(x):
    return jnp.concatenate([x] * (S // B), axis=1)


def kernel(src_ref, dst_ref, rows_ref, points_ref, ridge_ref, raw_hbm, stat_ref,
           marks_ref, packed_ref, along_ref, a_ref, d_ref, c_ref, l_ref, lt_ref, wt_ref, x_ref, r_ref, sems):
    m, width = marks_ref.shape
    count = points_ref.shape[0]
    scale = 1.0 / (2.0 * width)
    cap = packed_ref.shape[1] - m
    stages = m // S
    half = count // 2
    sub = lax.broadcasted_iota(jnp.int32, (8, B), 0)
    lane = lax.broadcasted_iota(jnp.int32, (8, B), 1)

    def place(d, carry):
        rows = rows_ref[pl.ds(pl.multiple_of(src_ref[d] * cap, cap), cap), :].astype(jnp.float32)
        for c in range(width // B):
            packed_ref[c, pl.ds(dst_ref[d], cap), :] = rows[:, c * B:(c + 1) * B]
        return carry

    lax.fori_loop(0, src_ref.shape[0], place, 0)
    marks_ref[...] = jnp.concatenate([packed_ref[c, :m] for c in range(width // B)], axis=1).astype(jnp.bfloat16)
    marks = marks_ref[...]
    along, down = square_sums(marks)
    along_ref[...] = along
    down = wide(down)
    stat_ref[...] = jnp.zeros_like(stat_ref)
    row = lax.broadcasted_iota(jnp.int32, (S, S), 0)
    col = lax.broadcasted_iota(jnp.int32, (S, S), 1)
    for j in range(stages):
        here = slice(j * S, (j + 1) * S)
        inner = dot_nt(marks[j * S:], marks[here])
        a_ref[j, j * S:, :] = jnp.exp(-(down[j * S:] + along[0:1, here] - 2.0 * inner) * scale)
        a_ref[j, here, :] += jnp.where(row == col, ridge_ref[0:1, here], 0.0)
    d_ref[0] = a_ref[0, :B, :B]

    def copy(p, odd):
        rows = pl.ds(pl.multiple_of(odd * half, half), half)
        return pltpu.make_async_copy(x_ref.at[p, rows, :], raw_hbm.at[rows, pl.ds(p * S, S)], sems.at[p, odd])

    def cross_piece(j, at):
        here = slice(j * S, (j + 1) * S)
        rows = pl.ds(at, ROWS)
        points = points_ref[rows, :]
        _, down = square_sums(points)
        inner = dot_nt(points, marks_ref[here, :])
        x_ref[j, rows, :] = jnp.exp(-(wide(down) + along_ref[0:1, here] - 2.0 * inner) * scale)

    def raw_piece(p, at):
        here = slice(p * S, (p + 1) * S)
        rows = pl.ds(at, ROWS)
        raw = dot3(split(x_ref[p, rows, :]), (wt_ref[0], wt_ref[1]))
        x_ref[p, rows, :] = raw
        r_ref[0, rows, :], r_ref[1, rows, :] = split(raw)
        mean = jnp.mean(raw, axis=0, keepdims=True)
        spread = jnp.sum(jnp.square(raw - mean), axis=0, keepdims=True)
        before = jnp.asarray(at).astype(jnp.float32)
        share = ROWS / (before + ROWS)
        delta = mean - stat_ref[0:1, here]
        stat_ref[1:2, here] += spread + jnp.square(delta) * (before * share)
        stat_ref[0:1, here] += delta * share

    def update_piece(p, j, at):
        rows = pl.ds(at, ROWS)
        right = [lt_ref[h, p * S:(p + 1) * S, j * S:(j + 1) * S] for h in range(2)]
        x_ref[j, rows, :] -= dot3((r_ref[0, rows, :], r_ref[1, rows, :]), right)

    def core_piece(p, j, odd):
        size = (m - j * S) // 2
        rows = pl.ds(pl.multiple_of(j * S + odd * size, B), size)
        right = [lt_ref[h, p * S:(p + 1) * S, j * S:(j + 1) * S] for h in range(2)]
        keep = 2 * (p % 2)
        a_ref[j, rows, :] -= dot3((l_ref[keep, rows, :], l_ref[keep + 1, rows, :]), right)

    def finish(p, odd):
        top = p * S + (odd + 1) * B
        here = slice(odd * B, (odd + 1) * B)
        at = slice(p * S + odd * B, p * S + (odd + 1) * B)
        keep = 2 * (p % 2)
        wt = jnp.transpose(d_ref[0])
        if top < m:
            block = dot3_narrow(split(a_ref[p, top:, here]), split(wt))
            left = split(block)
            right = split(jnp.transpose(block))
            for h in range(2):
                l_ref[keep + h, top:, here] = left[h]
                lt_ref[h, at, top:] = right[h]
        if odd == 0:
            a_ref[p, top:, B:] -= dot3_narrow(left, [r[:, :B] for r in right])
            d_ref[1] = wt
            d_ref[2] = jnp.transpose(block[:B])
            d_ref[0] = a_ref[p, top:top + B, B:]
        else:
            first = d_ref[1]
            inner = dot3_narrow(split(d_ref[2]), split(wt))
            corner = -dot3_narrow(split(first), split(inner))
            upper = jnp.concatenate([first, corner], axis=1)
            lower = jnp.concatenate([jnp.zeros_like(wt), wt], axis=1)
            wt_ref[0], wt_ref[1] = split(jnp.concatenate([upper, lower], axis=0))
            if top < m:
                right = [lt_ref[h, p * S:top, top:top + S] for h in range(2)]
                a_ref[p + 1, top:, :] -= dot3((l_ref[keep, top:, :], l_ref[keep + 1, top:, :]), right)
                d_ref[0] = a_ref[p + 1, top:top + B, :B]

    for p in range(stages):
        def stage(odd, carry, p=p):
            pieces = []
            for j in range(p + 1, stages):
                if p:
                    pieces.append(functools.partial(core_piece, p - 1, j, odd))
            for block in range(half // ROWS):
                at = pl.multiple_of(odd * half + block * ROWS, ROWS)
                if p == 0:
                    pieces += [functools.partial(cross_piece, j, at) for j in range(stages)]
                else:
                    pieces.append(functools.partial(raw_piece, p - 1, at))
                    pieces += [functools.partial(update_piece, p - 1, j, at) for j in range(p, stages)]
            done = 0
            for k in factor_block(d_ref.at[0], c_ref, sub, lane):
                until = -(-len(pieces) * (k + 1) // 14)
                for piece in pieces[done:until]:
                    piece()
                done = max(done, until)
            for o in range(2):
                pl.when(odd == o)(functools.partial(finish, p, o))
            if p:
                copy(p - 1, odd).start()
            return carry

        lax.fori_loop(0, 2, stage, 0)

    def last(odd, carry):
        for block in range(half // ROWS):
            raw_piece(stages - 1, pl.multiple_of(odd * half + block * ROWS, ROWS))
        copy(stages - 1, odd).start()
        return carry

    lax.fori_loop(0, 2, last, 0)
    for p in range(stages):
        for odd in range(2):
            copy(p, odd).wait()


def exchange(x, bit):
    dev = lax.axis_size("dev")
    axis, flip = ("dev", bit) if bit < dev else ("grp", bit // dev)
    size = lax.axis_size(axis)
    return lax.ppermute(x, axis, [(k, k ^ flip) for k in range(size)])


def shards(points, ridge, landmark_ids):
    count, width = points.shape
    m = landmark_ids.shape[0]
    devices = lax.axis_size(AXES)
    me = lax.axis_index(AXES)
    mean = m / devices
    cap = min(m, 16 * math.ceil((mean + 5.6 * math.sqrt(mean)) / 16))
    bits = [1 << b for b in range(devices.bit_length() - 1)]
    order = bits[1:] + bits[:1]

    bounds = jnp.sum(landmark_ids[None, :] < (jnp.arange(devices + 1) * count)[:, None], axis=1, dtype=jnp.int32)
    low = bounds[:-1]
    fits = jnp.max(bounds[1:] - low) <= cap

    def packed(points, ids):
        mine = lax.dynamic_slice(jnp.pad(ids, (0, cap)), (low[me],), (cap,))
        rows = points[jnp.clip(mine - me * count, 0, count - 1)]
        for bit in order:
            rows = jnp.concatenate([rows, exchange(rows, bit)], axis=0)
        far = jnp.arange(devices, dtype=jnp.int32) ^ me
        place = jnp.zeros_like(far)
        for k, bit in enumerate(order):
            place = place + jnp.where((far & bit) != 0, 1 << k, 0)
        return rows, place, low

    def summed(points, ids):
        offset = ids - me * count
        inside = (offset >= 0) & (offset < count)
        picked = points[jnp.clip(offset, 0, count - 1)]
        rows = lax.psum(jnp.where(inside[:, None], picked.astype(jnp.float32), 0.0), AXES).astype(points.dtype)
        rows = jnp.pad(rows, ((0, max(0, devices * cap - m)), (0, 0)))
        place = jnp.arange(devices, dtype=jnp.int32) % (m // cap)
        return rows, place, place * cap

    rows, src, dst = lax.cond(fits, packed, summed, points, landmark_ids)

    vmem = pl.BlockSpec(memory_space=pltpu.VMEM)
    raw, stat = pl.pallas_call(
        kernel,
        grid_spec=pltpu.PrefetchScalarGridSpec(
            num_scalar_prefetch=2,
            grid=(),
            in_specs=[vmem, vmem, vmem],
            out_specs=[pl.BlockSpec(memory_space=pl.ANY), vmem],
            scratch_shapes=[
                pltpu.VMEM((m, width), jnp.bfloat16),
                pltpu.VMEM((width // B, m + cap, B), jnp.float32),
                pltpu.VMEM((8, m), jnp.float32),
                pltpu.VMEM((m // S, m, S), jnp.float32),
                pltpu.VMEM((3, B, B), jnp.float32),
                pltpu.VMEM((B, B), jnp.float32),
                pltpu.VMEM((4, m, S), jnp.bfloat16),
                pltpu.VMEM((2, m, m), jnp.bfloat16),
                pltpu.VMEM((2, S, S), jnp.bfloat16),
                pltpu.VMEM((m // S, count, S), jnp.float32),
                pltpu.VMEM((2, count, S), jnp.bfloat16),
                pltpu.SemaphoreType.DMA((m // S, 2)),
            ],
        ),
        out_shape=(jax.ShapeDtypeStruct((count, m), jnp.float32), jax.ShapeDtypeStruct((8, m), jnp.float32)),
        compiler_params=pltpu.CompilerParams(vmem_limit_bytes=60 << 20),
        name="nystrom",
    )(src, dst, rows, points, ridge[None, :])

    stat = stat[:2]
    total = count
    for bit in bits:
        other = exchange(stat, bit)
        delta = other[0] - stat[0]
        stat = jnp.stack([0.5 * (stat[0] + other[0]), stat[1] + other[1] + jnp.square(delta) * (0.5 * total)])
        total *= 2
    var = stat[1] / total
    return ((raw - stat[0][None, :]) / jnp.sqrt(var + 1e-05)[None, :]).astype(jnp.bfloat16)


def solution(mesh):
    placed = (P(AXES, None), P(), P())
    return jax.shard_map(shards, mesh=mesh, in_specs=placed, out_specs=P(AXES, None), check_vma=False)
```

time: 128 us -> 101 us (0.79)
  Pallas kernels: 69.4 us -> 42.2 us
    pallas_call x1, Pallas kernels: 69.4 us -> 42.2 us  [shards(): pl.pallas_call(kernel, grid_spec=pltpu.PrefetchScalarGridSpec(num_scalar_...]
  transfers between devices with their start and end apart: 10 -> 10, of which waited for: 10 -> 10; matrix products, arithmetic and copies ran while one was open for 2% -> 3% of each run, Pallas kernels for 0% -> 0%
where the time goes in v2:
time: 101 us
  Pallas kernels  42.2 us (42%)
  waiting for transfers between devices  19.6 us (19%)
  starting transfers between devices  18.6 us (18%)
  other arithmetic  10.1 us (10%)
  local copies, waits for them, and re-layouts  7.48 us (7%)
  loops' own time  1.98 us (2%)
    pallas_call x1, Pallas kernels, shards(): pl.pallas_call(kernel, grid_spec=pltpu.PrefetchScalarGridSpec(num_scalar_...  42.2 us
    ppermute x10, waiting for transfers between devices, exchange(): return lax.ppermute(x, axis, [(k, k ^ flip) for k in range(size)])  19.6 us
    ppermute x10, starting transfers between devices, exchange(): return lax.ppermute(x, axis, [(k, k ^ flip) for k in range(size)])  18.6 us
    convert_element_type x1, other arithmetic, shards(): ((raw - stat[0][None, :]) / jnp.sqrt(var + 1e-05)[None, :]).astype(jnp.bf...  6.69 us
    cond x4, local copies, waits for them, and re-layouts  2.55 us
  transfers between devices with their start and end apart: 10, of which 10 were waited for; matrix products, arithmetic and copies ran while one was open for 3% of the time, Pallas kernels for 0%

profile of v2, /device:TPU:0, one launch (start us, length us, event | category | flops | bytes accessed | tf_op | source)
XLA Modules:
  0.0 100.6 jit_solution(1696676770503305713)
XLA Ops:
  0.0 0.9 convert_reduce_fusion
  0.9 0.7 fusion.10
  2.3 30.6 %conditional.1 = (bf16[2048,256]{1,0:T(8,128)(2,1)}, s32[32]{0:T(128)S(1)}, s32[32]{0:T(128)S(1)}) conditional(s32[]{:T(128)} %convert_element_type.18, (s32[]{:T(128)}, s32[1024]{0:T(1024)}, bf16[2048,256]{1,0:T(8,128)(2,1)}) %tuple.13, (s32[1024]{0:T(1024)}, s32[]{:T(128)}, s32[32]{0:T(128)S(1)}, bf16[2048,256]{1,0:T(8,128)(2,1)}) %tuple.14), branch_computations={%region_2.4_spmd, %region_4.5_spmd} | conditional | flops 1574855 | bytes 7677128 | solution.py:294
  2.3 0.6 dynamic_slice.4
  4.8 0.8 compare_select_fusion.1
  5.6 2.0 %gather_fusion = bf16[64,256]{1,0:T(8,128)(2,1)S(1)} fusion(bf16[2048,256]{1,0:T(8,128)(2,1)} %get-tuple-element.22, s32[1024]{0:T(1024)S(1)} %pad_clamp_fusion), kind=kCustom, calls=%fused_computation.1 | custom fusion | bytes 65792 | tf_op jit(solution)/shard_map/cond/branch_1_fun/gather | solution.py:276
  7.6 3.1 %collective-permute-start = (bf16[64,256]{1,0:T(8,128)(2,1)S(1)}, bf16[64,256]{1,0:T(8,128)(2,1)S(1)}, u32[]{:S(2)}, u32[]{:S(2)}) collective-permute-start(bf16[64,256]{1,0:T(8,128)(2,1)S(1)} %gather_fusion), channel_id=1, source_target_pairs={{0,2},{1,3},{2,0},{3,1},{4,6},{5,7},{6,4},{7,5},{8,10},{9,11},{10,... | collective-permute-start | bytes 98312 | tf_op jit(solution)/shard_map/cond/branch_1_fun/ppermute | solution.py:257
  10.7 1.9 %collective-permute-done = bf16[64,256]{1,0:T(8,128)(2,1)S(1)} collective-permute-done((bf16[64,256]{1,0:T(8,128)(2,1)S(1)}, bf16[64,256]{1,0:T(8,128)(2,1)S(1)}, u32[]{:S(2)}, u32[]{:S(2)}) %collective-permute-start) | collective-permute-done | bytes 32800 | tf_op jit(solution)/shard_map/cond/branch_1_fun/ppermute | solution.py:257
  12.6 3.0 %collective-permute-start.1 = (bf16[128,256]{1,0:T(8,128)(2,1)S(1)}, bf16[128,256]{1,0:T(8,128)(2,1)S(1)}, u32[]{:S(2)}, u32[]{:S(2)}) collective-permute-start(bf16[128,256]{1,0:T(8,128)(2,1)S(1)} %pad_maximum_fusion.2), channel_id=1, source_target_pairs={{0,4},{1,5},{2,6},{3,7},{4,0},{5,1},{6,2},{7,3},{8,12},{9,13},{10,... | collective-permute-start | bytes 196616 | tf_op jit(solution)/shard_map/cond/branch_1_fun/ppermute | solution.py:257
  15.7 2.2 %collective-permute-done.1 = bf16[128,256]{1,0:T(8,128)(2,1)S(1)} collective-permute-done((bf16[128,256]{1,0:T(8,128)(2,1)S(1)}, bf16[128,256]{1,0:T(8,128)(2,1)S(1)}, u32[]{:S(2)}, u32[]{:S(2)}) %collective-permute-start.1) | collective-permute-done | bytes 65568 | tf_op jit(solution)/shard_map/cond/branch_1_fun/ppermute | solution.py:257
  17.9 1.9 %collective-permute-start.2 = (bf16[256,256]{1,0:T(8,128)(2,1)S(1)}, bf16[256,256]{1,0:T(8,128)(2,1)S(1)}, u32[]{:S(2)}, u32[]{:S(2)}) collective-permute-start(bf16[256,256]{1,0:T(8,128)(2,1)S(1)} %pad_maximum_fusion.1), channel_id=1, source_target_pairs={{0,8},{8,0},{16,24},{24,16},{1,9},{9,1},{17,25},{25,17},{2,10},{10... | collective-permute-start | bytes 393224 | tf_op jit(solution)/shard_map/cond/branch_1_fun/ppermute | solution.py:257
  19.8 0.6 constant_dynamic-update-slice_fusion.4
  20.4 2.5 %collective-permute-done.2 = bf16[256,256]{1,0:T(8,128)(2,1)S(1)} collective-permute-done((bf16[256,256]{1,0:T(8,128)(2,1)S(1)}, bf16[256,256]{1,0:T(8,128)(2,1)S(1)}, u32[]{:S(2)}, u32[]{:S(2)}) %collective-permute-start.2) | collective-permute-done | bytes 131104 | tf_op jit(solution)/shard_map/cond/branch_1_fun/ppermute | solution.py:257
  23.0 1.9 %collective-permute-start.3 = (bf16[512,256]{1,0:T(8,128)(2,1)S(1)}, bf16[512,256]{1,0:T(8,128)(2,1)S(1)}, u32[]{:S(2)}, u32[]{:S(2)}) collective-permute-start(bf16[512,256]{1,0:T(8,128)(2,1)S(1)} %pad_maximum_fusion), channel_id=1, source_target_pairs={{0,16},{8,24},{16,0},{24,8},{1,17},{9,25},{17,1},{25,9},{2,18},{10... | collective-permute-start | bytes 786440 | tf_op jit(solution)/shard_map/cond/branch_1_fun/ppermute | solution.py:257
  24.9 0.6 constant_dynamic-update-slice_fusion.3
  25.5 0.6 constant_dynamic-update-slice_fusion.2
  26.1 0.7 constant_dynamic-update-slice_fusion.1
  26.8 2.6 %collective-permute-done.3 = bf16[512,256]{1,0:T(8,128)(2,1)S(1)} collective-permute-done((bf16[512,256]{1,0:T(8,128)(2,1)S(1)}, bf16[512,256]{1,0:T(8,128)(2,1)S(1)}, u32[]{:S(2)}, u32[]{:S(2)}) %collective-permute-start.3) | collective-permute-done | bytes 262176 | tf_op jit(solution)/shard_map/cond/branch_1_fun/ppermute | solution.py:257
  29.4 0.7 constant_dynamic-update-slice_fusion
  30.1 0.0 collective-permute-start.4
  30.2 1.9 %collective-permute-done.4 = bf16[1024,256]{1,0:T(8,128)(2,1)S(1)} collective-permute-done((bf16[1024,256]{1,0:T(8,128)(2,1)S(1)}, bf16[1024,256]{1,0:T(8,128)(2,1)S(1)}, u32[]{:S(2)}, u32[]{:S(2)}) %collective-permute-start.4) | collective-permute-done | bytes 524320 | tf_op jit(solution)/shard_map/cond/branch_1_fun/ppermute | solution.py:257
  32.1 0.8 constant_dynamic-update-slice_fusion.5
  32.9 42.2 %nystrom.1 = (f32[2048,1024]{1,0:T(8,128)}, f32[8,1024]{1,0:T(8,128)}) custom-call(s32[32]{0:T(128)S(1)} %get-tuple-element.31.src_ref, s32[32]{0:T(128)S(1)} %get-tuple-element.32.dst_ref, bf16[2048,256]{1,0:T(8,128)(2,1)} %get-tuple-element.33.rows_ref, bf16[2048,256]{1,0:T(8,128)(2,1)} %points_ref.1, f32[1,1024]{1,0:T(1,128)} %bitcast.6), custom_call_target="tpu_custom_call" | custom-call | tf_op jit(solution)/shard_map/nystrom/pallas_call | solution.py:297
  75.1 0.8 slice.56
  75.8 0.1 collective-permute-start.5
  75.9 1.1 %collective-permute-done.5 = f32[2,1024]{1,0:T(2,128)S(1)} collective-permute-done((f32[2,1024]{1,0:T(2,128)S(1)}, f32[2,1024]{1,0:T(2,128)S(1)}, u32[]{:S(2)}, u32[]{:S(2)}) %collective-permute-start.5) | collective-permute-done | bytes 8224 | tf_op jit(solution)/shard_map/ppermute | solution.py:257
  77.0 0.9 fusion.9
  77.9 2.0 %collective-permute-start.6 = (f32[2,1024]{1,0:T(2,128)S(1)}, f32[2,1024]{1,0:T(2,128)S(1)}, u32[]{:S(2)}, u32[]{:S(2)}) collective-permute-start(f32[2,1024]{1,0:T(2,128)S(1)} %pad_maximum_fusion.3), channel_id=1, source_target_pairs={{0,2},{1,3},{2,0},{3,1},{4,6},{5,7},{6,4},{7,5},{8,10},{9,11},{10,... | collective-permute-start | bytes 24584 | tf_op jit(solution)/shard_map/ppermute | solution.py:257
  79.8 1.8 %collective-permute-done.6 = f32[2,1024]{1,0:T(2,128)S(1)} collective-permute-done((f32[2,1024]{1,0:T(2,128)S(1)}, f32[2,1024]{1,0:T(2,128)S(1)}, u32[]{:S(2)}, u32[]{:S(2)}) %collective-permute-start.6) | collective-permute-done | bytes 8224 | tf_op jit(solution)/shard_map/ppermute | solution.py:257
  81.6 3.1 %collective-permute-start.7 = (f32[2,1024]{1,0:T(2,128)S(1)}, f32[2,1024]{1,0:T(2,128)S(1)}, u32[]{:S(2)}, u32[]{:S(2)}) collective-permute-start(f32[2,1024]{1,0:T(2,128)S(1)} %pad_maximum_fusion.4), channel_id=1, source_target_pairs={{0,4},{1,5},{2,6},{3,7},{4,0},{5,1},{6,2},{7,3},{8,12},{9,13},{10,... | collective-permute-start | bytes 24584 | tf_op jit(solution)/shard_map/ppermute | solution.py:257
  84.8 1.6 %collective-permute-done.7 = f32[2,1024]{1,0:T(2,128)S(1)} collective-permute-done((f32[2,1024]{1,0:T(2,128)S(1)}, f32[2,1024]{1,0:T(2,128)S(1)}, u32[]{:S(2)}, u32[]{:S(2)}) %collective-permute-start.7) | collective-permute-done | bytes 8224 | tf_op jit(solution)/shard_map/ppermute | solution.py:257
  86.4 1.7 %collective-permute-start.8 = (f32[2,1024]{1,0:T(2,128)S(1)}, f32[2,1024]{1,0:T(2,128)S(1)}, u32[]{:S(2)}, u32[]{:S(2)}) collective-permute-start(f32[2,1024]{1,0:T(2,128)S(1)} %pad_maximum_fusion.5), channel_id=1, source_target_pairs={{0,8},{8,0},{16,24},{24,16},{1,9},{9,1},{17,25},{25,17},{2,10},{10... | collective-permute-start | bytes 24584 | tf_op jit(solution)/shard_map/ppermute | solution.py:257
  88.1 2.0 %collective-permute-done.8 = f32[2,1024]{1,0:T(2,128)S(1)} collective-permute-done((f32[2,1024]{1,0:T(2,128)S(1)}, f32[2,1024]{1,0:T(2,128)S(1)}, u32[]{:S(2)}, u32[]{:S(2)}) %collective-permute-start.8) | collective-permute-done | bytes 8224 | tf_op jit(solution)/shard_map/ppermute | solution.py:257
  90.2 1.7 %collective-permute-start.9 = (f32[2,1024]{1,0:T(2,128)S(1)}, f32[2,1024]{1,0:T(2,128)S(1)}, u32[]{:S(2)}, u32[]{:S(2)}) collective-permute-start(f32[2,1024]{1,0:T(2,128)S(1)} %pad_maximum_fusion.6), channel_id=1, source_target_pairs={{0,16},{8,24},{16,0},{24,8},{1,17},{9,25},{17,1},{25,9},{2,18},{10... | collective-permute-start | bytes 24584 | tf_op jit(solution)/shard_map/ppermute | solution.py:257
  91.9 2.0 %collective-permute-done.9 = f32[2,1024]{1,0:T(2,128)S(1)} collective-permute-done((f32[2,1024]{1,0:T(2,128)S(1)}, f32[2,1024]{1,0:T(2,128)S(1)}, u32[]{:S(2)}, u32[]{:S(2)}) %collective-permute-start.9) | collective-permute-done | bytes 8224 | tf_op jit(solution)/shard_map/ppermute | solution.py:257
  93.9 6.7 %divide_convert_fusion = bf16[2048,1024]{1,0:T(8,128)(2,1)} fusion(f32[2048,1024]{1,0:T(8,128)} %get-tuple-element.34, f32[1024]{0:T(1024)S(1)} %bitcast.5, f32[1024]{0:T(1024)S(1)} %bitcast.4), kind=kLoop, calls=%fused_computation.34 | loop fusion | flops 6291456 | bytes 12591104 | tf_op jit(solution)/shard_map/convert_element_type | solution.py:332
  (14 shorter events, 0.2 us)
Async XLA Ops:
  7.6 5.0 %collective-permute-start = (bf16[64,256]{1,0:T(8,128)(2,1)S(1)}, bf16[64,256]{1,0:T(8,128)(2,1)S(1)}, u32[]{:S(2)}, u32[]{:S(2)}) collective-permute-start(bf16[64,256]{1,0:T(8,128)(2,1)S(1)} %gather_fusion), channel_id=1, source_target_pairs={{0,2},{1,3},{2,0},{3,1},{4,6},{5,7},{6,4},{7,5},{8,10},{9,11},{10,... | collective-permute-start | bytes 98312 | tf_op jit(solution)/shard_map/cond/branch_1_fun/ppermute | solution.py:257
  12.6 5.3 %collective-permute-start.1 = (bf16[128,256]{1,0:T(8,128)(2,1)S(1)}, bf16[128,256]{1,0:T(8,128)(2,1)S(1)}, u32[]{:S(2)}, u32[]{:S(2)}) collective-permute-start(bf16[128,256]{1,0:T(8,128)(2,1)S(1)} %pad_maximum_fusion.2), channel_id=1, source_target_pairs={{0,4},{1,5},{2,6},{3,7},{4,0},{5,1},{6,2},{7,3},{8,12},{9,13},{10,... | collective-permute-start | bytes 196616 | tf_op jit(solution)/shard_map/cond/branch_1_fun/ppermute | solution.py:257
  17.9 5.0 %collective-permute-start.2 = (bf16[256,256]{1,0:T(8,128)(2,1)S(1)}, bf16[256,256]{1,0:T(8,128)(2,1)S(1)}, u32[]{:S(2)}, u32[]{:S(2)}) collective-permute-start(bf16[256,256]{1,0:T(8,128)(2,1)S(1)} %pad_maximum_fusion.1), channel_id=1, source_target_pairs={{0,8},{8,0},{16,24},{24,16},{1,9},{9,1},{17,25},{25,17},{2,10},{10... | collective-permute-start | bytes 393224 | tf_op jit(solution)/shard_map/cond/branch_1_fun/ppermute | solution.py:257
  23.0 6.4 %collective-permute-start.3 = (bf16[512,256]{1,0:T(8,128)(2,1)S(1)}, bf16[512,256]{1,0:T(8,128)(2,1)S(1)}, u32[]{:S(2)}, u32[]{:S(2)}) collective-permute-start(bf16[512,256]{1,0:T(8,128)(2,1)S(1)} %pad_maximum_fusion), channel_id=1, source_target_pairs={{0,16},{8,24},{16,0},{24,8},{1,17},{9,25},{17,1},{25,9},{2,18},{10... | collective-permute-start | bytes 786440 | tf_op jit(solution)/shard_map/cond/branch_1_fun/ppermute | solution.py:257
  30.1 1.9 %collective-permute-start.4 = (bf16[1024,256]{1,0:T(8,128)(2,1)S(1)}, bf16[1024,256]{1,0:T(8,128)(2,1)S(1)}, u32[]{:S(2)}, u32[]{:S(2)}) collective-permute-start(bf16[1024,256]{1,0:T(8,128)(2,1)S(1)} %get-tuple-element.38), channel_id=1, source_target_pairs={{0,1},{1,0},{2,3},{3,2},{4,5},{5,4},{6,7},{7,6},{8,9},{9,8},{10,11... | collective-permute-start | bytes 1572872 | tf_op jit(solution)/shard_map/cond/branch_1_fun/ppermute | solution.py:257
  75.8 1.2 %collective-permute-start.5 = (f32[2,1024]{1,0:T(2,128)S(1)}, f32[2,1024]{1,0:T(2,128)S(1)}, u32[]{:S(2)}, u32[]{:S(2)}) collective-permute-start(f32[2,1024]{1,0:T(2,128)S(1)} %slice.56), channel_id=1, source_target_pairs={{0,1},{1,0},{2,3},{3,2},{4,5},{5,4},{6,7},{7,6},{8,9},{9,8},{10,11... | collective-permute-start | bytes 24584 | tf_op jit(solution)/shard_map/ppermute | solution.py:257
  77.9 3.7 %collective-permute-start.6 = (f32[2,1024]{1,0:T(2,128)S(1)}, f32[2,1024]{1,0:T(2,128)S(1)}, u32[]{:S(2)}, u32[]{:S(2)}) collective-permute-start(f32[2,1024]{1,0:T(2,128)S(1)} %pad_maximum_fusion.3), channel_id=1, source_target_pairs={{0,2},{1,3},{2,0},{3,1},{4,6},{5,7},{6,4},{7,5},{8,10},{9,11},{10,... | collective-permute-start | bytes 24584 | tf_op jit(solution)/shard_map/ppermute | solution.py:257
  81.6 4.8 %collective-permute-start.7 = (f32[2,1024]{1,0:T(2,128)S(1)}, f32[2,1024]{1,0:T(2,128)S(1)}, u32[]{:S(2)}, u32[]{:S(2)}) collective-permute-start(f32[2,1024]{1,0:T(2,128)S(1)} %pad_maximum_fusion.4), channel_id=1, source_target_pairs={{0,4},{1,5},{2,6},{3,7},{4,0},{5,1},{6,2},{7,3},{8,12},{9,13},{10,... | collective-permute-start | bytes 24584 | tf_op jit(solution)/shard_map/ppermute | solution.py:257
  86.4 3.7 %collective-permute-start.8 = (f32[2,1024]{1,0:T(2,128)S(1)}, f32[2,1024]{1,0:T(2,128)S(1)}, u32[]{:S(2)}, u32[]{:S(2)}) collective-permute-start(f32[2,1024]{1,0:T(2,128)S(1)} %pad_maximum_fusion.5), channel_id=1, source_target_pairs={{0,8},{8,0},{16,24},{24,16},{1,9},{9,1},{17,25},{25,17},{2,10},{10... | collective-permute-start | bytes 24584 | tf_op jit(solution)/shard_map/ppermute | solution.py:257
  90.2 3.7 %collective-permute-start.9 = (f32[2,1024]{1,0:T(2,128)S(1)}, f32[2,1024]{1,0:T(2,128)S(1)}, u32[]{:S(2)}, u32[]{:S(2)}) collective-permute-start(f32[2,1024]{1,0:T(2,128)S(1)} %pad_maximum_fusion.6), channel_id=1, source_target_pairs={{0,16},{8,24},{16,0},{24,8},{1,17},{9,25},{17,1},{25,9},{2,18},{10... | collective-permute-start | bytes 24584 | tf_op jit(solution)/shard_map/ppermute | solution.py:257

commit v3 on v2

--- a/solution.py
+++ b/solution.py
@@ -40,28 +40,31 @@
 def factor_block(d_ref, c_ref, sub, lane):
     n = B // 8
     rows = [d_ref[8 * t:8 * t + 8, :] for t in range(n)]
+
+    def column(t, at):
+        return jnp.broadcast_to(rows[t][:, at:at + 1], (8, B))
+
+    def spread(at):
+        return jnp.broadcast_to(c_ref[at:at + 1, :], (8, B))
+
+    ahead = [column(0, b) for b in range(8)]
     for k in range(n):
         first = 8 * k
-        group = rows[k]
-        slot = (k % 2) * 64
+        base = (k % 2) * 128
+        follow = k + 1 < n
         for b in range(8):
-            c_ref[slot + 8 * b:slot + 8 * b + 8, :] = jnp.broadcast_to(group[:, first + b:first + b + 1], (8, B))
-        below = {
-            t: [jnp.broadcast_to(rows[t][:, first + j:first + j + 1], (8, B)) for j in range(8)]
-            for t in range(k + 1, n)
-        }
+            c_ref[base + 8 * b:base + 8 * b + 8, :] = ahead[b]
+        s = {(a, b): spread(base + 8 * b + a) for b in range(8) for a in range(b + 1)}
+        if follow:
+            z = [column(k + 1, first + j) for j in range(8)]
+            ahead = [column(k + 1, first + 8 + b) for b in range(8)]
+            acc = rows[k + 1]
+        below = {t: [column(t, first + j) for j in range(8)] for t in range(k + 2, n)}
         pivot = (lane >= first) & (lane < first + 8)
-        start = jnp.where(pivot, (lane - first == sub).astype(jnp.float32), group)
-        s = {}
-        for b in range(8):
-            for a in range(b + 1):
-                at = slot + 8 * b + a
-                s[(a, b)] = jnp.broadcast_to(c_ref[at:at + 1, :], (8, B))
+        start = jnp.where(pivot, (lane - first == sub).astype(jnp.float32), rows[k])
         y = [jnp.broadcast_to(start[i:i + 1, :], (8, B)) for i in range(8)]
-        follow = k + 1 < n
         if follow:
-            z = list(below[k + 1])
-            acc = jnp.where(pivot, 0.0, rows[k + 1])
+            acc = jnp.where(pivot, 0.0, acc)
         inv = []
         for j in range(8):
             r = lax.rsqrt(s[(j, j)])
@@ -72,6 +75,10 @@
             if follow:
                 z[j] = z[j] * r
                 acc = acc - z[j] * y[j]
+                at = base + 64 + 8 * j
+                c_ref[at:at + 8, :] = z[j]
+                for b in range(8):
+                    ahead[b] = ahead[b] - z[j] * spread(at + b)
             for b in range(j + 1, 8):
                 for a in range(j + 1, b + 1):
                     s[(a, b)] = s[(a, b)] - s[(j, a)] * s[(j, b)]
@@ -110,8 +117,8 @@
     return jnp.concatenate([x] * (S // B), axis=1)
 
 
-def kernel(src_ref, dst_ref, rows_ref, points_ref, ridge_ref, raw_hbm, stat_ref,
-           marks_ref, packed_ref, along_ref, a_ref, d_ref, c_ref, l_ref, lt_ref, wt_ref, x_ref, r_ref, sems):
+def kernel(src_ref, dst_ref, rows_ref, points_ref, ridge_ref, x_ref, stat_ref,
+           marks_ref, packed_ref, along_ref, a_ref, d_ref, c_ref, l_ref, lt_ref, wt_ref, r_ref):
     m, width = marks_ref.shape
     count = points_ref.shape[0]
     scale = 1.0 / (2.0 * width)
@@ -142,10 +149,6 @@
         a_ref[j, j * S:, :] = jnp.exp(-(down[j * S:] + along[0:1, here] - 2.0 * inner) * scale)
         a_ref[j, here, :] += jnp.where(row == col, ridge_ref[0:1, here], 0.0)
     d_ref[0] = a_ref[0, :B, :B]
-
-    def copy(p, odd):
-        rows = pl.ds(pl.multiple_of(odd * half, half), half)
-        return pltpu.make_async_copy(x_ref.at[p, rows, :], raw_hbm.at[rows, pl.ds(p * S, S)], sems.at[p, odd])
 
     def cross_piece(j, at):
         here = slice(j * S, (j + 1) * S)
@@ -232,8 +235,6 @@
                 done = max(done, until)
             for o in range(2):
                 pl.when(odd == o)(functools.partial(finish, p, o))
-            if p:
-                copy(p - 1, odd).start()
             return carry
 
         lax.fori_loop(0, 2, stage, 0)
@@ -241,13 +242,17 @@
     def last(odd, carry):
         for block in range(half // ROWS):
             raw_piece(stages - 1, pl.multiple_of(odd * half + block * ROWS, ROWS))
-        copy(stages - 1, odd).start()
         return carry
 
     lax.fori_loop(0, 2, last, 0)
-    for p in range(stages):
-        for odd in range(2):
-            copy(p, odd).wait()
+
+
+def standardize(x_ref, shift_ref, gain_ref, out_ref):
+    size = out_ref.shape[0]
+    rows = pl.ds(pl.multiple_of(pl.program_id(0) * size, size), size)
+    for p in range(x_ref.shape[0]):
+        here = slice(p * S, (p + 1) * S)
+        out_ref[:, here] = ((x_ref[p, rows, :] - shift_ref[:, here]) * gain_ref[:, here]).astype(out_ref.dtype)
 
 
 def exchange(x, bit):
@@ -300,36 +305,42 @@
             num_scalar_prefetch=2,
             grid=(),
             in_specs=[vmem, vmem, vmem],
-            out_specs=[pl.BlockSpec(memory_space=pl.ANY), vmem],
+            out_specs=[vmem, vmem],
             scratch_shapes=[
                 pltpu.VMEM((m, width), jnp.bfloat16),
                 pltpu.VMEM((width // B, m + cap, B), jnp.float32),
                 pltpu.VMEM((8, m), jnp.float32),
                 pltpu.VMEM((m // S, m, S), jnp.float32),
                 pltpu.VMEM((3, B, B), jnp.float32),
-                pltpu.VMEM((B, B), jnp.float32),
+                pltpu.VMEM((2 * B, B), jnp.float32),
                 pltpu.VMEM((4, m, S), jnp.bfloat16),
                 pltpu.VMEM((2, m, m), jnp.bfloat16),
                 pltpu.VMEM((2, S, S), jnp.bfloat16),
-                pltpu.VMEM((m // S, count, S), jnp.float32),
                 pltpu.VMEM((2, count, S), jnp.bfloat16),
-                pltpu.SemaphoreType.DMA((m // S, 2)),
             ],
         ),
-        out_shape=(jax.ShapeDtypeStruct((count, m), jnp.float32), jax.ShapeDtypeStruct((8, m), jnp.float32)),
-        compiler_params=pltpu.CompilerParams(vmem_limit_bytes=60 << 20),
+        out_shape=(pltpu.VMEM((m // S, count, S), jnp.float32), jax.ShapeDtypeStruct((2, m), jnp.float32)),
+        compiler_params=pltpu.CompilerParams(vmem_limit_bytes=40 << 20),
         name="nystrom",
     )(src, dst, rows, points, ridge[None, :])
 
-    stat = stat[:2]
     total = count
     for bit in bits:
         other = exchange(stat, bit)
         delta = other[0] - stat[0]
         stat = jnp.stack([0.5 * (stat[0] + other[0]), stat[1] + other[1] + jnp.square(delta) * (0.5 * total)])
         total *= 2
-    var = stat[1] / total
-    return ((raw - stat[0][None, :]) / jnp.sqrt(var + 1e-05)[None, :]).astype(jnp.bfloat16)
+    gain = 1.0 / jnp.sqrt(stat[1:2] / total + 1e-05)
+    vector = pl.BlockSpec((1, m), lambda i: (0, 0))
+    return pl.pallas_call(
+        standardize,
+        grid=(count // 256,),
+        in_specs=[vmem, vector, vector],
+        out_specs=pl.BlockSpec((256, m), lambda i: (i, 0)),
+        out_shape=jax.ShapeDtypeStruct((count, m), jnp.bfloat16),
+        compiler_params=pltpu.CompilerParams(vmem_limit_bytes=16 << 20, dimension_semantics=("arbitrary",)),
+        name="standardize",
+    )(raw, stat[0:1], gain)
 
 
 def solution(mesh):

time: 101 us -> 93.1 us (0.922)
  other arithmetic: 10.1 us -> 2.56 us
    convert_element_type x1 -> x0, other arithmetic: 6.69 us -> none  [shards(): ((raw - stat[0][None, :]) / jnp.sqrt(var + 1e-05)[None, :]).astype(jnp.bf...]
    pallas_call x0 -> x1, Pallas kernels: none -> 3.72 us  [shards(): pl.pallas_call(standardize, grid=(count // 256,), in_specs=[vmem, vector,...]
    pallas_call x1, Pallas kernels: 42.2 us -> 38.9 us  [shards(): pl.pallas_call(kernel, grid_spec=pltpu.PrefetchScalarGridSpec(num_scalar_...]
where the time goes in v3:
time: 93.1 us; the launch traced here: 92.8 us
  Pallas kernels  42.6 us (46%)
  waiting for transfers between devices  19.4 us (21%)
  starting transfers between devices  18.8 us (20%)
  local copies, waits for them, and re-layouts  6.72 us (7%)
  other arithmetic  2.56 us (3%)
  loops' own time  1.98 us (2%)
    pallas_call x1, Pallas kernels, shards(): pl.pallas_call(kernel, grid_spec=pltpu.PrefetchScalarGridSpec(num_scalar_...  38.9 us
    ppermute x10, waiting for transfers between devices, exchange(): return lax.ppermute(x, axis, [(k, k ^ flip) for k in range(size)])  19.4 us
    ppermute x10, starting transfers between devices, exchange(): return lax.ppermute(x, axis, [(k, k ^ flip) for k in range(size)])  18.8 us
    pallas_call x1, Pallas kernels, shards(): pl.pallas_call(standardize, grid=(count // 256,), in_specs=[vmem, vector,...  3.72 us
    cond x4, local copies, waits for them, and re-layouts  2.55 us
    gather x1, local copies, waits for them, and re-layouts, packed(): rows = points[jnp.clip(mine - me * count, 0, count - 1)]  2.02 us
    another operation x1, loops' own time, shards(): rows, src, dst = lax.cond(fits, packed, summed, points, landmark_ids)  1.98 us
  transfers between devices with their start and end apart: 10, of which 10 were waited for; matrix products, arithmetic and copies ran while one was open for 3% of the time, Pallas kernels for 0%

profile of v3, /device:TPU:0, one launch (start us, length us, event | category | flops | bytes accessed | tf_op | source)
XLA Modules:
  0.0 92.8 jit_solution(14157354079791066217)
XLA Ops:
  0.0 0.0 copy-start
  0.0 0.9 convert_reduce_fusion
  0.9 0.7 fusion.10
  2.3 30.6 %conditional.1 = (bf16[2048,256]{1,0:T(8,128)(2,1)}, s32[32]{0:T(128)S(1)}, s32[32]{0:T(128)S(1)}) conditional(s32[]{:T(128)} %convert_element_type.15, (s32[]{:T(128)}, s32[1024]{0:T(1024)}, bf16[2048,256]{1,0:T(8,128)(2,1)}) %tuple.13, (s32[1024]{0:T(1024)}, s32[]{:T(128)}, s32[32]{0:T(128)S(1)}, bf16[2048,256]{1,0:T(8,128)(2,1)}) %tuple.14), branch_computations={%region_2.4_spmd, %region_4.5_spmd} | conditional | flops 1574855 | bytes 7677128 | solution.py:299
  2.3 0.6 dynamic_slice.4
  4.8 0.8 compare_select_fusion.1
  5.6 2.0 %gather_fusion = bf16[64,256]{1,0:T(8,128)(2,1)S(1)} fusion(bf16[2048,256]{1,0:T(8,128)(2,1)} %get-tuple-element.22, s32[1024]{0:T(1024)S(1)} %pad_clamp_fusion), kind=kCustom, calls=%fused_computation.1 | custom fusion | bytes 65792 | tf_op jit(solution)/shard_map/cond/branch_1_fun/gather | solution.py:281
  7.6 3.1 %collective-permute-start = (bf16[64,256]{1,0:T(8,128)(2,1)S(1)}, bf16[64,256]{1,0:T(8,128)(2,1)S(1)}, u32[]{:S(2)}, u32[]{:S(2)}) collective-permute-start(bf16[64,256]{1,0:T(8,128)(2,1)S(1)} %gather_fusion), channel_id=1, source_target_pairs={{0,2},{1,3},{2,0},{3,1},{4,6},{5,7},{6,4},{7,5},{8,10},{9,11},{10,... | collective-permute-start | bytes 98312 | tf_op jit(solution)/shard_map/cond/branch_1_fun/ppermute | solution.py:262
  10.7 1.9 %collective-permute-done = bf16[64,256]{1,0:T(8,128)(2,1)S(1)} collective-permute-done((bf16[64,256]{1,0:T(8,128)(2,1)S(1)}, bf16[64,256]{1,0:T(8,128)(2,1)S(1)}, u32[]{:S(2)}, u32[]{:S(2)}) %collective-permute-start) | collective-permute-done | bytes 32800 | tf_op jit(solution)/shard_map/cond/branch_1_fun/ppermute | solution.py:262
  12.6 3.0 %collective-permute-start.1 = (bf16[128,256]{1,0:T(8,128)(2,1)S(1)}, bf16[128,256]{1,0:T(8,128)(2,1)S(1)}, u32[]{:S(2)}, u32[]{:S(2)}) collective-permute-start(bf16[128,256]{1,0:T(8,128)(2,1)S(1)} %pad_maximum_fusion.2), channel_id=1, source_target_pairs={{0,4},{1,5},{2,6},{3,7},{4,0},{5,1},{6,2},{7,3},{8,12},{9,13},{10,... | collective-permute-start | bytes 196616 | tf_op jit(solution)/shard_map/cond/branch_1_fun/ppermute | solution.py:262
  15.7 2.2 %collective-permute-done.1 = bf16[128,256]{1,0:T(8,128)(2,1)S(1)} collective-permute-done((bf16[128,256]{1,0:T(8,128)(2,1)S(1)}, bf16[128,256]{1,0:T(8,128)(2,1)S(1)}, u32[]{:S(2)}, u32[]{:S(2)}) %collective-permute-start.1) | collective-permute-done | bytes 65568 | tf_op jit(solution)/shard_map/cond/branch_1_fun/ppermute | solution.py:262
  17.9 1.9 %collective-permute-start.2 = (bf16[256,256]{1,0:T(8,128)(2,1)S(1)}, bf16[256,256]{1,0:T(8,128)(2,1)S(1)}, u32[]{:S(2)}, u32[]{:S(2)}) collective-permute-start(bf16[256,256]{1,0:T(8,128)(2,1)S(1)} %pad_maximum_fusion.1), channel_id=1, source_target_pairs={{0,8},{8,0},{16,24},{24,16},{1,9},{9,1},{17,25},{25,17},{2,10},{10... | collective-permute-start | bytes 393224 | tf_op jit(solution)/shard_map/cond/branch_1_fun/ppermute | solution.py:262
  19.8 0.6 constant_dynamic-update-slice_fusion.4
  20.4 2.5 %collective-permute-done.2 = bf16[256,256]{1,0:T(8,128)(2,1)S(1)} collective-permute-done((bf16[256,256]{1,0:T(8,128)(2,1)S(1)}, bf16[256,256]{1,0:T(8,128)(2,1)S(1)}, u32[]{:S(2)}, u32[]{:S(2)}) %collective-permute-start.2) | collective-permute-done | bytes 131104 | tf_op jit(solution)/shard_map/cond/branch_1_fun/ppermute | solution.py:262
  23.0 1.9 %collective-permute-start.3 = (bf16[512,256]{1,0:T(8,128)(2,1)S(1)}, bf16[512,256]{1,0:T(8,128)(2,1)S(1)}, u32[]{:S(2)}, u32[]{:S(2)}) collective-permute-start(bf16[512,256]{1,0:T(8,128)(2,1)S(1)} %pad_maximum_fusion), channel_id=1, source_target_pairs={{0,16},{8,24},{16,0},{24,8},{1,17},{9,25},{17,1},{25,9},{2,18},{10... | collective-permute-start | bytes 786440 | tf_op jit(solution)/shard_map/cond/branch_1_fun/ppermute | solution.py:262
  24.9 0.6 constant_dynamic-update-slice_fusion.3
  25.5 0.6 constant_dynamic-update-slice_fusion.2
  26.2 0.7 constant_dynamic-update-slice_fusion.1
  26.8 2.6 %collective-permute-done.3 = bf16[512,256]{1,0:T(8,128)(2,1)S(1)} collective-permute-done((bf16[512,256]{1,0:T(8,128)(2,1)S(1)}, bf16[512,256]{1,0:T(8,128)(2,1)S(1)}, u32[]{:S(2)}, u32[]{:S(2)}) %collective-permute-start.3) | collective-permute-done | bytes 262176 | tf_op jit(solution)/shard_map/cond/branch_1_fun/ppermute | solution.py:262
  29.4 0.7 constant_dynamic-update-slice_fusion
  30.2 0.0 collective-permute-start.4
  30.2 1.9 %collective-permute-done.4 = bf16[1024,256]{1,0:T(8,128)(2,1)S(1)} collective-permute-done((bf16[1024,256]{1,0:T(8,128)(2,1)S(1)}, bf16[1024,256]{1,0:T(8,128)(2,1)S(1)}, u32[]{:S(2)}, u32[]{:S(2)}) %collective-permute-start.4) | collective-permute-done | bytes 524320 | tf_op jit(solution)/shard_map/cond/branch_1_fun/ppermute | solution.py:262
  32.1 0.8 constant_dynamic-update-slice_fusion.5
  32.9 0.0 copy-done
  32.9 38.9 %nystrom.1 = (f32[4,2048,256]{2,1,0:T(8,128)S(1)}, f32[2,1024]{1,0:T(2,128)S(1)}) custom-call(s32[32]{0:T(128)S(1)} %get-tuple-element.31.src_ref, s32[32]{0:T(128)S(1)} %get-tuple-element.32.dst_ref, bf16[2048,256]{1,0:T(8,128)(2,1)} %get-tuple-element.33.rows_ref, bf16[2048,256]{1,0:T(8,128)(2,1)} %points_ref.1, f32[1,1024]{1,0:T(1,128)S(1)} %bitcast.2), custom_call_target="tpu_custom_call" | custom-call | tf_op jit(solution)/shard_map/nystrom/pallas_call | solution.py:302
  71.8 0.2 collective-permute-start.5
  72.0 1.0 %collective-permute-done.5 = f32[2,1024]{1,0:T(2,128)S(1)} collective-permute-done((f32[2,1024]{1,0:T(2,128)S(1)}, f32[2,1024]{1,0:T(2,128)S(1)}, u32[]{:S(2)}, u32[]{:S(2)}) %collective-permute-start.5) | collective-permute-done | bytes 8224 | tf_op jit(solution)/shard_map/ppermute | solution.py:262
  73.1 2.0 %collective-permute-start.6 = (f32[2,1024]{1,0:T(2,128)S(1)}, f32[2,1024]{1,0:T(2,128)S(1)}, u32[]{:S(2)}, u32[]{:S(2)}) collective-permute-start(f32[2,1024]{1,0:T(2,128)S(1)} %pad_maximum_fusion.3), channel_id=1, source_target_pairs={{0,2},{1,3},{2,0},{3,1},{4,6},{5,7},{6,4},{7,5},{8,10},{9,11},{10,... | collective-permute-start | bytes 24584 | tf_op jit(solution)/shard_map/ppermute | solution.py:262
  75.0 1.7 %collective-permute-done.6 = f32[2,1024]{1,0:T(2,128)S(1)} collective-permute-done((f32[2,1024]{1,0:T(2,128)S(1)}, f32[2,1024]{1,0:T(2,128)S(1)}, u32[]{:S(2)}, u32[]{:S(2)}) %collective-permute-start.6) | collective-permute-done | bytes 8224 | tf_op jit(solution)/shard_map/ppermute | solution.py:262
  76.8 3.1 %collective-permute-start.7 = (f32[2,1024]{1,0:T(2,128)S(1)}, f32[2,1024]{1,0:T(2,128)S(1)}, u32[]{:S(2)}, u32[]{:S(2)}) collective-permute-start(f32[2,1024]{1,0:T(2,128)S(1)} %pad_maximum_fusion.4), channel_id=1, source_target_pairs={{0,4},{1,5},{2,6},{3,7},{4,0},{5,1},{6,2},{7,3},{8,12},{9,13},{10,... | collective-permute-start | bytes 24584 | tf_op jit(solution)/shard_map/ppermute | solution.py:262
  80.0 1.6 %collective-permute-done.7 = f32[2,1024]{1,0:T(2,128)S(1)} collective-permute-done((f32[2,1024]{1,0:T(2,128)S(1)}, f32[2,1024]{1,0:T(2,128)S(1)}, u32[]{:S(2)}, u32[]{:S(2)}) %collective-permute-start.7) | collective-permute-done | bytes 8224 | tf_op jit(solution)/shard_map/ppermute | solution.py:262
  81.6 1.8 %collective-permute-start.8 = (f32[2,1024]{1,0:T(2,128)S(1)}, f32[2,1024]{1,0:T(2,128)S(1)}, u32[]{:S(2)}, u32[]{:S(2)}) collective-permute-start(f32[2,1024]{1,0:T(2,128)S(1)} %pad_maximum_fusion.5), channel_id=1, source_target_pairs={{0,8},{8,0},{16,24},{24,16},{1,9},{9,1},{17,25},{25,17},{2,10},{10... | collective-permute-start | bytes 24584 | tf_op jit(solution)/shard_map/ppermute | solution.py:262
  83.4 2.0 %collective-permute-done.8 = f32[2,1024]{1,0:T(2,128)S(1)} collective-permute-done((f32[2,1024]{1,0:T(2,128)S(1)}, f32[2,1024]{1,0:T(2,128)S(1)}, u32[]{:S(2)}, u32[]{:S(2)}) %collective-permute-start.8) | collective-permute-done | bytes 8224 | tf_op jit(solution)/shard_map/ppermute | solution.py:262
  85.4 1.8 %collective-permute-start.9 = (f32[2,1024]{1,0:T(2,128)S(1)}, f32[2,1024]{1,0:T(2,128)S(1)}, u32[]{:S(2)}, u32[]{:S(2)}) collective-permute-start(f32[2,1024]{1,0:T(2,128)S(1)} %pad_maximum_fusion.6), channel_id=1, source_target_pairs={{0,16},{8,24},{16,0},{24,8},{1,17},{9,25},{17,1},{25,9},{2,18},{10... | collective-permute-start | bytes 24584 | tf_op jit(solution)/shard_map/ppermute | solution.py:262
  87.2 1.9 %collective-permute-done.9 = f32[2,1024]{1,0:T(2,128)S(1)} collective-permute-done((f32[2,1024]{1,0:T(2,128)S(1)}, f32[2,1024]{1,0:T(2,128)S(1)}, u32[]{:S(2)}, u32[]{:S(2)}) %collective-permute-start.9) | collective-permute-done | bytes 8224 | tf_op jit(solution)/shard_map/ppermute | solution.py:262
  89.1 3.7 %standardize.1 = bf16[2048,1024]{1,0:T(8,128)(2,1)} custom-call(f32[4,2048,256]{2,1,0:T(8,128)S(1)} %get-tuple-element.34.x_ref, f32[1,1024]{1,0:T(1,128)S(1)} %get-tuple-element.51.shift_ref, f32[1,1024]{1,0:T(1,128)S(1)} %get-tuple-element.50.gain_ref), custom_call_target="tpu_custom_call" | custom-call | tf_op jit(solution)/shard_map/standardize/pallas_call | solution.py:335
  (15 shorter events, 0.2 us)
Async XLA Ops:
  0.0 32.9 %copy-start = (f32[1024]{0:T(1024)S(1)}, f32[1024]{0:T(1024)}, u32[]{:S(2)}) copy-start(f32[1024]{0:T(1024)} %param.6) | copy-start | bytes 12292
  7.6 5.0 %collective-permute-start = (bf16[64,256]{1,0:T(8,128)(2,1)S(1)}, bf16[64,256]{1,0:T(8,128)(2,1)S(1)}, u32[]{:S(2)}, u32[]{:S(2)}) collective-permute-start(bf16[64,256]{1,0:T(8,128)(2,1)S(1)} %gather_fusion), channel_id=1, source_target_pairs={{0,2},{1,3},{2,0},{3,1},{4,6},{5,7},{6,4},{7,5},{8,10},{9,11},{10,... | collective-permute-start | bytes 98312 | tf_op jit(solution)/shard_map/cond/branch_1_fun/ppermute | solution.py:262
  12.6 5.3 %collective-permute-start.1 = (bf16[128,256]{1,0:T(8,128)(2,1)S(1)}, bf16[128,256]{1,0:T(8,128)(2,1)S(1)}, u32[]{:S(2)}, u32[]{:S(2)}) collective-permute-start(bf16[128,256]{1,0:T(8,128)(2,1)S(1)} %pad_maximum_fusion.2), channel_id=1, source_target_pairs={{0,4},{1,5},{2,6},{3,7},{4,0},{5,1},{6,2},{7,3},{8,12},{9,13},{10,... | collective-permute-start | bytes 196616 | tf_op jit(solution)/shard_map/cond/branch_1_fun/ppermute | solution.py:262
  17.9 5.0 %collective-permute-start.2 = (bf16[256,256]{1,0:T(8,128)(2,1)S(1)}, bf16[256,256]{1,0:T(8,128)(2,1)S(1)}, u32[]{:S(2)}, u32[]{:S(2)}) collective-permute-start(bf16[256,256]{1,0:T(8,128)(2,1)S(1)} %pad_maximum_fusion.1), channel_id=1, source_target_pairs={{0,8},{8,0},{16,24},{24,16},{1,9},{9,1},{17,25},{25,17},{2,10},{10... | collective-permute-start | bytes 393224 | tf_op jit(solution)/shard_map/cond/branch_1_fun/ppermute | solution.py:262
  23.0 6.4 %collective-permute-start.3 = (bf16[512,256]{1,0:T(8,128)(2,1)S(1)}, bf16[512,256]{1,0:T(8,128)(2,1)S(1)}, u32[]{:S(2)}, u32[]{:S(2)}) collective-permute-start(bf16[512,256]{1,0:T(8,128)(2,1)S(1)} %pad_maximum_fusion), channel_id=1, source_target_pairs={{0,16},{8,24},{16,0},{24,8},{1,17},{9,25},{17,1},{25,9},{2,18},{10... | collective-permute-start | bytes 786440 | tf_op jit(solution)/shard_map/cond/branch_1_fun/ppermute | solution.py:262
  30.2 1.9 %collective-permute-start.4 = (bf16[1024,256]{1,0:T(8,128)(2,1)S(1)}, bf16[1024,256]{1,0:T(8,128)(2,1)S(1)}, u32[]{:S(2)}, u32[]{:S(2)}) collective-permute-start(bf16[1024,256]{1,0:T(8,128)(2,1)S(1)} %get-tuple-element.38), channel_id=1, source_target_pairs={{0,1},{1,0},{2,3},{3,2},{4,5},{5,4},{6,7},{7,6},{8,9},{9,8},{10,11... | collective-permute-start | bytes 1572872 | tf_op jit(solution)/shard_map/cond/branch_1_fun/ppermute | solution.py:262
  71.8 1.2 %collective-permute-start.5 = (f32[2,1024]{1,0:T(2,128)S(1)}, f32[2,1024]{1,0:T(2,128)S(1)}, u32[]{:S(2)}, u32[]{:S(2)}) collective-permute-start(f32[2,1024]{1,0:T(2,128)S(1)} %get-tuple-element.35), channel_id=1, source_target_pairs={{0,1},{1,0},{2,3},{3,2},{4,5},{5,4},{6,7},{7,6},{8,9},{9,8},{10,11... | collective-permute-start | bytes 24584 | tf_op jit(solution)/shard_map/ppermute | solution.py:262
  73.1 3.7 %collective-permute-start.6 = (f32[2,1024]{1,0:T(2,128)S(1)}, f32[2,1024]{1,0:T(2,128)S(1)}, u32[]{:S(2)}, u32[]{:S(2)}) collective-permute-start(f32[2,1024]{1,0:T(2,128)S(1)} %pad_maximum_fusion.3), channel_id=1, source_target_pairs={{0,2},{1,3},{2,0},{3,1},{4,6},{5,7},{6,4},{7,5},{8,10},{9,11},{10,... | collective-permute-start | bytes 24584 | tf_op jit(solution)/shard_map/ppermute | solution.py:262
  76.8 4.8 %collective-permute-start.7 = (f32[2,1024]{1,0:T(2,128)S(1)}, f32[2,1024]{1,0:T(2,128)S(1)}, u32[]{:S(2)}, u32[]{:S(2)}) collective-permute-start(f32[2,1024]{1,0:T(2,128)S(1)} %pad_maximum_fusion.4), channel_id=1, source_target_pairs={{0,4},{1,5},{2,6},{3,7},{4,0},{5,1},{6,2},{7,3},{8,12},{9,13},{10,... | collective-permute-start | bytes 24584 | tf_op jit(solution)/shard_map/ppermute | solution.py:262
  81.6 3.7 %collective-permute-start.8 = (f32[2,1024]{1,0:T(2,128)S(1)}, f32[2,1024]{1,0:T(2,128)S(1)}, u32[]{:S(2)}, u32[]{:S(2)}) collective-permute-start(f32[2,1024]{1,0:T(2,128)S(1)} %pad_maximum_fusion.5), channel_id=1, source_target_pairs={{0,8},{8,0},{16,24},{24,16},{1,9},{9,1},{17,25},{25,17},{2,10},{10... | collective-permute-start | bytes 24584 | tf_op jit(solution)/shard_map/ppermute | solution.py:262
  85.4 3.7 %collective-permute-start.9 = (f32[2,1024]{1,0:T(2,128)S(1)}, f32[2,1024]{1,0:T(2,128)S(1)}, u32[]{:S(2)}, u32[]{:S(2)}) collective-permute-start(f32[2,1024]{1,0:T(2,128)S(1)} %pad_maximum_fusion.6), channel_id=1, source_target_pairs={{0,16},{8,24},{16,0},{24,8},{1,17},{9,25},{17,1},{25,9},{2,18},{10... | collective-permute-start | bytes 24584 | tf_op jit(solution)/shard_map/ppermute | solution.py:262

commit v4 on v3

--- a/solution.py
+++ b/solution.py
@@ -117,7 +117,7 @@
     return jnp.concatenate([x] * (S // B), axis=1)
 
 
-def kernel(src_ref, dst_ref, rows_ref, points_ref, ridge_ref, x_ref, stat_ref,
+def kernel(order, info_ref, low_ref, own_ref, other_ref, points_ref, ridge_ref, x_ref, stat_ref,
            marks_ref, packed_ref, along_ref, a_ref, d_ref, c_ref, l_ref, lt_ref, wt_ref, r_ref):
     m, width = marks_ref.shape
     count = points_ref.shape[0]
@@ -128,13 +128,24 @@
     sub = lax.broadcasted_iota(jnp.int32, (8, B), 0)
     lane = lax.broadcasted_iota(jnp.int32, (8, B), 1)
 
+    half_rows = own_ref.shape[0]
+
     def place(d, carry):
-        rows = rows_ref[pl.ds(pl.multiple_of(src_ref[d] * cap, cap), cap), :].astype(jnp.float32)
+        packed = info_ref[0] != 0
+        far = d ^ info_ref[1]
+        block = 0
+        for k, bit in enumerate(order):
+            block = block + jnp.where((far & bit) != 0, 1 << k, 0)
+        plain = d % (m // cap)
+        source = jnp.where(packed, block, plain) * cap
+        target = jnp.where(packed, low_ref[d], plain * cap)
+        at = pl.ds(pl.multiple_of(source % half_rows, cap), cap)
+        rows = jnp.where(source < half_rows, own_ref[at, :], other_ref[at, :]).astype(jnp.float32)
         for c in range(width // B):
-            packed_ref[c, pl.ds(dst_ref[d], cap), :] = rows[:, c * B:(c + 1) * B]
+            packed_ref[c, pl.ds(target, cap), :] = rows[:, c * B:(c + 1) * B]
         return carry
 
-    lax.fori_loop(0, src_ref.shape[0], place, 0)
+    lax.fori_loop(0, 1 << len(order), place, 0)
     marks_ref[...] = jnp.concatenate([packed_ref[c, :m] for c in range(width // B)], axis=1).astype(jnp.bfloat16)
     marks = marks_ref[...]
     along, down = square_sums(marks)
@@ -255,6 +266,40 @@
         out_ref[:, here] = ((x_ref[p, rows, :] - shift_ref[:, here]) * gain_ref[:, here]).astype(out_ref.dtype)
 
 
+def pack(devices, me_ref, ids_ref, line_ref, points_ref, rows_ref, low_ref, most_ref):
+    cap = rows_ref.shape[0]
+    count = points_ref.shape[0]
+    m = ids_ref.shape[0]
+    start = me_ref[0] * count
+
+    def search(_, bounds):
+        low, high = bounds
+        middle = (low + high) // 2
+        inside = (low < high) & (ids_ref[jnp.minimum(middle, m - 1)] < start)
+        return jnp.where(inside, middle + 1, low), jnp.where(inside, high, jnp.where(low < high, middle, high))
+
+    first, _ = lax.fori_loop(0, m.bit_length(), search, (jnp.int32(0), jnp.int32(m)))
+    sub = lax.broadcasted_iota(jnp.int32, (8, B), 0)
+    groups = []
+    for g in range(cap // 8):
+        slots = jnp.zeros((8, B), jnp.int32)
+        for i in range(8):
+            slots = jnp.where(sub == i, ids_ref[jnp.minimum(first + 8 * g + i, m - 1)] - start, slots)
+        groups.append(slots)
+    slots = jnp.concatenate(groups, axis=0)
+    lane = lax.broadcasted_iota(jnp.int32, (cap, B), 1)
+    picks = [(slots == lane + c * B).astype(jnp.float32).astype(jnp.bfloat16) for c in range(count // B)]
+    rows_ref[...] = dot(jnp.concatenate(picks, axis=1), points_ref[...]).astype(rows_ref.dtype)
+    size = low_ref.shape[1]
+    device = lax.broadcasted_iota(jnp.int32, (size, m), 0)
+    line = jnp.broadcast_to(line_ref[...], (size, m))
+    ones = jnp.ones((8, m), jnp.bfloat16)
+    low = dot_nt(ones, (line < device * count).astype(jnp.float32).astype(jnp.bfloat16))
+    high = dot_nt(ones, (line < (device + 1) * count).astype(jnp.float32).astype(jnp.bfloat16))
+    low_ref[...] = low[0:1].astype(jnp.int32)
+    most_ref[...] = jnp.broadcast_to(jnp.max(high - low, axis=1, keepdims=True)[0:1], most_ref.shape).astype(jnp.int32)
+
+
 def exchange(x, bit):
     dev = lax.axis_size("dev")
     axis, flip = ("dev", bit) if bit < dev else ("grp", bit // dev)
@@ -270,41 +315,52 @@
     mean = m / devices
     cap = min(m, 16 * math.ceil((mean + 5.6 * math.sqrt(mean)) / 16))
     bits = [1 << b for b in range(devices.bit_length() - 1)]
-    order = bits[1:] + bits[:1]
-
-    bounds = jnp.sum(landmark_ids[None, :] < (jnp.arange(devices + 1) * count)[:, None], axis=1, dtype=jnp.int32)
-    low = bounds[:-1]
-    fits = jnp.max(bounds[1:] - low) <= cap
-
-    def packed(points, ids):
-        mine = lax.dynamic_slice(jnp.pad(ids, (0, cap)), (low[me],), (cap,))
-        rows = points[jnp.clip(mine - me * count, 0, count - 1)]
-        for bit in order:
-            rows = jnp.concatenate([rows, exchange(rows, bit)], axis=0)
-        far = jnp.arange(devices, dtype=jnp.int32) ^ me
-        place = jnp.zeros_like(far)
-        for k, bit in enumerate(order):
-            place = place + jnp.where((far & bit) != 0, 1 << k, 0)
-        return rows, place, low
-
-    def summed(points, ids):
+    near = [bit for bit in bits[1:] if bit < lax.axis_size("dev")]
+    far = [bit for bit in bits[1:] if bit >= lax.axis_size("dev")]
+    order = (*near, *far, bits[0])
+    vmem = pl.BlockSpec(memory_space=pltpu.VMEM)
+    table = -(-devices // B) * B
+
+    rows, low, most = pl.pallas_call(
+        functools.partial(pack, devices),
+        grid_spec=pltpu.PrefetchScalarGridSpec(
+            num_scalar_prefetch=2, grid=(), in_specs=[vmem, vmem], out_specs=[vmem, vmem, vmem],
+        ),
+        out_shape=(
+            jax.ShapeDtypeStruct((cap, width), points.dtype),
+            jax.ShapeDtypeStruct((1, table), jnp.int32),
+            jax.ShapeDtypeStruct((1, B), jnp.int32),
+        ),
+        compiler_params=pltpu.CompilerParams(vmem_limit_bytes=16 << 20),
+        name="pack",
+    )(me[None], landmark_ids, landmark_ids[None, :], points)
+    fits = most[0, 0] <= cap
+
+    def packed(rows, points, ids):
+        for some in (near, far):
+            for at in range(0, len(some), 2):
+                pair = some[at:at + 2]
+                moves = pair if len(pair) == 1 else (pair[0], pair[1], pair[0] | pair[1])
+                rows = jnp.concatenate([rows, *(exchange(rows, move) for move in moves)], axis=0)
+        return rows, exchange(rows, bits[0])
+
+    def summed(rows, points, ids):
         offset = ids - me * count
         inside = (offset >= 0) & (offset < count)
         picked = points[jnp.clip(offset, 0, count - 1)]
         rows = lax.psum(jnp.where(inside[:, None], picked.astype(jnp.float32), 0.0), AXES).astype(points.dtype)
-        rows = jnp.pad(rows, ((0, max(0, devices * cap - m)), (0, 0)))
-        place = jnp.arange(devices, dtype=jnp.int32) % (m // cap)
-        return rows, place, place * cap
-
-    rows, src, dst = lax.cond(fits, packed, summed, points, landmark_ids)
-
-    vmem = pl.BlockSpec(memory_space=pltpu.VMEM)
+        rows = jnp.pad(rows, ((0, devices * cap - m), (0, 0)))
+        return rows[:devices * cap // 2], rows[devices * cap // 2:]
+
+    own, other = lax.cond(fits, packed, summed, rows, points, landmark_ids)
+    info = jnp.stack([fits.astype(jnp.int32), me])
+
     raw, stat = pl.pallas_call(
-        kernel,
+        functools.partial(kernel, order),
         grid_spec=pltpu.PrefetchScalarGridSpec(
             num_scalar_prefetch=2,
             grid=(),
-            in_specs=[vmem, vmem, vmem],
+            in_specs=[vmem, vmem, vmem, vmem],
             out_specs=[vmem, vmem],
             scratch_shapes=[
                 pltpu.VMEM((m, width), jnp.bfloat16),
@@ -322,7 +378,7 @@
         out_shape=(pltpu.VMEM((m // S, count, S), jnp.float32), jax.ShapeDtypeStruct((2, m), jnp.float32)),
         compiler_params=pltpu.CompilerParams(vmem_limit_bytes=40 << 20),
         name="nystrom",
-    )(src, dst, rows, points, ridge[None, :])
+    )(info, low[0], own, other, points, ridge[None, :])
 
     total = count
     for bit in bits:

time: 93.1 us -> 86.1 us (0.925)
  Pallas kernels: 42.6 us -> 45.7 us
  starting transfers between devices: 18.8 us -> 15.9 us
  other arithmetic: 2.56 us -> 0.21 us
  local copies, waits for them, and re-layouts: 6.72 us -> 4.47 us
  loops' own time: 1.98 us -> 0.01 us
    pallas_call x1 -> x2, Pallas kernels: 38.9 us -> 41.9 us  [the longest x1 39.4 us: shards(): pl.pallas_call(functools.partial(kernel, order), grid_spec=pltpu.Prefetch...]
    ppermute x10 -> x12, starting transfers between devices: 18.8 us -> 15.9 us  [exchange(): return lax.ppermute(x, axis, [(k, k ^ flip) for k in range(size)])]
    gather x1 -> x0, local copies, waits for them, and re-layouts: 2.02 us -> none  [packed(): rows = points[jnp.clip(mine - me * count, 0, count - 1)]]
    another operation x1, loops' own time: 1.98 us -> 0.01 us  [shards(): own, other = lax.cond(fits, packed, summed, rows, points, landmark_ids)]
    cond x4 -> x5, local copies, waits for them, and re-layouts: 2.55 us -> 3.19 us
    ppermute x10 -> x12, waiting for transfers between devices: 19.4 us -> 19.6 us  [exchange(): return lax.ppermute(x, axis, [(k, k ^ flip) for k in range(size)])]
  transfers between devices with their start and end apart: 10 -> 12, of which waited for: 10 -> 11; matrix products, arithmetic and copies ran while one was open for 3% -> 4% of each run, Pallas kernels for 0% -> 0%
where the time goes in v4:
time: 86.1 us; the launch traced here: 85.9 us
  Pallas kernels  45.7 us (53%)
  waiting for transfers between devices  19.6 us (23%)
  starting transfers between devices  15.9 us (18%)
  local copies, waits for them, and re-layouts  4.47 us (5%)
    pallas_call x1, Pallas kernels, shards(): pl.pallas_call(functools.partial(kernel, order), grid_spec=pltpu.Prefetch...  39.4 us
    ppermute x12, waiting for transfers between devices, exchange(): return lax.ppermute(x, axis, [(k, k ^ flip) for k in range(size)])  19.6 us
    ppermute x12, starting transfers between devices, exchange(): return lax.ppermute(x, axis, [(k, k ^ flip) for k in range(size)])  15.9 us
    pallas_call x1, Pallas kernels, shards(): pl.pallas_call(standardize, grid=(count // 256,), in_specs=[vmem, vector,...  3.73 us
    cond x5, local copies, waits for them, and re-layouts  3.19 us
    pallas_call x1, Pallas kernels, shards(): pl.pallas_call(functools.partial(pack, devices), grid_spec=pltpu.Prefetch...  2.55 us
  transfers between devices with their start and end apart: 12, of which 11 were waited for; matrix products, arithmetic and copies ran while one was open for 4% of the time, Pallas kernels for 0%

profile of v4, /device:TPU:0, one launch (start us, length us, event | category | flops | bytes accessed | tf_op | source)
XLA Modules:
  0.0 85.9 jit_solution(2896661571014733163)
XLA Ops:
  0.0 0.0 copy-start
  0.0 2.6 %pack.1 = (bf16[64,256]{1,0:T(8,128)(2,1)S(1)}, s32[1,128]{1,0:T(1,128)S(1)}, s32[1,128]{1,0:T(1,128)S(1)}) custom-call(s32[1]{0:T(128)} %bitcast.me_ref, s32[1024]{0:T(1024)} %ids_ref.1, s32[1,1024]{1,0:T(1,128)} %bitcast.10, bf16[2048,256]{1,0:T(8,128)(2,1)} %points_ref.3), custom_call_target="tpu_custom_call" | custom-call | tf_op jit(solution)/shard_map/pack/pallas_call | solution.py:324
  2.6 0.1 pad_add_fusion.info_ref
  2.7 23.0 %conditional.1 = (bf16[1024,256]{1,0:T(8,128)(2,1)}, bf16[1024,256]{1,0:T(8,128)(2,1)}) conditional(s32[]{:T(128)} %bitcast.4, (s32[]{:T(128)}, s32[1024]{0:T(1024)}, bf16[2048,256]{1,0:T(8,128)(2,1)}) %tuple.13, bf16[64,256]{1,0:T(8,128)(2,1)S(1)} %get-tuple-element.24), branch_computations={%region_0.2_spmd, %region_2.3_spmd} | conditional | flops 796673 | bytes 5243176 | solution.py:355
  2.7 5.1 %collective-permute-start.2 = (bf16[64,256]{1,0:T(8,128)(2,1)S(1)}, bf16[64,256]{1,0:T(8,128)(2,1)S(1)}, u32[]{:S(2)}, u32[]{:S(2)}) collective-permute-start(bf16[64,256]{1,0:T(8,128)(2,1)S(1)} %param.1), channel_id=1, source_target_pairs={{0,6},{1,7},{2,4},{3,5},{4,2},{5,3},{6,0},{7,1},{8,14},{9,15},{10,... | collective-permute-start | bytes 98312 | tf_op jit(solution)/shard_map/cond/branch_1_fun/ppermute | solution.py:307
  7.8 0.0 collective-permute-start.1
  7.8 0.6 collective-permute-start
  8.4 0.6 constant_dynamic-update-slice_fusion.3
  9.1 2.7 %collective-permute-done = bf16[64,256]{1,0:T(8,128)(2,1)S(1)} collective-permute-done((bf16[64,256]{1,0:T(8,128)(2,1)S(1)}, bf16[64,256]{1,0:T(8,128)(2,1)S(1)}, u32[]{:S(2)}, u32[]{:S(2)}) %collective-permute-start) | collective-permute-done | bytes 32800 | tf_op jit(solution)/shard_map/cond/branch_1_fun/ppermute | solution.py:307
  11.7 0.6 constant_dynamic-update-slice_fusion.2
  12.3 0.3 collective-permute-done.1
  12.6 0.6 constant_dynamic-update-slice_fusion.1
  13.2 0.0 collective-permute-done.2
  13.2 0.6 constant_dynamic-update-slice_fusion
  13.9 1.5 %collective-permute-start.3 = (bf16[256,256]{1,0:T(8,128)(2,1)S(1)}, bf16[256,256]{1,0:T(8,128)(2,1)S(1)}, u32[]{:S(2)}, u32[]{:S(2)}) collective-permute-start(bf16[256,256]{1,0:T(8,128)(2,1)S(1)} %get-tuple-element.29), channel_id=1, source_target_pairs={{0,8},{8,0},{16,24},{24,16},{1,9},{9,1},{17,25},{25,17},{2,10},{10... | collective-permute-start | bytes 393224 | tf_op jit(solution)/shard_map/cond/branch_1_fun/ppermute | solution.py:307
  15.3 1.5 %collective-permute-start.4 = (bf16[256,256]{1,0:T(8,128)(2,1)S(1)}, bf16[256,256]{1,0:T(8,128)(2,1)S(1)}, u32[]{:S(2)}, u32[]{:S(2)}) collective-permute-start(bf16[256,256]{1,0:T(8,128)(2,1)S(1)} %get-tuple-element.29), channel_id=1, source_target_pairs={{0,16},{8,24},{16,0},{24,8},{1,17},{9,25},{17,1},{25,9},{2,18},{10... | collective-permute-start | bytes 393224 | tf_op jit(solution)/shard_map/cond/branch_1_fun/ppermute | solution.py:307
  16.9 0.5 collective-permute-start.5
  17.3 2.7 %collective-permute-done.3 = bf16[256,256]{1,0:T(8,128)(2,1)S(1)} collective-permute-done((bf16[256,256]{1,0:T(8,128)(2,1)S(1)}, bf16[256,256]{1,0:T(8,128)(2,1)S(1)}, u32[]{:S(2)}, u32[]{:S(2)}) %collective-permute-start.3) | collective-permute-done | bytes 131104 | tf_op jit(solution)/shard_map/cond/branch_1_fun/ppermute | solution.py:307
  20.1 0.7 constant_dynamic-update-slice_fusion.6
  20.7 0.6 collective-permute-done.4
  21.3 0.7 constant_dynamic-update-slice_fusion.5
  21.9 0.8 collective-permute-done.5
  22.7 0.7 constant_dynamic-update-slice_fusion.4
  23.4 0.0 collective-permute-start.6
  23.4 2.2 %collective-permute-done.6 = bf16[1024,256]{1,0:T(8,128)(2,1)} collective-permute-done((bf16[1024,256]{1,0:T(8,128)(2,1)}, bf16[1024,256]{1,0:T(8,128)(2,1)}, u32[]{:S(2)}, u32[]{:S(2)}) %collective-permute-start.6) | collective-permute-done | bytes 524320 | tf_op jit(solution)/shard_map/cond/branch_1_fun/ppermute | solution.py:307
  25.6 0.0 copy-done
  25.7 39.4 %nystrom.1 = (f32[4,2048,256]{2,1,0:T(8,128)S(1)}, f32[2,1024]{1,0:T(2,128)S(1)}) custom-call(s32[2]{0:T(128)S(1)} %pad_add_fusion.info_ref, s32[128]{0:T(128)S(1)} %bitcast.8, bf16[1024,256]{1,0:T(8,128)(2,1)} %get-tuple-element.25.own_ref, bf16[1024,256]{1,0:T(8,128)(2,1)} %get-tuple-element.26.other_ref, bf16[2048,256]{1,0:T(8,128)(2,1)} %points_ref.3, ...), custom_call_target="tpu_custom_call" | custom-call | tf_op jit(solution)/shard_map/nystrom/pallas_call | solution.py:358
  65.0 0.2 collective-permute-start.7
  65.2 1.0 %collective-permute-done.7 = f32[2,1024]{1,0:T(2,128)S(1)} collective-permute-done((f32[2,1024]{1,0:T(2,128)S(1)}, f32[2,1024]{1,0:T(2,128)S(1)}, u32[]{:S(2)}, u32[]{:S(2)}) %collective-permute-start.7) | collective-permute-done | bytes 8224 | tf_op jit(solution)/shard_map/ppermute | solution.py:307
  66.3 1.4 %collective-permute-start.8 = (f32[2,1024]{1,0:T(2,128)S(1)}, f32[2,1024]{1,0:T(2,128)S(1)}, u32[]{:S(2)}, u32[]{:S(2)}) collective-permute-start(f32[2,1024]{1,0:T(2,128)S(1)} %pad_maximum_fusion), channel_id=1, source_target_pairs={{0,2},{1,3},{2,0},{3,1},{4,6},{5,7},{6,4},{7,5},{8,10},{9,11},{10,... | collective-permute-start | bytes 24584 | tf_op jit(solution)/shard_map/ppermute | solution.py:307
  67.7 2.3 %collective-permute-done.8 = f32[2,1024]{1,0:T(2,128)S(1)} collective-permute-done((f32[2,1024]{1,0:T(2,128)S(1)}, f32[2,1024]{1,0:T(2,128)S(1)}, u32[]{:S(2)}, u32[]{:S(2)}) %collective-permute-start.8) | collective-permute-done | bytes 8224 | tf_op jit(solution)/shard_map/ppermute | solution.py:307
  70.1 2.7 %collective-permute-start.9 = (f32[2,1024]{1,0:T(2,128)S(1)}, f32[2,1024]{1,0:T(2,128)S(1)}, u32[]{:S(2)}, u32[]{:S(2)}) collective-permute-start(f32[2,1024]{1,0:T(2,128)S(1)} %pad_maximum_fusion.1), channel_id=1, source_target_pairs={{0,4},{1,5},{2,6},{3,7},{4,0},{5,1},{6,2},{7,3},{8,12},{9,13},{10,... | collective-permute-start | bytes 24584 | tf_op jit(solution)/shard_map/ppermute | solution.py:307
  72.8 1.9 %collective-permute-done.9 = f32[2,1024]{1,0:T(2,128)S(1)} collective-permute-done((f32[2,1024]{1,0:T(2,128)S(1)}, f32[2,1024]{1,0:T(2,128)S(1)}, u32[]{:S(2)}, u32[]{:S(2)}) %collective-permute-start.9) | collective-permute-done | bytes 8224 | tf_op jit(solution)/shard_map/ppermute | solution.py:307
  74.7 0.6 collective-permute-start.10
  75.3 3.1 %collective-permute-done.10 = f32[2,1024]{1,0:T(2,128)S(1)} collective-permute-done((f32[2,1024]{1,0:T(2,128)S(1)}, f32[2,1024]{1,0:T(2,128)S(1)}, u32[]{:S(2)}, u32[]{:S(2)}) %collective-permute-start.10) | collective-permute-done | bytes 8224 | tf_op jit(solution)/shard_map/ppermute | solution.py:307
  78.5 1.7 %collective-permute-start.11 = (f32[2,1024]{1,0:T(2,128)S(1)}, f32[2,1024]{1,0:T(2,128)S(1)}, u32[]{:S(2)}, u32[]{:S(2)}) collective-permute-start(f32[2,1024]{1,0:T(2,128)S(1)} %pad_maximum_fusion.3), channel_id=1, source_target_pairs={{0,16},{8,24},{16,0},{24,8},{1,17},{9,25},{17,1},{25,9},{2,18},{10... | collective-permute-start | bytes 24584 | tf_op jit(solution)/shard_map/ppermute | solution.py:307
  80.2 2.0 %collective-permute-done.11 = f32[2,1024]{1,0:T(2,128)S(1)} collective-permute-done((f32[2,1024]{1,0:T(2,128)S(1)}, f32[2,1024]{1,0:T(2,128)S(1)}, u32[]{:S(2)}, u32[]{:S(2)}) %collective-permute-start.11) | collective-permute-done | bytes 8224 | tf_op jit(solution)/shard_map/ppermute | solution.py:307
  82.2 3.7 %standardize.1 = bf16[2048,1024]{1,0:T(8,128)(2,1)} custom-call(f32[4,2048,256]{2,1,0:T(8,128)S(1)} %get-tuple-element.27.x_ref, f32[1,1024]{1,0:T(1,128)S(1)} %get-tuple-element.40.shift_ref, f32[1,1024]{1,0:T(1,128)S(1)} %get-tuple-element.39.gain_ref), custom_call_target="tpu_custom_call" | custom-call | tf_op jit(solution)/shard_map/standardize/pallas_call | solution.py:391
  (9 shorter events, 0.1 us)
Async XLA Ops:
  0.0 25.7 %copy-start = (f32[1024]{0:T(1024)S(1)}, f32[1024]{0:T(1024)}, u32[]{:S(2)}) copy-start(f32[1024]{0:T(1024)} %param.6) | copy-start | bytes 12292
  2.7 10.5 %collective-permute-start.2 = (bf16[64,256]{1,0:T(8,128)(2,1)S(1)}, bf16[64,256]{1,0:T(8,128)(2,1)S(1)}, u32[]{:S(2)}, u32[]{:S(2)}) collective-permute-start(bf16[64,256]{1,0:T(8,128)(2,1)S(1)} %param.1), channel_id=1, source_target_pairs={{0,6},{1,7},{2,4},{3,5},{4,2},{5,3},{6,0},{7,1},{8,14},{9,15},{10,... | collective-permute-start | bytes 98312 | tf_op jit(solution)/shard_map/cond/branch_1_fun/ppermute | solution.py:307
  7.8 4.8 %collective-permute-start.1 = (bf16[64,256]{1,0:T(8,128)(2,1)S(1)}, bf16[64,256]{1,0:T(8,128)(2,1)S(1)}, u32[]{:S(2)}, u32[]{:S(2)}) collective-permute-start(bf16[64,256]{1,0:T(8,128)(2,1)S(1)} %param.1), channel_id=1, source_target_pairs={{0,4},{1,5},{2,6},{3,7},{4,0},{5,1},{6,2},{7,3},{8,12},{9,13},{10,... | collective-permute-start | bytes 98312 | tf_op jit(solution)/shard_map/cond/branch_1_fun/ppermute | solution.py:307
  7.8 3.9 %collective-permute-start = (bf16[64,256]{1,0:T(8,128)(2,1)S(1)}, bf16[64,256]{1,0:T(8,128)(2,1)S(1)}, u32[]{:S(2)}, u32[]{:S(2)}) collective-permute-start(bf16[64,256]{1,0:T(8,128)(2,1)S(1)} %param.1), channel_id=1, source_target_pairs={{0,2},{1,3},{2,0},{3,1},{4,6},{5,7},{6,4},{7,5},{8,10},{9,11},{10,... | collective-permute-start | bytes 98312 | tf_op jit(solution)/shard_map/cond/branch_1_fun/ppermute | solution.py:307
  13.9 6.2 %collective-permute-start.3 = (bf16[256,256]{1,0:T(8,128)(2,1)S(1)}, bf16[256,256]{1,0:T(8,128)(2,1)S(1)}, u32[]{:S(2)}, u32[]{:S(2)}) collective-permute-start(bf16[256,256]{1,0:T(8,128)(2,1)S(1)} %get-tuple-element.29), channel_id=1, source_target_pairs={{0,8},{8,0},{16,24},{24,16},{1,9},{9,1},{17,25},{25,17},{2,10},{10... | collective-permute-start | bytes 393224 | tf_op jit(solution)/shard_map/cond/branch_1_fun/ppermute | solution.py:307
  15.3 5.9 %collective-permute-start.4 = (bf16[256,256]{1,0:T(8,128)(2,1)S(1)}, bf16[256,256]{1,0:T(8,128)(2,1)S(1)}, u32[]{:S(2)}, u32[]{:S(2)}) collective-permute-start(bf16[256,256]{1,0:T(8,128)(2,1)S(1)} %get-tuple-element.29), channel_id=1, source_target_pairs={{0,16},{8,24},{16,0},{24,8},{1,17},{9,25},{17,1},{25,9},{2,18},{10... | collective-permute-start | bytes 393224 | tf_op jit(solution)/shard_map/cond/branch_1_fun/ppermute | solution.py:307
  16.9 5.9 %collective-permute-start.5 = (bf16[256,256]{1,0:T(8,128)(2,1)S(1)}, bf16[256,256]{1,0:T(8,128)(2,1)S(1)}, u32[]{:S(2)}, u32[]{:S(2)}) collective-permute-start(bf16[256,256]{1,0:T(8,128)(2,1)S(1)} %get-tuple-element.29), channel_id=1, source_target_pairs={{0,24},{8,16},{16,8},{24,0},{1,25},{9,17},{17,9},{25,1},{2,26},{10... | collective-permute-start | bytes 393224 | tf_op jit(solution)/shard_map/cond/branch_1_fun/ppermute | solution.py:307
  23.4 2.3 %collective-permute-start.6 = (bf16[1024,256]{1,0:T(8,128)(2,1)}, bf16[1024,256]{1,0:T(8,128)(2,1)}, u32[]{:S(2)}, u32[]{:S(2)}) collective-permute-start(bf16[1024,256]{1,0:T(8,128)(2,1)} %constant_dynamic-update-slice_fusion.4), channel_id=1, source_target_pairs={{0,1},{1,0},{2,3},{3,2},{4,5},{5,4},{6,7},{7,6},{8,9},{9,8},{10,11... | collective-permute-start | bytes 1572872 | tf_op jit(solution)/shard_map/cond/branch_1_fun/ppermute | solution.py:307
  65.0 1.2 %collective-permute-start.7 = (f32[2,1024]{1,0:T(2,128)S(1)}, f32[2,1024]{1,0:T(2,128)S(1)}, u32[]{:S(2)}, u32[]{:S(2)}) collective-permute-start(f32[2,1024]{1,0:T(2,128)S(1)} %get-tuple-element.28), channel_id=1, source_target_pairs={{0,1},{1,0},{2,3},{3,2},{4,5},{5,4},{6,7},{7,6},{8,9},{9,8},{10,11... | collective-permute-start | bytes 24584 | tf_op jit(solution)/shard_map/ppermute | solution.py:307
  66.3 3.7 %collective-permute-start.8 = (f32[2,1024]{1,0:T(2,128)S(1)}, f32[2,1024]{1,0:T(2,128)S(1)}, u32[]{:S(2)}, u32[]{:S(2)}) collective-permute-start(f32[2,1024]{1,0:T(2,128)S(1)} %pad_maximum_fusion), channel_id=1, source_target_pairs={{0,2},{1,3},{2,0},{3,1},{4,6},{5,7},{6,4},{7,5},{8,10},{9,11},{10,... | collective-permute-start | bytes 24584 | tf_op jit(solution)/shard_map/ppermute | solution.py:307
  70.1 4.6 %collective-permute-start.9 = (f32[2,1024]{1,0:T(2,128)S(1)}, f32[2,1024]{1,0:T(2,128)S(1)}, u32[]{:S(2)}, u32[]{:S(2)}) collective-permute-start(f32[2,1024]{1,0:T(2,128)S(1)} %pad_maximum_fusion.1), channel_id=1, source_target_pairs={{0,4},{1,5},{2,6},{3,7},{4,0},{5,1},{6,2},{7,3},{8,12},{9,13},{10,... | collective-permute-start | bytes 24584 | tf_op jit(solution)/shard_map/ppermute | solution.py:307
  74.7 3.7 %collective-permute-start.10 = (f32[2,1024]{1,0:T(2,128)S(1)}, f32[2,1024]{1,0:T(2,128)S(1)}, u32[]{:S(2)}, u32[]{:S(2)}) collective-permute-start(f32[2,1024]{1,0:T(2,128)S(1)} %pad_maximum_fusion.2), channel_id=1, source_target_pairs={{0,8},{8,0},{16,24},{24,16},{1,9},{9,1},{17,25},{25,17},{2,10},{10... | collective-permute-start | bytes 24584 | tf_op jit(solution)/shard_map/ppermute | solution.py:307
  78.5 3.7 %collective-permute-start.11 = (f32[2,1024]{1,0:T(2,128)S(1)}, f32[2,1024]{1,0:T(2,128)S(1)}, u32[]{:S(2)}, u32[]{:S(2)}) collective-permute-start(f32[2,1024]{1,0:T(2,128)S(1)} %pad_maximum_fusion.3), channel_id=1, source_target_pairs={{0,16},{8,24},{16,0},{24,8},{1,17},{9,25},{17,1},{25,9},{2,18},{10... | collective-permute-start | bytes 24584 | tf_op jit(solution)/shard_map/ppermute | solution.py:307

commit v5 on v4

--- a/solution.py
+++ b/solution.py
@@ -117,8 +117,9 @@
     return jnp.concatenate([x] * (S // B), axis=1)
 
 
-def kernel(order, info_ref, low_ref, own_ref, other_ref, points_ref, ridge_ref, x_ref, stat_ref,
-           marks_ref, packed_ref, along_ref, a_ref, d_ref, c_ref, l_ref, lt_ref, wt_ref, r_ref):
+def kernel(order, info_ref, low_ref, *refs):
+    (*piece_refs, points_ref, ridge_ref, x_ref, stat_ref, marks_ref, rows_ref, packed_ref, along_ref, a_ref, d_ref,
+     c_ref, l_ref, lt_ref, wt_ref, r_ref) = refs
     m, width = marks_ref.shape
     count = points_ref.shape[0]
     scale = 1.0 / (2.0 * width)
@@ -128,7 +129,9 @@
     sub = lax.broadcasted_iota(jnp.int32, (8, B), 0)
     lane = lax.broadcasted_iota(jnp.int32, (8, B), 1)
 
-    half_rows = own_ref.shape[0]
+    size = piece_refs[0].shape[0]
+    for k, piece_ref in enumerate(piece_refs):
+        rows_ref[k * size:(k + 1) * size, :] = piece_ref[...]
 
     def place(d, carry):
         packed = info_ref[0] != 0
@@ -139,8 +142,7 @@
         plain = d % (m // cap)
         source = jnp.where(packed, block, plain) * cap
         target = jnp.where(packed, low_ref[d], plain * cap)
-        at = pl.ds(pl.multiple_of(source % half_rows, cap), cap)
-        rows = jnp.where(source < half_rows, own_ref[at, :], other_ref[at, :]).astype(jnp.float32)
+        rows = rows_ref[pl.ds(pl.multiple_of(source, cap), cap), :].astype(jnp.float32)
         for c in range(width // B):
             packed_ref[c, pl.ds(target, cap), :] = rows[:, c * B:(c + 1) * B]
         return carry
@@ -174,7 +176,8 @@
         rows = pl.ds(at, ROWS)
         raw = dot3(split(x_ref[p, rows, :]), (wt_ref[0], wt_ref[1]))
         x_ref[p, rows, :] = raw
-        r_ref[0, rows, :], r_ref[1, rows, :] = split(raw)
+        keep = 2 * (p % 2)
+        r_ref[keep, rows, :], r_ref[keep + 1, rows, :] = split(raw)
         mean = jnp.mean(raw, axis=0, keepdims=True)
         spread = jnp.sum(jnp.square(raw - mean), axis=0, keepdims=True)
         before = jnp.asarray(at).astype(jnp.float32)
@@ -186,7 +189,8 @@
     def update_piece(p, j, at):
         rows = pl.ds(at, ROWS)
         right = [lt_ref[h, p * S:(p + 1) * S, j * S:(j + 1) * S] for h in range(2)]
-        x_ref[j, rows, :] -= dot3((r_ref[0, rows, :], r_ref[1, rows, :]), right)
+        keep = 2 * (p % 2)
+        x_ref[j, rows, :] -= dot3((r_ref[keep, rows, :], r_ref[keep + 1, rows, :]), right)
 
     def core_piece(p, j, odd):
         size = (m - j * S) // 2
@@ -225,6 +229,9 @@
                 a_ref[p + 1, top:, :] -= dot3((l_ref[keep, top:, :], l_ref[keep + 1, top:, :]), right)
                 d_ref[0] = a_ref[p + 1, top:top + B, :B]
 
+    def turn(q, j):
+        return q + 2 if q and j > q + 1 else min(max(j - 1, q + 1), q + 2)
+
     for p in range(stages):
         def stage(odd, carry, p=p):
             pieces = []
@@ -233,11 +240,12 @@
                     pieces.append(functools.partial(core_piece, p - 1, j, odd))
             for block in range(half // ROWS):
                 at = pl.multiple_of(odd * half + block * ROWS, ROWS)
-                if p == 0:
-                    pieces += [functools.partial(cross_piece, j, at) for j in range(stages)]
-                else:
+                if p:
                     pieces.append(functools.partial(raw_piece, p - 1, at))
-                    pieces += [functools.partial(update_piece, p - 1, j, at) for j in range(p, stages)]
+                for j in range(stages):
+                    if p == min(max(j - 1, 0), 2):
+                        pieces.append(functools.partial(cross_piece, j, at))
+                    pieces += [functools.partial(update_piece, q, j, at) for q in range(j) if p == turn(q, j)]
             done = 0
             for k in factor_block(d_ref.at[0], c_ref, sub, lane):
                 until = -(-len(pieces) * (k + 1) // 14)
@@ -258,18 +266,27 @@
     lax.fori_loop(0, 2, last, 0)
 
 
-def standardize(x_ref, shift_ref, gain_ref, out_ref):
-    size = out_ref.shape[0]
-    rows = pl.ds(pl.multiple_of(pl.program_id(0) * size, size), size)
-    for p in range(x_ref.shape[0]):
-        here = slice(p * S, (p + 1) * S)
-        out_ref[:, here] = ((x_ref[p, rows, :] - shift_ref[:, here]) * gain_ref[:, here]).astype(out_ref.dtype)
-
-
-def pack(devices, me_ref, ids_ref, line_ref, points_ref, rows_ref, low_ref, most_ref):
+def standardize(x_ref, shift_ref, gain_ref, out_hbm, out_ref, sems):
+    steps, size, _ = out_ref.shape
+
+    def copy(k):
+        return pltpu.make_async_copy(out_ref.at[k], out_hbm.at[k * size:(k + 1) * size, :], sems.at[k])
+
+    for k in range(steps):
+        for p in range(x_ref.shape[0]):
+            here = slice(p * S, (p + 1) * S)
+            x = x_ref[p, k * size:(k + 1) * size, :]
+            out_ref[k, :, here] = ((x - shift_ref[:, here]) * gain_ref[:, here]).astype(out_ref.dtype)
+        copy(k).start()
+    for k in range(steps):
+        copy(k).wait()
+
+
+def pack(devices, me_ref, ids_ref, line_ref, points_ref, rows_ref, low_ref, most_ref, kept_ref):
     cap = rows_ref.shape[0]
     count = points_ref.shape[0]
     m = ids_ref.shape[0]
+    kept_ref[...] = points_ref[...]
     start = me_ref[0] * count
 
     def search(_, bounds):
@@ -307,6 +324,15 @@
     return lax.ppermute(x, axis, [(k, k ^ flip) for k in range(size)])
 
 
+def join(parts):
+    size = parts[0].shape[0]
+    total = size * len(parts)
+    lowest = jnp.array(-jnp.inf, parts[0].dtype)
+    return functools.reduce(jnp.maximum, [
+        lax.pad(part, lowest, ((k * size, total - (k + 1) * size, 0), (0, 0, 0))) for k, part in enumerate(parts)
+    ])
+
+
 def shards(points, ridge, landmark_ids):
     count, width = points.shape
     m = landmark_ids.shape[0]
@@ -321,28 +347,32 @@
     vmem = pl.BlockSpec(memory_space=pltpu.VMEM)
     table = -(-devices // B) * B
 
-    rows, low, most = pl.pallas_call(
+    rows, low, most, kept = pl.pallas_call(
         functools.partial(pack, devices),
         grid_spec=pltpu.PrefetchScalarGridSpec(
-            num_scalar_prefetch=2, grid=(), in_specs=[vmem, vmem], out_specs=[vmem, vmem, vmem],
+            num_scalar_prefetch=2, grid=(), in_specs=[vmem, vmem], out_specs=[vmem] * 4,
         ),
         out_shape=(
             jax.ShapeDtypeStruct((cap, width), points.dtype),
             jax.ShapeDtypeStruct((1, table), jnp.int32),
             jax.ShapeDtypeStruct((1, B), jnp.int32),
+            pltpu.VMEM((count, width), points.dtype),
         ),
         compiler_params=pltpu.CompilerParams(vmem_limit_bytes=16 << 20),
         name="pack",
     )(me[None], landmark_ids, landmark_ids[None, :], points)
     fits = most[0, 0] <= cap
 
+    groups = [some[at:at + 2] for some in (near, far) for at in range(0, len(some), 2)]
+    count_pieces = 2 << len(groups[-1])
+
     def packed(rows, points, ids):
-        for some in (near, far):
-            for at in range(0, len(some), 2):
-                pair = some[at:at + 2]
-                moves = pair if len(pair) == 1 else (pair[0], pair[1], pair[0] | pair[1])
-                rows = jnp.concatenate([rows, *(exchange(rows, move) for move in moves)], axis=0)
-        return rows, exchange(rows, bits[0])
+        for k, pair in enumerate(groups):
+            moves = pair if len(pair) == 1 else (pair[0], pair[1], pair[0] | pair[1])
+            parts = [rows, *(exchange(rows, move) for move in moves)]
+            if k + 1 < len(groups):
+                rows = join(parts)
+        return *parts, *(exchange(part, bits[0]) for part in parts)
 
     def summed(rows, points, ids):
         offset = ids - me * count
@@ -350,9 +380,9 @@
         picked = points[jnp.clip(offset, 0, count - 1)]
         rows = lax.psum(jnp.where(inside[:, None], picked.astype(jnp.float32), 0.0), AXES).astype(points.dtype)
         rows = jnp.pad(rows, ((0, devices * cap - m), (0, 0)))
-        return rows[:devices * cap // 2], rows[devices * cap // 2:]
-
-    own, other = lax.cond(fits, packed, summed, rows, points, landmark_ids)
+        return tuple(jnp.split(rows, count_pieces, axis=0))
+
+    pieces = lax.cond(fits, packed, summed, rows, points, landmark_ids)
     info = jnp.stack([fits.astype(jnp.int32), me])
 
     raw, stat = pl.pallas_call(
@@ -360,10 +390,11 @@
         grid_spec=pltpu.PrefetchScalarGridSpec(
             num_scalar_prefetch=2,
             grid=(),
-            in_specs=[vmem, vmem, vmem, vmem],
+            in_specs=[vmem] * (len(pieces) + 2),
             out_specs=[vmem, vmem],
             scratch_shapes=[
                 pltpu.VMEM((m, width), jnp.bfloat16),
+                pltpu.VMEM((devices * cap, width), jnp.bfloat16),
                 pltpu.VMEM((width // B, m + cap, B), jnp.float32),
                 pltpu.VMEM((8, m), jnp.float32),
                 pltpu.VMEM((m // S, m, S), jnp.float32),
@@ -372,29 +403,30 @@
                 pltpu.VMEM((4, m, S), jnp.bfloat16),
                 pltpu.VMEM((2, m, m), jnp.bfloat16),
                 pltpu.VMEM((2, S, S), jnp.bfloat16),
-                pltpu.VMEM((2, count, S), jnp.bfloat16),
+                pltpu.VMEM((4, count, S), jnp.bfloat16),
             ],
         ),
         out_shape=(pltpu.VMEM((m // S, count, S), jnp.float32), jax.ShapeDtypeStruct((2, m), jnp.float32)),
         compiler_params=pltpu.CompilerParams(vmem_limit_bytes=40 << 20),
         name="nystrom",
-    )(info, low[0], own, other, points, ridge[None, :])
+    )(info, low[0], *pieces, kept, ridge[None, :])
 
     total = count
-    for bit in bits:
-        other = exchange(stat, bit)
+    flips = [bit | near[0] if bit in near[1:2] else bit for bit in bits]
+    for flip in flips:
+        other = exchange(stat, flip)
         delta = other[0] - stat[0]
         stat = jnp.stack([0.5 * (stat[0] + other[0]), stat[1] + other[1] + jnp.square(delta) * (0.5 * total)])
         total *= 2
     gain = 1.0 / jnp.sqrt(stat[1:2] / total + 1e-05)
-    vector = pl.BlockSpec((1, m), lambda i: (0, 0))
+    steps = 8
     return pl.pallas_call(
         standardize,
-        grid=(count // 256,),
-        in_specs=[vmem, vector, vector],
-        out_specs=pl.BlockSpec((256, m), lambda i: (i, 0)),
+        in_specs=[vmem] * 3,
+        out_specs=pl.BlockSpec(memory_space=pl.ANY),
+        scratch_shapes=[pltpu.VMEM((steps, count // steps, m), jnp.bfloat16), pltpu.SemaphoreType.DMA((steps,))],
         out_shape=jax.ShapeDtypeStruct((count, m), jnp.bfloat16),
-        compiler_params=pltpu.CompilerParams(vmem_limit_bytes=16 << 20, dimension_semantics=("arbitrary",)),
+        compiler_params=pltpu.CompilerParams(vmem_limit_bytes=16 << 20),
         name="standardize",
     )(raw, stat[0:1], gain)
 

time: 86.1 us -> 83.3 us (0.967)
  local copies, waits for them, and re-layouts: 4.47 us -> 0.01 us
  waiting for transfers between devices: 19.6 us -> 24 us
  Pallas kernels: 45.7 us -> 43.9 us
  starting transfers between devices: 15.9 us -> 14.1 us
    ppermute x12 -> x15, waiting for transfers between devices: 19.6 us -> 24 us  [exchange(): return lax.ppermute(x, axis, [(k, k ^ flip) for k in range(size)])]
    cond x5 -> x0, local copies, waits for them, and re-layouts: 3.19 us -> none
    ppermute x12 -> x15, starting transfers between devices: 15.9 us -> 14.1 us  [exchange(): return lax.ppermute(x, axis, [(k, k ^ flip) for k in range(size)])]
    pallas_call x1, Pallas kernels: 3.73 us -> 2.16 us  [shards(): pl.pallas_call(standardize, in_specs=[vmem] * 3, out_specs=pl.BlockSpec(m...]
    concatenate x2 -> x0, local copies, waits for them, and re-layouts: 1.28 us -> none  [packed(): jnp.concatenate([rows, *(exchange(rows, move) for move in moves)], axis=0)]
  transfers between devices with their start and end apart: 12 -> 15, of which waited for: 11 -> 12; matrix products, arithmetic and copies ran while one was open for 4% -> 0% of each run, Pallas kernels for 0% -> 0%
where the time goes in v5:
time: 83.3 us; the launch traced here: 83.1 us
  Pallas kernels  43.9 us (53%)
  waiting for transfers between devices  24 us (29%)
  starting transfers between devices  14.1 us (17%)
  other arithmetic  0.87 us (1%)
    pallas_call x1, Pallas kernels, shards(): pl.pallas_call(functools.partial(kernel, order), grid_spec=pltpu.Prefetch...  38.9 us
    ppermute x15, waiting for transfers between devices, exchange(): return lax.ppermute(x, axis, [(k, k ^ flip) for k in range(size)])  24 us
    ppermute x15, starting transfers between devices, exchange(): return lax.ppermute(x, axis, [(k, k ^ flip) for k in range(size)])  14.1 us
    pallas_call x1, Pallas kernels, shards(): pl.pallas_call(functools.partial(pack, devices), grid_spec=pltpu.Prefetch...  2.78 us
    pallas_call x1, Pallas kernels, shards(): pl.pallas_call(standardize, in_specs=[vmem] * 3, out_specs=pl.BlockSpec(m...  2.16 us
  transfers between devices with their start and end apart: 15, of which 12 were waited for; matrix products, arithmetic and copies ran while one was open for 0% of the time, Pallas kernels for 0%

profile of v5, /device:TPU:0, one launch (start us, length us, event | category | flops | bytes accessed | tf_op | source)
XLA Modules:
  0.0 83.1 jit_solution(2810148883239958384)
XLA Ops:
  0.0 0.0 copy-start
  0.0 2.8 %pack.1 = (bf16[64,256]{1,0:T(8,128)(2,1)S(1)}, s32[1,128]{1,0:T(1,128)S(1)}, s32[1,128]{1,0:T(1,128)S(1)}, bf16[2048,256]{1,0:T(8,128)(2,1)S(1)}) custom-call(s32[1]{0:T(128)} %bitcast.me_ref, s32[1024]{0:T(1024)} %ids_ref.1, s32[1,1024]{1,0:T(1,128)} %bitcast.10, bf16[2048,256]{1,0:T(8,128)(2,1)} %points_ref.1), custom_call_target="tpu_custom_call" | custom-call | tf_op jit(solution)/shard_map/pack/pallas_call | solution.py:350
  2.8 0.1 pad_add_fusion.info_ref
  2.9 20.8 %conditional.1 = (bf16[256,256]{1,0:T(8,128)(2,1)}, bf16[256,256]{1,0:T(8,128)(2,1)}, bf16[256,256]{1,0:T(8,128)(2,1)}, bf16[256,256]{1,0:T(8,128)(2,1)}, bf16[2...) conditional(s32[]{:T(128)} %bitcast.4, (s32[]{:T(128)}, ...), branch_computations={%region_0.2_spmd, %region_2.3_spmd} | conditional | flops 796673 | bytes 5785692 | solution.py:385
  2.9 5.1 %collective-permute-start.2 = (bf16[64,256]{1,0:T(8,128)(2,1)S(1)}, bf16[64,256]{1,0:T(8,128)(2,1)S(1)}, u32[]{:S(2)}, u32[]{:S(2)}) collective-permute-start(bf16[64,256]{1,0:T(8,128)(2,1)S(1)} %param.1), channel_id=1, source_target_pairs={{0,6},{1,7},{2,4},{3,5},{4,2},{5,3},{6,0},{7,1},{8,14},{9,15},{10,... | collective-permute-start | bytes 98312 | tf_op jit(solution)/shard_map/cond/branch_1_fun/ppermute | solution.py:324
  8.0 0.0 collective-permute-start.1
  8.0 0.6 collective-permute-start
  8.7 1.3 %collective-permute-done.2 = bf16[64,256]{1,0:T(8,128)(2,1)S(1)} collective-permute-done((bf16[64,256]{1,0:T(8,128)(2,1)S(1)}, bf16[64,256]{1,0:T(8,128)(2,1)S(1)}, u32[]{:S(2)}, u32[]{:S(2)}) %collective-permute-start.2) | collective-permute-done | bytes 32800 | tf_op jit(solution)/shard_map/cond/branch_1_fun/ppermute | solution.py:324
  9.9 2.9 %collective-permute-done.1 = bf16[64,256]{1,0:T(8,128)(2,1)S(1)} collective-permute-done((bf16[64,256]{1,0:T(8,128)(2,1)S(1)}, bf16[64,256]{1,0:T(8,128)(2,1)S(1)}, u32[]{:S(2)}, u32[]{:S(2)}) %collective-permute-start.1) | collective-permute-done | bytes 32800 | tf_op jit(solution)/shard_map/cond/branch_1_fun/ppermute | solution.py:324
  12.8 0.0 collective-permute-done
  12.8 0.7 pad_maximum_fusion
  13.5 2.4 %collective-permute-start.5 = (bf16[256,256]{1,0:T(8,128)(2,1)}, bf16[256,256]{1,0:T(8,128)(2,1)}, u32[]{:S(2)}, u32[]{:S(2)}) collective-permute-start(bf16[256,256]{1,0:T(8,128)(2,1)} %pad_maximum_fusion), channel_id=1, source_target_pairs={{0,24},{8,16},{16,8},{24,0},{1,25},{9,17},{17,9},{25,1},{2,26},{10... | collective-permute-start | bytes 393224 | tf_op jit(solution)/shard_map/cond/branch_1_fun/ppermute | solution.py:324
  16.0 0.5 collective-permute-start.4
  16.5 0.5 collective-permute-start.3
  17.0 0.0 collective-permute-start.6
  17.0 4.1 %collective-permute-done.5 = bf16[256,256]{1,0:T(8,128)(2,1)} collective-permute-done((bf16[256,256]{1,0:T(8,128)(2,1)}, bf16[256,256]{1,0:T(8,128)(2,1)}, u32[]{:S(2)}, u32[]{:S(2)}) %collective-permute-start.5) | collective-permute-done | bytes 131104 | tf_op jit(solution)/shard_map/cond/branch_1_fun/ppermute | solution.py:324
  21.1 0.0 collective-permute-start.9
  21.1 0.8 collective-permute-done.4
  21.9 0.0 collective-permute-start.8
  21.9 0.0 collective-permute-done.3
  21.9 0.5 collective-permute-start.7
  22.4 0.0 collective-permute-done.6
  22.4 0.4 collective-permute-done.9
  22.8 0.8 collective-permute-done.8
  23.6 0.2 collective-permute-done.7
  23.7 0.0 copy-done
  23.7 38.9 %nystrom.1 = (f32[4,2048,256]{2,1,0:T(8,128)S(1)}, f32[2,1024]{1,0:T(2,128)S(1)}) custom-call(s32[2]{0:T(128)S(1)} %pad_add_fusion.info_ref, s32[128]{0:T(128)S(1)} %bitcast.8, bf16[256,256]{1,0:T(8,128)(2,1)} %get-tuple-element.32.refs_0_, bf16[256,256]{1,0:T(8,128)(2,1)} %get-tuple-element.33.refs_1_, bf16[256,256]{1,0:T(8,128)(2,1)} %get-tuple-element.34.refs_2_, ...), custom_call_target="tpu_custom_call" | custom-call | tf_op jit(solution)/shard_map/nystrom/pallas_call | solution.py:388
  62.7 0.4 collective-permute-start.10
  63.1 0.8 %collective-permute-done.10 = f32[2,1024]{1,0:T(2,128)S(1)} collective-permute-done((f32[2,1024]{1,0:T(2,128)S(1)}, f32[2,1024]{1,0:T(2,128)S(1)}, u32[]{:S(2)}, u32[]{:S(2)}) %collective-permute-start.10) | collective-permute-done | bytes 8224 | tf_op jit(solution)/shard_map/ppermute | solution.py:324
  64.0 0.1 collective-permute-start.11
  64.0 3.6 %collective-permute-done.11 = f32[2,1024]{1,0:T(2,128)S(1)} collective-permute-done((f32[2,1024]{1,0:T(2,128)S(1)}, f32[2,1024]{1,0:T(2,128)S(1)}, u32[]{:S(2)}, u32[]{:S(2)}) %collective-permute-start.11) | collective-permute-done | bytes 8224 | tf_op jit(solution)/shard_map/ppermute | solution.py:324
  67.7 1.5 %collective-permute-start.12 = (f32[2,1024]{1,0:T(2,128)S(1)}, f32[2,1024]{1,0:T(2,128)S(1)}, u32[]{:S(2)}, u32[]{:S(2)}) collective-permute-start(f32[2,1024]{1,0:T(2,128)S(1)} %pad_maximum_fusion.2), channel_id=1, source_target_pairs={{0,6},{1,7},{2,4},{3,5},{4,2},{5,3},{6,0},{7,1},{8,14},{9,15},{10,... | collective-permute-start | bytes 24584 | tf_op jit(solution)/shard_map/ppermute | solution.py:324
  69.3 4.0 %collective-permute-done.12 = f32[2,1024]{1,0:T(2,128)S(1)} collective-permute-done((f32[2,1024]{1,0:T(2,128)S(1)}, f32[2,1024]{1,0:T(2,128)S(1)}, u32[]{:S(2)}, u32[]{:S(2)}) %collective-permute-start.12) | collective-permute-done | bytes 8224 | tf_op jit(solution)/shard_map/ppermute | solution.py:324
  73.3 1.1 %collective-permute-start.13 = (f32[2,1024]{1,0:T(2,128)S(1)}, f32[2,1024]{1,0:T(2,128)S(1)}, u32[]{:S(2)}, u32[]{:S(2)}) collective-permute-start(f32[2,1024]{1,0:T(2,128)S(1)} %pad_maximum_fusion.3), channel_id=1, source_target_pairs={{0,8},{8,0},{16,24},{24,16},{1,9},{9,1},{17,25},{25,17},{2,10},{10... | collective-permute-start | bytes 24584 | tf_op jit(solution)/shard_map/ppermute | solution.py:324
  74.3 2.6 %collective-permute-done.13 = f32[2,1024]{1,0:T(2,128)S(1)} collective-permute-done((f32[2,1024]{1,0:T(2,128)S(1)}, f32[2,1024]{1,0:T(2,128)S(1)}, u32[]{:S(2)}, u32[]{:S(2)}) %collective-permute-start.13) | collective-permute-done | bytes 8224 | tf_op jit(solution)/shard_map/ppermute | solution.py:324
  77.0 1.3 %collective-permute-start.14 = (f32[2,1024]{1,0:T(2,128)S(1)}, f32[2,1024]{1,0:T(2,128)S(1)}, u32[]{:S(2)}, u32[]{:S(2)}) collective-permute-start(f32[2,1024]{1,0:T(2,128)S(1)} %pad_maximum_fusion.4), channel_id=1, source_target_pairs={{0,16},{8,24},{16,0},{24,8},{1,17},{9,25},{17,1},{25,9},{2,18},{10... | collective-permute-start | bytes 24584 | tf_op jit(solution)/shard_map/ppermute | solution.py:324
  78.3 2.4 %collective-permute-done.14 = f32[2,1024]{1,0:T(2,128)S(1)} collective-permute-done((f32[2,1024]{1,0:T(2,128)S(1)}, f32[2,1024]{1,0:T(2,128)S(1)}, u32[]{:S(2)}, u32[]{:S(2)}) %collective-permute-start.14) | collective-permute-done | bytes 8224 | tf_op jit(solution)/shard_map/ppermute | solution.py:324
  80.8 2.2 %standardize.1 = bf16[2048,1024]{1,0:T(8,128)(2,1)} custom-call(f32[4,2048,256]{2,1,0:T(8,128)S(1)} %get-tuple-element.41.x_ref, f32[1,1024]{1,0:T(1,128)S(1)} %get-tuple-element.50.shift_ref, f32[1,1024]{1,0:T(1,128)S(1)} %get-tuple-element.49.gain_ref), custom_call_target="tpu_custom_call" | custom-call | tf_op jit(solution)/shard_map/standardize/pallas_call | solution.py:423
  (9 shorter events, 0.1 us)
Async XLA Ops:
  0.0 23.7 %copy-start = (f32[1024]{0:T(1024)S(1)}, f32[1024]{0:T(1024)}, u32[]{:S(2)}) copy-start(f32[1024]{0:T(1024)} %param.6) | copy-start | bytes 12292
  2.9 7.0 %collective-permute-start.2 = (bf16[64,256]{1,0:T(8,128)(2,1)S(1)}, bf16[64,256]{1,0:T(8,128)(2,1)S(1)}, u32[]{:S(2)}, u32[]{:S(2)}) collective-permute-start(bf16[64,256]{1,0:T(8,128)(2,1)S(1)} %param.1), channel_id=1, source_target_pairs={{0,6},{1,7},{2,4},{3,5},{4,2},{5,3},{6,0},{7,1},{8,14},{9,15},{10,... | collective-permute-start | bytes 98312 | tf_op jit(solution)/shard_map/cond/branch_1_fun/ppermute | solution.py:324
  8.0 4.8 %collective-permute-start.1 = (bf16[64,256]{1,0:T(8,128)(2,1)S(1)}, bf16[64,256]{1,0:T(8,128)(2,1)S(1)}, u32[]{:S(2)}, u32[]{:S(2)}) collective-permute-start(bf16[64,256]{1,0:T(8,128)(2,1)S(1)} %param.1), channel_id=1, source_target_pairs={{0,4},{1,5},{2,6},{3,7},{4,0},{5,1},{6,2},{7,3},{8,12},{9,13},{10,... | collective-permute-start | bytes 98312 | tf_op jit(solution)/shard_map/cond/branch_1_fun/ppermute | solution.py:324
  8.0 4.8 %collective-permute-start = (bf16[64,256]{1,0:T(8,128)(2,1)S(1)}, bf16[64,256]{1,0:T(8,128)(2,1)S(1)}, u32[]{:S(2)}, u32[]{:S(2)}) collective-permute-start(bf16[64,256]{1,0:T(8,128)(2,1)S(1)} %param.1), channel_id=1, source_target_pairs={{0,2},{1,3},{2,0},{3,1},{4,6},{5,7},{6,4},{7,5},{8,10},{9,11},{10,... | collective-permute-start | bytes 98312 | tf_op jit(solution)/shard_map/cond/branch_1_fun/ppermute | solution.py:324
  13.5 7.6 %collective-permute-start.5 = (bf16[256,256]{1,0:T(8,128)(2,1)}, bf16[256,256]{1,0:T(8,128)(2,1)}, u32[]{:S(2)}, u32[]{:S(2)}) collective-permute-start(bf16[256,256]{1,0:T(8,128)(2,1)} %pad_maximum_fusion), channel_id=1, source_target_pairs={{0,24},{8,16},{16,8},{24,0},{1,25},{9,17},{17,9},{25,1},{2,26},{10... | collective-permute-start | bytes 393224 | tf_op jit(solution)/shard_map/cond/branch_1_fun/ppermute | solution.py:324
  16.0 5.9 %collective-permute-start.4 = (bf16[256,256]{1,0:T(8,128)(2,1)}, bf16[256,256]{1,0:T(8,128)(2,1)}, u32[]{:S(2)}, u32[]{:S(2)}) collective-permute-start(bf16[256,256]{1,0:T(8,128)(2,1)} %pad_maximum_fusion), channel_id=1, source_target_pairs={{0,16},{8,24},{16,0},{24,8},{1,17},{9,25},{17,1},{25,9},{2,18},{10... | collective-permute-start | bytes 393224 | tf_op jit(solution)/shard_map/cond/branch_1_fun/ppermute | solution.py:324
  16.5 5.4 %collective-permute-start.3 = (bf16[256,256]{1,0:T(8,128)(2,1)}, bf16[256,256]{1,0:T(8,128)(2,1)}, u32[]{:S(2)}, u32[]{:S(2)}) collective-permute-start(bf16[256,256]{1,0:T(8,128)(2,1)} %pad_maximum_fusion), channel_id=1, source_target_pairs={{0,8},{8,0},{16,24},{24,16},{1,9},{9,1},{17,25},{25,17},{2,10},{10... | collective-permute-start | bytes 393224 | tf_op jit(solution)/shard_map/cond/branch_1_fun/ppermute | solution.py:324
  17.0 5.4 %collective-permute-start.6 = (bf16[256,256]{1,0:T(8,128)(2,1)}, bf16[256,256]{1,0:T(8,128)(2,1)}, u32[]{:S(2)}, u32[]{:S(2)}) collective-permute-start(bf16[256,256]{1,0:T(8,128)(2,1)} %pad_maximum_fusion), channel_id=1, source_target_pairs={{0,1},{1,0},{2,3},{3,2},{4,5},{5,4},{6,7},{7,6},{8,9},{9,8},{10,11... | collective-permute-start | bytes 393224 | tf_op jit(solution)/shard_map/cond/branch_1_fun/ppermute | solution.py:324
  21.1 1.7 %collective-permute-start.9 = (bf16[256,256]{1,0:T(8,128)(2,1)}, bf16[256,256]{1,0:T(8,128)(2,1)}, u32[]{:S(2)}, u32[]{:S(2)}) collective-permute-start(bf16[256,256]{1,0:T(8,128)(2,1)} %collective-permute-done.5), channel_id=1, source_target_pairs={{0,1},{1,0},{2,3},{3,2},{4,5},{5,4},{6,7},{7,6},{8,9},{9,8},{10,11... | collective-permute-start | bytes 393224 | tf_op jit(solution)/shard_map/cond/branch_1_fun/ppermute | solution.py:324
  21.9 1.7 %collective-permute-start.8 = (bf16[256,256]{1,0:T(8,128)(2,1)}, bf16[256,256]{1,0:T(8,128)(2,1)}, u32[]{:S(2)}, u32[]{:S(2)}) collective-permute-start(bf16[256,256]{1,0:T(8,128)(2,1)} %collective-permute-done.4), channel_id=1, source_target_pairs={{0,1},{1,0},{2,3},{3,2},{4,5},{5,4},{6,7},{7,6},{8,9},{9,8},{10,11... | collective-permute-start | bytes 393224 | tf_op jit(solution)/shard_map/cond/branch_1_fun/ppermute | solution.py:324
  21.9 1.9 %collective-permute-start.7 = (bf16[256,256]{1,0:T(8,128)(2,1)}, bf16[256,256]{1,0:T(8,128)(2,1)}, u32[]{:S(2)}, u32[]{:S(2)}) collective-permute-start(bf16[256,256]{1,0:T(8,128)(2,1)} %collective-permute-done.3), channel_id=1, source_target_pairs={{0,1},{1,0},{2,3},{3,2},{4,5},{5,4},{6,7},{7,6},{8,9},{9,8},{10,11... | collective-permute-start | bytes 393224 | tf_op jit(solution)/shard_map/cond/branch_1_fun/ppermute | solution.py:324
  62.7 1.2 %collective-permute-start.10 = (f32[2,1024]{1,0:T(2,128)S(1)}, f32[2,1024]{1,0:T(2,128)S(1)}, u32[]{:S(2)}, u32[]{:S(2)}) collective-permute-start(f32[2,1024]{1,0:T(2,128)S(1)} %get-tuple-element.42), channel_id=1, source_target_pairs={{0,1},{1,0},{2,3},{3,2},{4,5},{5,4},{6,7},{7,6},{8,9},{9,8},{10,11... | collective-permute-start | bytes 24584 | tf_op jit(solution)/shard_map/ppermute | solution.py:324
  64.0 3.7 %collective-permute-start.11 = (f32[2,1024]{1,0:T(2,128)S(1)}, f32[2,1024]{1,0:T(2,128)S(1)}, u32[]{:S(2)}, u32[]{:S(2)}) collective-permute-start(f32[2,1024]{1,0:T(2,128)S(1)} %pad_maximum_fusion.1), channel_id=1, source_target_pairs={{0,2},{1,3},{2,0},{3,1},{4,6},{5,7},{6,4},{7,5},{8,10},{9,11},{10,... | collective-permute-start | bytes 24584 | tf_op jit(solution)/shard_map/ppermute | solution.py:324
  67.7 5.5 %collective-permute-start.12 = (f32[2,1024]{1,0:T(2,128)S(1)}, f32[2,1024]{1,0:T(2,128)S(1)}, u32[]{:S(2)}, u32[]{:S(2)}) collective-permute-start(f32[2,1024]{1,0:T(2,128)S(1)} %pad_maximum_fusion.2), channel_id=1, source_target_pairs={{0,6},{1,7},{2,4},{3,5},{4,2},{5,3},{6,0},{7,1},{8,14},{9,15},{10,... | collective-permute-start | bytes 24584 | tf_op jit(solution)/shard_map/ppermute | solution.py:324
  73.3 3.7 %collective-permute-start.13 = (f32[2,1024]{1,0:T(2,128)S(1)}, f32[2,1024]{1,0:T(2,128)S(1)}, u32[]{:S(2)}, u32[]{:S(2)}) collective-permute-start(f32[2,1024]{1,0:T(2,128)S(1)} %pad_maximum_fusion.3), channel_id=1, source_target_pairs={{0,8},{8,0},{16,24},{24,16},{1,9},{9,1},{17,25},{25,17},{2,10},{10... | collective-permute-start | bytes 24584 | tf_op jit(solution)/shard_map/ppermute | solution.py:324
  77.0 3.7 %collective-permute-start.14 = (f32[2,1024]{1,0:T(2,128)S(1)}, f32[2,1024]{1,0:T(2,128)S(1)}, u32[]{:S(2)}, u32[]{:S(2)}) collective-permute-start(f32[2,1024]{1,0:T(2,128)S(1)} %pad_maximum_fusion.4), channel_id=1, source_target_pairs={{0,16},{8,24},{16,0},{24,8},{1,17},{9,25},{17,1},{25,9},{2,18},{10... | collective-permute-start | bytes 24584 | tf_op jit(solution)/shard_map/ppermute | solution.py:324

commit v6 on v5

--- a/solution.py
+++ b/solution.py
@@ -11,6 +11,7 @@
 AXES = ("grp", "dev")
 B = 128
 S = 256
+HEAD, FAR = 5, 7
 ROWS = 512
 
 
@@ -48,7 +49,9 @@
         return jnp.broadcast_to(c_ref[at:at + 1, :], (8, B))
 
     ahead = [column(0, b) for b in range(8)]
+    done = []
     for k in range(n):
+        stop = FAR if k < HEAD else n
         first = 8 * k
         base = (k % 2) * 128
         follow = k + 1 < n
@@ -59,7 +62,7 @@
             z = [column(k + 1, first + j) for j in range(8)]
             ahead = [column(k + 1, first + 8 + b) for b in range(8)]
             acc = rows[k + 1]
-        below = {t: [column(t, first + j) for j in range(8)] for t in range(k + 2, n)}
+        below = {t: [column(t, first + j) for j in range(7, -1, -1)][::-1] for t in range(k + 2, stop)}
         pivot = (lane >= first) & (lane < first + 8)
         start = jnp.where(pivot, (lane - first == sub).astype(jnp.float32), rows[k])
         y = [jnp.broadcast_to(start[i:i + 1, :], (8, B)) for i in range(8)]
@@ -90,20 +93,30 @@
         for i in range(7):
             w = jnp.where(sub == i, y[i], w)
         d_ref[first:first + 8, :] = jnp.where(lane < first + 8, w, 0.0)
+        done.append(w)
         if follow:
             rows[k + 1] = acc
         if k + 2 < n:
             q = [None] * 8
             for j in range(7, -1, -1):
                 v = y[j]
-                for i in range(j + 1, 8):
+                for i in range(7, j, -1):
                     v = v - s[(j, i)] * q[i]
                 q[j] = v * inv[j]
-            for t in range(k + 2, n):
+            for t in range(k + 2, stop):
                 v = jnp.where(pivot, 0.0, rows[t])
-                for j in range(8):
+                for j in range(7, -1, -1):
                     v = v - below[t][j] * q[j]
                 rows[t] = v
+        if k == HEAD - 1:
+            left = split(jnp.concatenate(done, axis=0))
+            kept = [jnp.where((lane < 8 * i + 8) | (lane >= 8 * HEAD), u, 0.0) for i, u in enumerate(done)]
+            right = split(jnp.concatenate(kept, axis=0))
+            left = jnp.concatenate([left[0], left[1], left[0]], axis=0)
+            right = jnp.concatenate([right[0], right[0], right[1]], axis=0)
+            part = dot(left, right, ((0,), (0,)))
+            for t in range(FAR, n):
+                rows[t] = jnp.where(lane < 8 * HEAD, 0.0, rows[t]) - part[8 * t:8 * t + 8]
         yield k
 
 
@@ -119,7 +132,7 @@
 
 def kernel(order, info_ref, low_ref, *refs):
     (*piece_refs, points_ref, ridge_ref, x_ref, stat_ref, marks_ref, rows_ref, packed_ref, along_ref, a_ref, d_ref,
-     c_ref, l_ref, lt_ref, wt_ref, r_ref) = refs
+     c_ref, l_ref, lt_ref, wt_ref, r_ref, norm_ref) = refs
     m, width = marks_ref.shape
     count = points_ref.shape[0]
     scale = 1.0 / (2.0 * width)
@@ -167,9 +180,10 @@
         here = slice(j * S, (j + 1) * S)
         rows = pl.ds(at, ROWS)
         points = points_ref[rows, :]
-        _, down = square_sums(points)
+        if j == 0:
+            norm_ref[rows, :] = square_sums(points)[1]
         inner = dot_nt(points, marks_ref[here, :])
-        x_ref[j, rows, :] = jnp.exp(-(wide(down) + along_ref[0:1, here] - 2.0 * inner) * scale)
+        x_ref[j, rows, :] = jnp.exp(-(wide(norm_ref[rows, :]) + along_ref[0:1, here] - 2.0 * inner) * scale)
 
     def raw_piece(p, at):
         here = slice(p * S, (p + 1) * S)
@@ -404,6 +418,7 @@
                 pltpu.VMEM((2, m, m), jnp.bfloat16),
                 pltpu.VMEM((2, S, S), jnp.bfloat16),
                 pltpu.VMEM((4, count, S), jnp.bfloat16),
+                pltpu.VMEM((count, B), jnp.float32),
             ],
         ),
         out_shape=(pltpu.VMEM((m // S, count, S), jnp.float32), jax.ShapeDtypeStruct((2, m), jnp.float32)),

time: 83.3 us -> 80.4 us (0.965)
  Pallas kernels: 43.9 us -> 40.9 us
    pallas_call x1, Pallas kernels: 38.9 us -> 36 us  [shards(): pl.pallas_call(functools.partial(kernel, order), grid_spec=pltpu.Prefetch...]
where the time goes in v6:
time: 80.4 us; the launch traced here: 80.2 us
  Pallas kernels  40.9 us (51%)
  waiting for transfers between devices  24 us (30%)
  starting transfers between devices  14.1 us (18%)
  other arithmetic  0.87 us (1%)
    pallas_call x1, Pallas kernels, shards(): pl.pallas_call(functools.partial(kernel, order), grid_spec=pltpu.Prefetch...  36 us
    ppermute x15, waiting for transfers between devices, exchange(): return lax.ppermute(x, axis, [(k, k ^ flip) for k in range(size)])  24 us
    ppermute x15, starting transfers between devices, exchange(): return lax.ppermute(x, axis, [(k, k ^ flip) for k in range(size)])  14.1 us
    pallas_call x1, Pallas kernels, shards(): pl.pallas_call(functools.partial(pack, devices), grid_spec=pltpu.Prefetch...  2.78 us
    pallas_call x1, Pallas kernels, shards(): pl.pallas_call(standardize, in_specs=[vmem] * 3, out_specs=pl.BlockSpec(m...  2.16 us
  transfers between devices with their start and end apart: 15, of which 12 were waited for; matrix products, arithmetic and copies ran while one was open for 0% of the time, Pallas kernels for 0%

profile of v6, /device:TPU:0, one launch (start us, length us, event | category | flops | bytes accessed | tf_op | source)
XLA Modules:
  0.0 80.2 jit_solution(7351149004947315991)
XLA Ops:
  0.0 0.0 copy-start
  0.0 2.8 %pack.1 = (bf16[64,256]{1,0:T(8,128)(2,1)S(1)}, s32[1,128]{1,0:T(1,128)S(1)}, s32[1,128]{1,0:T(1,128)S(1)}, bf16[2048,256]{1,0:T(8,128)(2,1)S(1)}) custom-call(s32[1]{0:T(128)} %bitcast.me_ref, s32[1024]{0:T(1024)} %ids_ref.1, s32[1,1024]{1,0:T(1,128)} %bitcast.10, bf16[2048,256]{1,0:T(8,128)(2,1)} %points_ref.1), custom_call_target="tpu_custom_call" | custom-call | tf_op jit(solution)/shard_map/pack/pallas_call | solution.py:364
  2.8 0.1 pad_add_fusion.info_ref
  2.9 20.8 %conditional.1 = (bf16[256,256]{1,0:T(8,128)(2,1)}, bf16[256,256]{1,0:T(8,128)(2,1)}, bf16[256,256]{1,0:T(8,128)(2,1)}, bf16[256,256]{1,0:T(8,128)(2,1)}, bf16[2...) conditional(s32[]{:T(128)} %bitcast.4, (s32[]{:T(128)}, ...), branch_computations={%region_0.2_spmd, %region_2.3_spmd} | conditional | flops 796673 | bytes 5785692 | solution.py:399
  2.9 5.1 %collective-permute-start.2 = (bf16[64,256]{1,0:T(8,128)(2,1)S(1)}, bf16[64,256]{1,0:T(8,128)(2,1)S(1)}, u32[]{:S(2)}, u32[]{:S(2)}) collective-permute-start(bf16[64,256]{1,0:T(8,128)(2,1)S(1)} %param.1), channel_id=1, source_target_pairs={{0,6},{1,7},{2,4},{3,5},{4,2},{5,3},{6,0},{7,1},{8,14},{9,15},{10,... | collective-permute-start | bytes 98312 | tf_op jit(solution)/shard_map/cond/branch_1_fun/ppermute | solution.py:338
  8.0 0.0 collective-permute-start.1
  8.0 0.6 collective-permute-start
  8.7 1.3 %collective-permute-done.2 = bf16[64,256]{1,0:T(8,128)(2,1)S(1)} collective-permute-done((bf16[64,256]{1,0:T(8,128)(2,1)S(1)}, bf16[64,256]{1,0:T(8,128)(2,1)S(1)}, u32[]{:S(2)}, u32[]{:S(2)}) %collective-permute-start.2) | collective-permute-done | bytes 32800 | tf_op jit(solution)/shard_map/cond/branch_1_fun/ppermute | solution.py:338
  9.9 2.9 %collective-permute-done.1 = bf16[64,256]{1,0:T(8,128)(2,1)S(1)} collective-permute-done((bf16[64,256]{1,0:T(8,128)(2,1)S(1)}, bf16[64,256]{1,0:T(8,128)(2,1)S(1)}, u32[]{:S(2)}, u32[]{:S(2)}) %collective-permute-start.1) | collective-permute-done | bytes 32800 | tf_op jit(solution)/shard_map/cond/branch_1_fun/ppermute | solution.py:338
  12.8 0.0 collective-permute-done
  12.8 0.7 pad_maximum_fusion
  13.5 2.4 %collective-permute-start.5 = (bf16[256,256]{1,0:T(8,128)(2,1)}, bf16[256,256]{1,0:T(8,128)(2,1)}, u32[]{:S(2)}, u32[]{:S(2)}) collective-permute-start(bf16[256,256]{1,0:T(8,128)(2,1)} %pad_maximum_fusion), channel_id=1, source_target_pairs={{0,24},{8,16},{16,8},{24,0},{1,25},{9,17},{17,9},{25,1},{2,26},{10... | collective-permute-start | bytes 393224 | tf_op jit(solution)/shard_map/cond/branch_1_fun/ppermute | solution.py:338
  16.0 0.5 collective-permute-start.4
  16.5 0.5 collective-permute-start.3
  17.0 0.0 collective-permute-start.6
  17.0 4.1 %collective-permute-done.5 = bf16[256,256]{1,0:T(8,128)(2,1)} collective-permute-done((bf16[256,256]{1,0:T(8,128)(2,1)}, bf16[256,256]{1,0:T(8,128)(2,1)}, u32[]{:S(2)}, u32[]{:S(2)}) %collective-permute-start.5) | collective-permute-done | bytes 131104 | tf_op jit(solution)/shard_map/cond/branch_1_fun/ppermute | solution.py:338
  21.1 0.0 collective-permute-start.9
  21.1 0.8 collective-permute-done.4
  21.9 0.0 collective-permute-start.8
  21.9 0.0 collective-permute-done.3
  21.9 0.5 collective-permute-start.7
  22.4 0.0 collective-permute-done.6
  22.4 0.4 collective-permute-done.9
  22.8 0.8 collective-permute-done.8
  23.6 0.2 collective-permute-done.7
  23.7 0.0 copy-done
  23.7 36.0 %nystrom.1 = (f32[4,2048,256]{2,1,0:T(8,128)S(1)}, f32[2,1024]{1,0:T(2,128)S(1)}) custom-call(s32[2]{0:T(128)S(1)} %pad_add_fusion.info_ref, s32[128]{0:T(128)S(1)} %bitcast.8, bf16[256,256]{1,0:T(8,128)(2,1)} %get-tuple-element.32.refs_0_, bf16[256,256]{1,0:T(8,128)(2,1)} %get-tuple-element.33.refs_1_, bf16[256,256]{1,0:T(8,128)(2,1)} %get-tuple-element.34.refs_2_, ...), custom_call_target="tpu_custom_call" | custom-call | tf_op jit(solution)/shard_map/nystrom/pallas_call | solution.py:402
  59.7 0.4 collective-permute-start.10
  60.1 0.9 %collective-permute-done.10 = f32[2,1024]{1,0:T(2,128)S(1)} collective-permute-done((f32[2,1024]{1,0:T(2,128)S(1)}, f32[2,1024]{1,0:T(2,128)S(1)}, u32[]{:S(2)}, u32[]{:S(2)}) %collective-permute-start.10) | collective-permute-done | bytes 8224 | tf_op jit(solution)/shard_map/ppermute | solution.py:338
  61.0 0.1 collective-permute-start.11
  61.1 3.6 %collective-permute-done.11 = f32[2,1024]{1,0:T(2,128)S(1)} collective-permute-done((f32[2,1024]{1,0:T(2,128)S(1)}, f32[2,1024]{1,0:T(2,128)S(1)}, u32[]{:S(2)}, u32[]{:S(2)}) %collective-permute-start.11) | collective-permute-done | bytes 8224 | tf_op jit(solution)/shard_map/ppermute | solution.py:338
  64.8 1.5 %collective-permute-start.12 = (f32[2,1024]{1,0:T(2,128)S(1)}, f32[2,1024]{1,0:T(2,128)S(1)}, u32[]{:S(2)}, u32[]{:S(2)}) collective-permute-start(f32[2,1024]{1,0:T(2,128)S(1)} %pad_maximum_fusion.2), channel_id=1, source_target_pairs={{0,6},{1,7},{2,4},{3,5},{4,2},{5,3},{6,0},{7,1},{8,14},{9,15},{10,... | collective-permute-start | bytes 24584 | tf_op jit(solution)/shard_map/ppermute | solution.py:338
  66.3 4.0 %collective-permute-done.12 = f32[2,1024]{1,0:T(2,128)S(1)} collective-permute-done((f32[2,1024]{1,0:T(2,128)S(1)}, f32[2,1024]{1,0:T(2,128)S(1)}, u32[]{:S(2)}, u32[]{:S(2)}) %collective-permute-start.12) | collective-permute-done | bytes 8224 | tf_op jit(solution)/shard_map/ppermute | solution.py:338
  70.3 1.1 %collective-permute-start.13 = (f32[2,1024]{1,0:T(2,128)S(1)}, f32[2,1024]{1,0:T(2,128)S(1)}, u32[]{:S(2)}, u32[]{:S(2)}) collective-permute-start(f32[2,1024]{1,0:T(2,128)S(1)} %pad_maximum_fusion.3), channel_id=1, source_target_pairs={{0,8},{8,0},{16,24},{24,16},{1,9},{9,1},{17,25},{25,17},{2,10},{10... | collective-permute-start | bytes 24584 | tf_op jit(solution)/shard_map/ppermute | solution.py:338
  71.4 2.6 %collective-permute-done.13 = f32[2,1024]{1,0:T(2,128)S(1)} collective-permute-done((f32[2,1024]{1,0:T(2,128)S(1)}, f32[2,1024]{1,0:T(2,128)S(1)}, u32[]{:S(2)}, u32[]{:S(2)}) %collective-permute-start.13) | collective-permute-done | bytes 8224 | tf_op jit(solution)/shard_map/ppermute | solution.py:338
  74.1 1.3 %collective-permute-start.14 = (f32[2,1024]{1,0:T(2,128)S(1)}, f32[2,1024]{1,0:T(2,128)S(1)}, u32[]{:S(2)}, u32[]{:S(2)}) collective-permute-start(f32[2,1024]{1,0:T(2,128)S(1)} %pad_maximum_fusion.4), channel_id=1, source_target_pairs={{0,16},{8,24},{16,0},{24,8},{1,17},{9,25},{17,1},{25,9},{2,18},{10... | collective-permute-start | bytes 24584 | tf_op jit(solution)/shard_map/ppermute | solution.py:338
  75.3 2.5 %collective-permute-done.14 = f32[2,1024]{1,0:T(2,128)S(1)} collective-permute-done((f32[2,1024]{1,0:T(2,128)S(1)}, f32[2,1024]{1,0:T(2,128)S(1)}, u32[]{:S(2)}, u32[]{:S(2)}) %collective-permute-start.14) | collective-permute-done | bytes 8224 | tf_op jit(solution)/shard_map/ppermute | solution.py:338
  77.8 2.2 %standardize.1 = bf16[2048,1024]{1,0:T(8,128)(2,1)} custom-call(f32[4,2048,256]{2,1,0:T(8,128)S(1)} %get-tuple-element.41.x_ref, f32[1,1024]{1,0:T(1,128)S(1)} %get-tuple-element.50.shift_ref, f32[1,1024]{1,0:T(1,128)S(1)} %get-tuple-element.49.gain_ref), custom_call_target="tpu_custom_call" | custom-call | tf_op jit(solution)/shard_map/standardize/pallas_call | solution.py:438
  (9 shorter events, 0.1 us)
Async XLA Ops:
  0.0 23.7 %copy-start = (f32[1024]{0:T(1024)S(1)}, f32[1024]{0:T(1024)}, u32[]{:S(2)}) copy-start(f32[1024]{0:T(1024)} %param.6) | copy-start | bytes 12292
  2.9 7.0 %collective-permute-start.2 = (bf16[64,256]{1,0:T(8,128)(2,1)S(1)}, bf16[64,256]{1,0:T(8,128)(2,1)S(1)}, u32[]{:S(2)}, u32[]{:S(2)}) collective-permute-start(bf16[64,256]{1,0:T(8,128)(2,1)S(1)} %param.1), channel_id=1, source_target_pairs={{0,6},{1,7},{2,4},{3,5},{4,2},{5,3},{6,0},{7,1},{8,14},{9,15},{10,... | collective-permute-start | bytes 98312 | tf_op jit(solution)/shard_map/cond/branch_1_fun/ppermute | solution.py:338
  8.0 4.8 %collective-permute-start.1 = (bf16[64,256]{1,0:T(8,128)(2,1)S(1)}, bf16[64,256]{1,0:T(8,128)(2,1)S(1)}, u32[]{:S(2)}, u32[]{:S(2)}) collective-permute-start(bf16[64,256]{1,0:T(8,128)(2,1)S(1)} %param.1), channel_id=1, source_target_pairs={{0,4},{1,5},{2,6},{3,7},{4,0},{5,1},{6,2},{7,3},{8,12},{9,13},{10,... | collective-permute-start | bytes 98312 | tf_op jit(solution)/shard_map/cond/branch_1_fun/ppermute | solution.py:338
  8.0 4.8 %collective-permute-start = (bf16[64,256]{1,0:T(8,128)(2,1)S(1)}, bf16[64,256]{1,0:T(8,128)(2,1)S(1)}, u32[]{:S(2)}, u32[]{:S(2)}) collective-permute-start(bf16[64,256]{1,0:T(8,128)(2,1)S(1)} %param.1), channel_id=1, source_target_pairs={{0,2},{1,3},{2,0},{3,1},{4,6},{5,7},{6,4},{7,5},{8,10},{9,11},{10,... | collective-permute-start | bytes 98312 | tf_op jit(solution)/shard_map/cond/branch_1_fun/ppermute | solution.py:338
  13.5 7.6 %collective-permute-start.5 = (bf16[256,256]{1,0:T(8,128)(2,1)}, bf16[256,256]{1,0:T(8,128)(2,1)}, u32[]{:S(2)}, u32[]{:S(2)}) collective-permute-start(bf16[256,256]{1,0:T(8,128)(2,1)} %pad_maximum_fusion), channel_id=1, source_target_pairs={{0,24},{8,16},{16,8},{24,0},{1,25},{9,17},{17,9},{25,1},{2,26},{10... | collective-permute-start | bytes 393224 | tf_op jit(solution)/shard_map/cond/branch_1_fun/ppermute | solution.py:338
  16.0 5.9 %collective-permute-start.4 = (bf16[256,256]{1,0:T(8,128)(2,1)}, bf16[256,256]{1,0:T(8,128)(2,1)}, u32[]{:S(2)}, u32[]{:S(2)}) collective-permute-start(bf16[256,256]{1,0:T(8,128)(2,1)} %pad_maximum_fusion), channel_id=1, source_target_pairs={{0,16},{8,24},{16,0},{24,8},{1,17},{9,25},{17,1},{25,9},{2,18},{10... | collective-permute-start | bytes 393224 | tf_op jit(solution)/shard_map/cond/branch_1_fun/ppermute | solution.py:338
  16.5 5.4 %collective-permute-start.3 = (bf16[256,256]{1,0:T(8,128)(2,1)}, bf16[256,256]{1,0:T(8,128)(2,1)}, u32[]{:S(2)}, u32[]{:S(2)}) collective-permute-start(bf16[256,256]{1,0:T(8,128)(2,1)} %pad_maximum_fusion), channel_id=1, source_target_pairs={{0,8},{8,0},{16,24},{24,16},{1,9},{9,1},{17,25},{25,17},{2,10},{10... | collective-permute-start | bytes 393224 | tf_op jit(solution)/shard_map/cond/branch_1_fun/ppermute | solution.py:338
  17.0 5.4 %collective-permute-start.6 = (bf16[256,256]{1,0:T(8,128)(2,1)}, bf16[256,256]{1,0:T(8,128)(2,1)}, u32[]{:S(2)}, u32[]{:S(2)}) collective-permute-start(bf16[256,256]{1,0:T(8,128)(2,1)} %pad_maximum_fusion), channel_id=1, source_target_pairs={{0,1},{1,0},{2,3},{3,2},{4,5},{5,4},{6,7},{7,6},{8,9},{9,8},{10,11... | collective-permute-start | bytes 393224 | tf_op jit(solution)/shard_map/cond/branch_1_fun/ppermute | solution.py:338
  21.1 1.7 %collective-permute-start.9 = (bf16[256,256]{1,0:T(8,128)(2,1)}, bf16[256,256]{1,0:T(8,128)(2,1)}, u32[]{:S(2)}, u32[]{:S(2)}) collective-permute-start(bf16[256,256]{1,0:T(8,128)(2,1)} %collective-permute-done.5), channel_id=1, source_target_pairs={{0,1},{1,0},{2,3},{3,2},{4,5},{5,4},{6,7},{7,6},{8,9},{9,8},{10,11... | collective-permute-start | bytes 393224 | tf_op jit(solution)/shard_map/cond/branch_1_fun/ppermute | solution.py:338
  21.9 1.7 %collective-permute-start.8 = (bf16[256,256]{1,0:T(8,128)(2,1)}, bf16[256,256]{1,0:T(8,128)(2,1)}, u32[]{:S(2)}, u32[]{:S(2)}) collective-permute-start(bf16[256,256]{1,0:T(8,128)(2,1)} %collective-permute-done.4), channel_id=1, source_target_pairs={{0,1},{1,0},{2,3},{3,2},{4,5},{5,4},{6,7},{7,6},{8,9},{9,8},{10,11... | collective-permute-start | bytes 393224 | tf_op jit(solution)/shard_map/cond/branch_1_fun/ppermute | solution.py:338
  21.9 1.9 %collective-permute-start.7 = (bf16[256,256]{1,0:T(8,128)(2,1)}, bf16[256,256]{1,0:T(8,128)(2,1)}, u32[]{:S(2)}, u32[]{:S(2)}) collective-permute-start(bf16[256,256]{1,0:T(8,128)(2,1)} %collective-permute-done.3), channel_id=1, source_target_pairs={{0,1},{1,0},{2,3},{3,2},{4,5},{5,4},{6,7},{7,6},{8,9},{9,8},{10,11... | collective-permute-start | bytes 393224 | tf_op jit(solution)/shard_map/cond/branch_1_fun/ppermute | solution.py:338
  59.7 1.2 %collective-permute-start.10 = (f32[2,1024]{1,0:T(2,128)S(1)}, f32[2,1024]{1,0:T(2,128)S(1)}, u32[]{:S(2)}, u32[]{:S(2)}) collective-permute-start(f32[2,1024]{1,0:T(2,128)S(1)} %get-tuple-element.42), channel_id=1, source_target_pairs={{0,1},{1,0},{2,3},{3,2},{4,5},{5,4},{6,7},{7,6},{8,9},{9,8},{10,11... | collective-permute-start | bytes 24584 | tf_op jit(solution)/shard_map/ppermute | solution.py:338
  61.0 3.7 %collective-permute-start.11 = (f32[2,1024]{1,0:T(2,128)S(1)}, f32[2,1024]{1,0:T(2,128)S(1)}, u32[]{:S(2)}, u32[]{:S(2)}) collective-permute-start(f32[2,1024]{1,0:T(2,128)S(1)} %pad_maximum_fusion.1), channel_id=1, source_target_pairs={{0,2},{1,3},{2,0},{3,1},{4,6},{5,7},{6,4},{7,5},{8,10},{9,11},{10,... | collective-permute-start | bytes 24584 | tf_op jit(solution)/shard_map/ppermute | solution.py:338
  64.8 5.5 %collective-permute-start.12 = (f32[2,1024]{1,0:T(2,128)S(1)}, f32[2,1024]{1,0:T(2,128)S(1)}, u32[]{:S(2)}, u32[]{:S(2)}) collective-permute-start(f32[2,1024]{1,0:T(2,128)S(1)} %pad_maximum_fusion.2), channel_id=1, source_target_pairs={{0,6},{1,7},{2,4},{3,5},{4,2},{5,3},{6,0},{7,1},{8,14},{9,15},{10,... | collective-permute-start | bytes 24584 | tf_op jit(solution)/shard_map/ppermute | solution.py:338
  70.3 3.7 %collective-permute-start.13 = (f32[2,1024]{1,0:T(2,128)S(1)}, f32[2,1024]{1,0:T(2,128)S(1)}, u32[]{:S(2)}, u32[]{:S(2)}) collective-permute-start(f32[2,1024]{1,0:T(2,128)S(1)} %pad_maximum_fusion.3), channel_id=1, source_target_pairs={{0,8},{8,0},{16,24},{24,16},{1,9},{9,1},{17,25},{25,17},{2,10},{10... | collective-permute-start | bytes 24584 | tf_op jit(solution)/shard_map/ppermute | solution.py:338
  74.1 3.7 %collective-permute-start.14 = (f32[2,1024]{1,0:T(2,128)S(1)}, f32[2,1024]{1,0:T(2,128)S(1)}, u32[]{:S(2)}, u32[]{:S(2)}) collective-permute-start(f32[2,1024]{1,0:T(2,128)S(1)} %pad_maximum_fusion.4), channel_id=1, source_target_pairs={{0,16},{8,24},{16,0},{24,8},{1,17},{9,25},{17,1},{25,9},{2,18},{10... | collective-permute-start | bytes 24584 | tf_op jit(solution)/shard_map/ppermute | solution.py:338

commit v7 on v6

--- a/solution.py
+++ b/solution.py
@@ -427,9 +427,8 @@
     )(info, low[0], *pieces, kept, ridge[None, :])
 
     total = count
-    flips = [bit | near[0] if bit in near[1:2] else bit for bit in bits]
-    for flip in flips:
-        other = exchange(stat, flip)
+    for bit in bits:
+        other = exchange(stat, bit)
         delta = other[0] - stat[0]
         stat = jnp.stack([0.5 * (stat[0] + other[0]), stat[1] + other[1] + jnp.square(delta) * (0.5 * total)])
         total *= 2

time: 80.4 us -> 79.5 us (0.989)
  waiting for transfers between devices: 24 us -> 22.5 us
    ppermute x15, waiting for transfers between devices: 24 us -> 22.5 us  [exchange(): return lax.ppermute(x, axis, [(k, k ^ flip) for k in range(size)])]
where the time goes in v7:
time: 79.5 us; the launch traced here: 79.3 us
  Pallas kernels  40.9 us (51%)
  waiting for transfers between devices  22.5 us (28%)
  starting transfers between devices  14.6 us (18%)
  other arithmetic  0.87 us (1%)
    pallas_call x1, Pallas kernels, shards(): pl.pallas_call(functools.partial(kernel, order), grid_spec=pltpu.Prefetch...  36 us
    ppermute x15, waiting for transfers between devices, exchange(): return lax.ppermute(x, axis, [(k, k ^ flip) for k in range(size)])  22.5 us
    ppermute x15, starting transfers between devices, exchange(): return lax.ppermute(x, axis, [(k, k ^ flip) for k in range(size)])  14.6 us
    pallas_call x1, Pallas kernels, shards(): pl.pallas_call(functools.partial(pack, devices), grid_spec=pltpu.Prefetch...  2.78 us
    pallas_call x1, Pallas kernels, shards(): pl.pallas_call(standardize, in_specs=[vmem] * 3, out_specs=pl.BlockSpec(m...  2.16 us
  transfers between devices with their start and end apart: 15, of which 12 were waited for; matrix products, arithmetic and copies ran while one was open for 0% of the time, Pallas kernels for 0%

profile of v7, /device:TPU:0, one launch (start us, length us, event | category | flops | bytes accessed | tf_op | source)
XLA Modules:
  0.0 79.3 jit_solution(5657715123036516374)
XLA Ops:
  0.0 0.0 copy-start
  0.0 2.8 %pack.1 = (bf16[64,256]{1,0:T(8,128)(2,1)S(1)}, s32[1,128]{1,0:T(1,128)S(1)}, s32[1,128]{1,0:T(1,128)S(1)}, bf16[2048,256]{1,0:T(8,128)(2,1)S(1)}) custom-call(s32[1]{0:T(128)} %bitcast.me_ref, s32[1024]{0:T(1024)} %ids_ref.1, s32[1,1024]{1,0:T(1,128)} %bitcast.10, bf16[2048,256]{1,0:T(8,128)(2,1)} %points_ref.1), custom_call_target="tpu_custom_call" | custom-call | tf_op jit(solution)/shard_map/pack/pallas_call | solution.py:364
  2.8 0.1 pad_add_fusion.info_ref
  2.9 20.8 %conditional.1 = (bf16[256,256]{1,0:T(8,128)(2,1)}, bf16[256,256]{1,0:T(8,128)(2,1)}, bf16[256,256]{1,0:T(8,128)(2,1)}, bf16[256,256]{1,0:T(8,128)(2,1)}, bf16[2...) conditional(s32[]{:T(128)} %bitcast.4, (s32[]{:T(128)}, ...), branch_computations={%region_0.2_spmd, %region_2.3_spmd} | conditional | flops 796673 | bytes 5785692 | solution.py:399
  2.9 5.1 %collective-permute-start.2 = (bf16[64,256]{1,0:T(8,128)(2,1)S(1)}, bf16[64,256]{1,0:T(8,128)(2,1)S(1)}, u32[]{:S(2)}, u32[]{:S(2)}) collective-permute-start(bf16[64,256]{1,0:T(8,128)(2,1)S(1)} %param.1), channel_id=1, source_target_pairs={{0,6},{1,7},{2,4},{3,5},{4,2},{5,3},{6,0},{7,1},{8,14},{9,15},{10,... | collective-permute-start | bytes 98312 | tf_op jit(solution)/shard_map/cond/branch_1_fun/ppermute | solution.py:338
  8.0 0.0 collective-permute-start.1
  8.0 0.6 collective-permute-start
  8.7 1.3 %collective-permute-done.2 = bf16[64,256]{1,0:T(8,128)(2,1)S(1)} collective-permute-done((bf16[64,256]{1,0:T(8,128)(2,1)S(1)}, bf16[64,256]{1,0:T(8,128)(2,1)S(1)}, u32[]{:S(2)}, u32[]{:S(2)}) %collective-permute-start.2) | collective-permute-done | bytes 32800 | tf_op jit(solution)/shard_map/cond/branch_1_fun/ppermute | solution.py:338
  9.9 2.9 %collective-permute-done.1 = bf16[64,256]{1,0:T(8,128)(2,1)S(1)} collective-permute-done((bf16[64,256]{1,0:T(8,128)(2,1)S(1)}, bf16[64,256]{1,0:T(8,128)(2,1)S(1)}, u32[]{:S(2)}, u32[]{:S(2)}) %collective-permute-start.1) | collective-permute-done | bytes 32800 | tf_op jit(solution)/shard_map/cond/branch_1_fun/ppermute | solution.py:338
  12.8 0.0 collective-permute-done
  12.8 0.7 pad_maximum_fusion
  13.5 2.4 %collective-permute-start.5 = (bf16[256,256]{1,0:T(8,128)(2,1)}, bf16[256,256]{1,0:T(8,128)(2,1)}, u32[]{:S(2)}, u32[]{:S(2)}) collective-permute-start(bf16[256,256]{1,0:T(8,128)(2,1)} %pad_maximum_fusion), channel_id=1, source_target_pairs={{0,24},{8,16},{16,8},{24,0},{1,25},{9,17},{17,9},{25,1},{2,26},{10... | collective-permute-start | bytes 393224 | tf_op jit(solution)/shard_map/cond/branch_1_fun/ppermute | solution.py:338
  16.0 0.5 collective-permute-start.4
  16.5 0.5 collective-permute-start.3
  17.0 0.0 collective-permute-start.6
  17.0 4.1 %collective-permute-done.5 = bf16[256,256]{1,0:T(8,128)(2,1)} collective-permute-done((bf16[256,256]{1,0:T(8,128)(2,1)}, bf16[256,256]{1,0:T(8,128)(2,1)}, u32[]{:S(2)}, u32[]{:S(2)}) %collective-permute-start.5) | collective-permute-done | bytes 131104 | tf_op jit(solution)/shard_map/cond/branch_1_fun/ppermute | solution.py:338
  21.1 0.0 collective-permute-start.9
  21.1 0.8 collective-permute-done.4
  21.9 0.0 collective-permute-start.8
  21.9 0.0 collective-permute-done.3
  21.9 0.5 collective-permute-start.7
  22.4 0.0 collective-permute-done.6
  22.4 0.4 collective-permute-done.9
  22.8 0.8 collective-permute-done.8
  23.6 0.2 collective-permute-done.7
  23.7 0.0 copy-done
  23.7 36.0 %nystrom.1 = (f32[4,2048,256]{2,1,0:T(8,128)S(1)}, f32[2,1024]{1,0:T(2,128)S(1)}) custom-call(s32[2]{0:T(128)S(1)} %pad_add_fusion.info_ref, s32[128]{0:T(128)S(1)} %bitcast.8, bf16[256,256]{1,0:T(8,128)(2,1)} %get-tuple-element.32.refs_0_, bf16[256,256]{1,0:T(8,128)(2,1)} %get-tuple-element.33.refs_1_, bf16[256,256]{1,0:T(8,128)(2,1)} %get-tuple-element.34.refs_2_, ...), custom_call_target="tpu_custom_call" | custom-call | tf_op jit(solution)/shard_map/nystrom/pallas_call | solution.py:402
  59.7 0.4 collective-permute-start.10
  60.1 0.9 %collective-permute-done.10 = f32[2,1024]{1,0:T(2,128)S(1)} collective-permute-done((f32[2,1024]{1,0:T(2,128)S(1)}, f32[2,1024]{1,0:T(2,128)S(1)}, u32[]{:S(2)}, u32[]{:S(2)}) %collective-permute-start.10) | collective-permute-done | bytes 8224 | tf_op jit(solution)/shard_map/ppermute | solution.py:338
  61.0 0.1 collective-permute-start.11
  61.1 3.6 %collective-permute-done.11 = f32[2,1024]{1,0:T(2,128)S(1)} collective-permute-done((f32[2,1024]{1,0:T(2,128)S(1)}, f32[2,1024]{1,0:T(2,128)S(1)}, u32[]{:S(2)}, u32[]{:S(2)}) %collective-permute-start.11) | collective-permute-done | bytes 8224 | tf_op jit(solution)/shard_map/ppermute | solution.py:338
  64.8 2.1 %collective-permute-start.12 = (f32[2,1024]{1,0:T(2,128)S(1)}, f32[2,1024]{1,0:T(2,128)S(1)}, u32[]{:S(2)}, u32[]{:S(2)}) collective-permute-start(f32[2,1024]{1,0:T(2,128)S(1)} %pad_maximum_fusion.2), channel_id=1, source_target_pairs={{0,4},{1,5},{2,6},{3,7},{4,0},{5,1},{6,2},{7,3},{8,12},{9,13},{10,... | collective-permute-start | bytes 24584 | tf_op jit(solution)/shard_map/ppermute | solution.py:338
  66.9 2.5 %collective-permute-done.12 = f32[2,1024]{1,0:T(2,128)S(1)} collective-permute-done((f32[2,1024]{1,0:T(2,128)S(1)}, f32[2,1024]{1,0:T(2,128)S(1)}, u32[]{:S(2)}, u32[]{:S(2)}) %collective-permute-start.12) | collective-permute-done | bytes 8224 | tf_op jit(solution)/shard_map/ppermute | solution.py:338
  69.4 1.1 %collective-permute-start.13 = (f32[2,1024]{1,0:T(2,128)S(1)}, f32[2,1024]{1,0:T(2,128)S(1)}, u32[]{:S(2)}, u32[]{:S(2)}) collective-permute-start(f32[2,1024]{1,0:T(2,128)S(1)} %pad_maximum_fusion.3), channel_id=1, source_target_pairs={{0,8},{8,0},{16,24},{24,16},{1,9},{9,1},{17,25},{25,17},{2,10},{10... | collective-permute-start | bytes 24584 | tf_op jit(solution)/shard_map/ppermute | solution.py:338
  70.5 2.6 %collective-permute-done.13 = f32[2,1024]{1,0:T(2,128)S(1)} collective-permute-done((f32[2,1024]{1,0:T(2,128)S(1)}, f32[2,1024]{1,0:T(2,128)S(1)}, u32[]{:S(2)}, u32[]{:S(2)}) %collective-permute-start.13) | collective-permute-done | bytes 8224 | tf_op jit(solution)/shard_map/ppermute | solution.py:338
  73.2 1.3 %collective-permute-start.14 = (f32[2,1024]{1,0:T(2,128)S(1)}, f32[2,1024]{1,0:T(2,128)S(1)}, u32[]{:S(2)}, u32[]{:S(2)}) collective-permute-start(f32[2,1024]{1,0:T(2,128)S(1)} %pad_maximum_fusion.4), channel_id=1, source_target_pairs={{0,16},{8,24},{16,0},{24,8},{1,17},{9,25},{17,1},{25,9},{2,18},{10... | collective-permute-start | bytes 24584 | tf_op jit(solution)/shard_map/ppermute | solution.py:338
  74.4 2.5 %collective-permute-done.14 = f32[2,1024]{1,0:T(2,128)S(1)} collective-permute-done((f32[2,1024]{1,0:T(2,128)S(1)}, f32[2,1024]{1,0:T(2,128)S(1)}, u32[]{:S(2)}, u32[]{:S(2)}) %collective-permute-start.14) | collective-permute-done | bytes 8224 | tf_op jit(solution)/shard_map/ppermute | solution.py:338
  76.9 2.2 %standardize.1 = bf16[2048,1024]{1,0:T(8,128)(2,1)} custom-call(f32[4,2048,256]{2,1,0:T(8,128)S(1)} %get-tuple-element.41.x_ref, f32[1,1024]{1,0:T(1,128)S(1)} %get-tuple-element.50.shift_ref, f32[1,1024]{1,0:T(1,128)S(1)} %get-tuple-element.49.gain_ref), custom_call_target="tpu_custom_call" | custom-call | tf_op jit(solution)/shard_map/standardize/pallas_call | solution.py:437
  (9 shorter events, 0.1 us)
Async XLA Ops:
  0.0 23.7 %copy-start = (f32[1024]{0:T(1024)S(1)}, f32[1024]{0:T(1024)}, u32[]{:S(2)}) copy-start(f32[1024]{0:T(1024)} %param.6) | copy-start | bytes 12292
  2.9 7.0 %collective-permute-start.2 = (bf16[64,256]{1,0:T(8,128)(2,1)S(1)}, bf16[64,256]{1,0:T(8,128)(2,1)S(1)}, u32[]{:S(2)}, u32[]{:S(2)}) collective-permute-start(bf16[64,256]{1,0:T(8,128)(2,1)S(1)} %param.1), channel_id=1, source_target_pairs={{0,6},{1,7},{2,4},{3,5},{4,2},{5,3},{6,0},{7,1},{8,14},{9,15},{10,... | collective-permute-start | bytes 98312 | tf_op jit(solution)/shard_map/cond/branch_1_fun/ppermute | solution.py:338
  8.0 4.8 %collective-permute-start.1 = (bf16[64,256]{1,0:T(8,128)(2,1)S(1)}, bf16[64,256]{1,0:T(8,128)(2,1)S(1)}, u32[]{:S(2)}, u32[]{:S(2)}) collective-permute-start(bf16[64,256]{1,0:T(8,128)(2,1)S(1)} %param.1), channel_id=1, source_target_pairs={{0,4},{1,5},{2,6},{3,7},{4,0},{5,1},{6,2},{7,3},{8,12},{9,13},{10,... | collective-permute-start | bytes 98312 | tf_op jit(solution)/shard_map/cond/branch_1_fun/ppermute | solution.py:338
  8.0 4.8 %collective-permute-start = (bf16[64,256]{1,0:T(8,128)(2,1)S(1)}, bf16[64,256]{1,0:T(8,128)(2,1)S(1)}, u32[]{:S(2)}, u32[]{:S(2)}) collective-permute-start(bf16[64,256]{1,0:T(8,128)(2,1)S(1)} %param.1), channel_id=1, source_target_pairs={{0,2},{1,3},{2,0},{3,1},{4,6},{5,7},{6,4},{7,5},{8,10},{9,11},{10,... | collective-permute-start | bytes 98312 | tf_op jit(solution)/shard_map/cond/branch_1_fun/ppermute | solution.py:338
  13.5 7.6 %collective-permute-start.5 = (bf16[256,256]{1,0:T(8,128)(2,1)}, bf16[256,256]{1,0:T(8,128)(2,1)}, u32[]{:S(2)}, u32[]{:S(2)}) collective-permute-start(bf16[256,256]{1,0:T(8,128)(2,1)} %pad_maximum_fusion), channel_id=1, source_target_pairs={{0,24},{8,16},{16,8},{24,0},{1,25},{9,17},{17,9},{25,1},{2,26},{10... | collective-permute-start | bytes 393224 | tf_op jit(solution)/shard_map/cond/branch_1_fun/ppermute | solution.py:338
  16.0 5.9 %collective-permute-start.4 = (bf16[256,256]{1,0:T(8,128)(2,1)}, bf16[256,256]{1,0:T(8,128)(2,1)}, u32[]{:S(2)}, u32[]{:S(2)}) collective-permute-start(bf16[256,256]{1,0:T(8,128)(2,1)} %pad_maximum_fusion), channel_id=1, source_target_pairs={{0,16},{8,24},{16,0},{24,8},{1,17},{9,25},{17,1},{25,9},{2,18},{10... | collective-permute-start | bytes 393224 | tf_op jit(solution)/shard_map/cond/branch_1_fun/ppermute | solution.py:338
  16.5 5.4 %collective-permute-start.3 = (bf16[256,256]{1,0:T(8,128)(2,1)}, bf16[256,256]{1,0:T(8,128)(2,1)}, u32[]{:S(2)}, u32[]{:S(2)}) collective-permute-start(bf16[256,256]{1,0:T(8,128)(2,1)} %pad_maximum_fusion), channel_id=1, source_target_pairs={{0,8},{8,0},{16,24},{24,16},{1,9},{9,1},{17,25},{25,17},{2,10},{10... | collective-permute-start | bytes 393224 | tf_op jit(solution)/shard_map/cond/branch_1_fun/ppermute | solution.py:338
  17.0 5.4 %collective-permute-start.6 = (bf16[256,256]{1,0:T(8,128)(2,1)}, bf16[256,256]{1,0:T(8,128)(2,1)}, u32[]{:S(2)}, u32[]{:S(2)}) collective-permute-start(bf16[256,256]{1,0:T(8,128)(2,1)} %pad_maximum_fusion), channel_id=1, source_target_pairs={{0,1},{1,0},{2,3},{3,2},{4,5},{5,4},{6,7},{7,6},{8,9},{9,8},{10,11... | collective-permute-start | bytes 393224 | tf_op jit(solution)/shard_map/cond/branch_1_fun/ppermute | solution.py:338
  21.1 1.7 %collective-permute-start.9 = (bf16[256,256]{1,0:T(8,128)(2,1)}, bf16[256,256]{1,0:T(8,128)(2,1)}, u32[]{:S(2)}, u32[]{:S(2)}) collective-permute-start(bf16[256,256]{1,0:T(8,128)(2,1)} %collective-permute-done.5), channel_id=1, source_target_pairs={{0,1},{1,0},{2,3},{3,2},{4,5},{5,4},{6,7},{7,6},{8,9},{9,8},{10,11... | collective-permute-start | bytes 393224 | tf_op jit(solution)/shard_map/cond/branch_1_fun/ppermute | solution.py:338
  21.9 1.7 %collective-permute-start.8 = (bf16[256,256]{1,0:T(8,128)(2,1)}, bf16[256,256]{1,0:T(8,128)(2,1)}, u32[]{:S(2)}, u32[]{:S(2)}) collective-permute-start(bf16[256,256]{1,0:T(8,128)(2,1)} %collective-permute-done.4), channel_id=1, source_target_pairs={{0,1},{1,0},{2,3},{3,2},{4,5},{5,4},{6,7},{7,6},{8,9},{9,8},{10,11... | collective-permute-start | bytes 393224 | tf_op jit(solution)/shard_map/cond/branch_1_fun/ppermute | solution.py:338
  21.9 1.9 %collective-permute-start.7 = (bf16[256,256]{1,0:T(8,128)(2,1)}, bf16[256,256]{1,0:T(8,128)(2,1)}, u32[]{:S(2)}, u32[]{:S(2)}) collective-permute-start(bf16[256,256]{1,0:T(8,128)(2,1)} %collective-permute-done.3), channel_id=1, source_target_pairs={{0,1},{1,0},{2,3},{3,2},{4,5},{5,4},{6,7},{7,6},{8,9},{9,8},{10,11... | collective-permute-start | bytes 393224 | tf_op jit(solution)/shard_map/cond/branch_1_fun/ppermute | solution.py:338
  59.7 1.2 %collective-permute-start.10 = (f32[2,1024]{1,0:T(2,128)S(1)}, f32[2,1024]{1,0:T(2,128)S(1)}, u32[]{:S(2)}, u32[]{:S(2)}) collective-permute-start(f32[2,1024]{1,0:T(2,128)S(1)} %get-tuple-element.42), channel_id=1, source_target_pairs={{0,1},{1,0},{2,3},{3,2},{4,5},{5,4},{6,7},{7,6},{8,9},{9,8},{10,11... | collective-permute-start | bytes 24584 | tf_op jit(solution)/shard_map/ppermute | solution.py:338
  61.0 3.7 %collective-permute-start.11 = (f32[2,1024]{1,0:T(2,128)S(1)}, f32[2,1024]{1,0:T(2,128)S(1)}, u32[]{:S(2)}, u32[]{:S(2)}) collective-permute-start(f32[2,1024]{1,0:T(2,128)S(1)} %pad_maximum_fusion.1), channel_id=1, source_target_pairs={{0,2},{1,3},{2,0},{3,1},{4,6},{5,7},{6,4},{7,5},{8,10},{9,11},{10,... | collective-permute-start | bytes 24584 | tf_op jit(solution)/shard_map/ppermute | solution.py:338
  64.8 4.6 %collective-permute-start.12 = (f32[2,1024]{1,0:T(2,128)S(1)}, f32[2,1024]{1,0:T(2,128)S(1)}, u32[]{:S(2)}, u32[]{:S(2)}) collective-permute-start(f32[2,1024]{1,0:T(2,128)S(1)} %pad_maximum_fusion.2), channel_id=1, source_target_pairs={{0,4},{1,5},{2,6},{3,7},{4,0},{5,1},{6,2},{7,3},{8,12},{9,13},{10,... | collective-permute-start | bytes 24584 | tf_op jit(solution)/shard_map/ppermute | solution.py:338
  69.4 3.7 %collective-permute-start.13 = (f32[2,1024]{1,0:T(2,128)S(1)}, f32[2,1024]{1,0:T(2,128)S(1)}, u32[]{:S(2)}, u32[]{:S(2)}) collective-permute-start(f32[2,1024]{1,0:T(2,128)S(1)} %pad_maximum_fusion.3), channel_id=1, source_target_pairs={{0,8},{8,0},{16,24},{24,16},{1,9},{9,1},{17,25},{25,17},{2,10},{10... | collective-permute-start | bytes 24584 | tf_op jit(solution)/shard_map/ppermute | solution.py:338
  73.2 3.7 %collective-permute-start.14 = (f32[2,1024]{1,0:T(2,128)S(1)}, f32[2,1024]{1,0:T(2,128)S(1)}, u32[]{:S(2)}, u32[]{:S(2)}) collective-permute-start(f32[2,1024]{1,0:T(2,128)S(1)} %pad_maximum_fusion.4), channel_id=1, source_target_pairs={{0,16},{8,24},{16,0},{24,8},{1,17},{9,25},{17,1},{25,9},{2,18},{10... | collective-permute-start | bytes 24584 | tf_op jit(solution)/shard_map/ppermute | solution.py:338
